TPU v7x, 8 devices: a whole 2x2x1 slice. The times are simulated.
8 devices in a mesh: dp: 2 (over z, y), tp: 4 (over x, core).
Axes of the slice: x: 2, y: 2, z: 1, core: 2. Of those that a mesh axis runs over, the one named last changes fastest.
Arguments:
- x_seq: bfloat16 [4, 1024, 6144], P('dp', 'tp'), parts along dimension 0
- ln_gain: bfloat16 [6144], replicated
- w_qkv: bfloat16 [6144, 8, 1024], P(None, 'tp')
- w_out: bfloat16 [6144, 6144], P('tp')
- y_grad: bfloat16 [4, 1024, 6144], P('dp', 'tp'), parts along dimension 0
Outputs:
- output 1: bfloat16 [4, 1024, 6144], P('dp', 'tp'), parts along dimension 0
- output 2: bfloat16 [4, 1024, 6144], P('dp', 'tp'), parts along dimension 0
- output 3: bfloat16 [12288], P('dp'), parts along dimension 0
- output 4: bfloat16 [12288, 8, 1024], P('dp', 'tp'), parts along dimension 0
- output 5: bfloat16 [12288, 6144], P(('dp', 'tp')), parts along dimension 0
There are 2 independent parts. A program takes and returns all parts, laid end to end along the dimension named above; an argument that names none is the same for every part.
All inputs are finite; a program needn't handle non-finite values.
Results may differ from a plain program's by a relative error of at most 0.0162463.
Values are sent between devices in bfloat16 or wider.
A program may use at most 1 GiB of HBM per device.

v0:
```python
import functools
import jax
import jax.numpy as jnp
from jax import lax
from jax.experimental import pallas as pl
from jax.experimental.pallas import tpu as pltpu
from jax.sharding import PartitionSpec as P

CLIP_QKV = 8.0
ROPE_THETA = 500000.0
LN_EPS = 1e-5
LOG2E = 1.4426950408889634
HEAD_DIM = 128
TILE_Q = 256
NEG_BIG = -1e30
NT = (((1,), (1,)), ((), ()))
TN = (((0,), (0,)), ((), ()))
NN = (((1,), (0,)), ((), ()))


def dot(a, b, dims):
    return lax.dot_general(a, b, dims, preferred_element_type=jnp.float32)


def rope_tables(seq_len):
    inv_freq = 1.0 / (ROPE_THETA ** (jnp.arange(0, HEAD_DIM, 2, dtype=jnp.float32) / HEAD_DIM))
    angles = jnp.arange(seq_len, dtype=jnp.float32)[:, None] * inv_freq[None, :]
    cos_t, sin_t = jnp.cos(angles), jnp.sin(angles)
    return jnp.concatenate([cos_t, cos_t], axis=-1), jnp.concatenate([-sin_t, sin_t], axis=-1)


def clipped(raw):
    return jnp.minimum(jnp.maximum(raw.astype(jnp.float32), -CLIP_QKV), CLIP_QKV)


def rotate(vec, cos_t, sin_t):
    return (vec * cos_t + pltpu.roll(vec, HEAD_DIM // 2, 1) * sin_t).astype(jnp.bfloat16)


def unrotate(grad, cos_t, sin_t):
    grad = grad.astype(jnp.bfloat16).astype(jnp.float32)
    return grad * cos_t - pltpu.roll(grad, HEAD_DIM // 2, 1) * sin_t


def pass_clip(grad, raw):
    inside = jnp.abs(raw.astype(jnp.float32)) < CLIP_QKV
    return jnp.where(inside, grad, 0.0).astype(jnp.bfloat16)


def diagonal_mask():
    row = lax.broadcasted_iota(jnp.int32, (TILE_Q, TILE_Q), 0)
    col = lax.broadcasted_iota(jnp.int32, (TILE_Q, TILE_Q), 1)
    return row >= col


def mask_scores(scores, width, mask):
    tail = jnp.where(mask, scores[:, width - TILE_Q:], NEG_BIG)
    if width == TILE_Q:
        return tail
    return jnp.concatenate([scores[:, :width - TILE_Q], tail], axis=1)


def half_rows(own, size):
    side = lax.axis_index("tp") // 2
    start = side if own else 1 - side
    return pl.ds(pl.multiple_of(start * size, size), size)


def attn_fwd_kernel(groups, own_ref, far_ref, cos_ref, sin_ref, oown_ref, ofar_ref, lse_ref, qkv_ref, out_ref, k_scr, v_scr):
    half = own_ref.shape[0]
    own, far = half_rows(True, half), half_rows(False, half)
    qkv_ref[own, :] = own_ref[...]
    qkv_ref[far, :] = far_ref[...]
    seq_len = qkv_ref.shape[0]
    k_col = groups * HEAD_DIM
    k_scr[...] = rotate(clipped(qkv_ref[:, k_col:k_col + HEAD_DIM]), cos_ref[...], sin_ref[...])
    v_scr[...] = clipped(qkv_ref[:, k_col + HEAD_DIM:k_col + 2 * HEAD_DIM]).astype(jnp.bfloat16)
    mask = diagonal_mask()
    coef = HEAD_DIM ** -0.5 * LOG2E

    def head(g, carry):
        cols = pl.ds(pl.multiple_of(g * HEAD_DIM, HEAD_DIM), HEAD_DIM)
        for qi in range(seq_len // TILE_Q):
            rows = slice(qi * TILE_Q, (qi + 1) * TILE_Q)
            width = (qi + 1) * TILE_Q
            query = rotate(clipped(qkv_ref[rows, cols]), cos_ref[rows, :], sin_ref[rows, :])
            scores = mask_scores(dot(query, k_scr[:width, :], NT), width, mask)
            peak = jnp.max(scores, axis=1, keepdims=True)
            prob = jnp.exp2((scores - peak) * coef)
            total = jnp.sum(prob, axis=1, keepdims=True)
            prob = (prob * (1.0 / total)).astype(jnp.bfloat16)
            out_ref[rows, cols] = dot(prob, v_scr[:width, :], NN).astype(jnp.bfloat16)
            lse = peak * coef + jnp.log2(total)
            lse_ref[rows, cols] = jnp.broadcast_to(lse, (TILE_Q, HEAD_DIM))
        return carry

    lax.fori_loop(0, groups, head, 0)
    oown_ref[...] = out_ref[own, :]
    ofar_ref[...] = out_ref[far, :]


def attn_bwd_kernel(groups, own_ref, far_ref, aown_ref, afar_ref, down_ref, dfar_ref, lse_ref, cos_ref, sin_ref, gown_ref, gfar_ref, qkv_ref, attn_ref, dattn_ref, k_scr, v_scr, dk_scr, dv_scr):
    half = own_ref.shape[0]
    own, far = half_rows(True, half), half_rows(False, half)
    for dst, near, away in ((qkv_ref, own_ref, far_ref), (attn_ref, aown_ref, afar_ref), (dattn_ref, down_ref, dfar_ref)):
        dst[own, :] = near[...]
        dst[far, :] = away[...]
    seq_len = qkv_ref.shape[0]
    k_col = groups * HEAD_DIM
    v_col = k_col + HEAD_DIM
    scale = HEAD_DIM ** -0.5
    coef = scale * LOG2E
    k_scr[...] = rotate(clipped(qkv_ref[:, k_col:v_col]), cos_ref[...], sin_ref[...])
    v_scr[...] = clipped(qkv_ref[:, v_col:v_col + HEAD_DIM]).astype(jnp.bfloat16)
    dk_scr[...] = jnp.zeros_like(dk_scr)
    dv_scr[...] = jnp.zeros_like(dv_scr)
    mask = diagonal_mask()

    def head(g, carry):
        cols = pl.ds(pl.multiple_of(g * HEAD_DIM, HEAD_DIM), HEAD_DIM)
        for qi in range(seq_len // TILE_Q):
            rows = slice(qi * TILE_Q, (qi + 1) * TILE_Q)
            width = (qi + 1) * TILE_Q
            raw = qkv_ref[rows, cols]
            cos_t, sin_t = cos_ref[rows, :], sin_ref[rows, :]
            query = rotate(clipped(raw), cos_t, sin_t)
            dout = dattn_ref[rows, cols]
            delta = jnp.sum(dout.astype(jnp.float32) * attn_ref[rows, cols].astype(jnp.float32), axis=1, keepdims=True)
            scores = mask_scores(dot(query, k_scr[:width, :], NT), width, mask)
            lse = jnp.concatenate([lse_ref[rows, cols]] * (width // HEAD_DIM), axis=1)
            prob = jnp.exp2(scores * coef - lse)
            dprob = dot(dout, v_scr[:width, :], NT).astype(jnp.bfloat16).astype(jnp.float32)
            dscore = (prob * (dprob - delta)).astype(jnp.bfloat16)
            prob = prob.astype(jnp.bfloat16)
            dv_scr[:, :width] += dot(dout, prob, TN)
            dk_scr[:, :width] += dot(query, dscore, TN)
            dquery = dot(dscore, k_scr[:width, :], NN) * scale
            qkv_ref[rows, cols] = pass_clip(unrotate(dquery, cos_t, sin_t), raw)
        return carry

    lax.fori_loop(0, groups, head, 0)
    dkey = unrotate(dk_scr[...].T * scale, cos_ref[...], sin_ref[...])
    qkv_ref[:, k_col:v_col] = pass_clip(dkey, qkv_ref[:, k_col:v_col])
    qkv_ref[:, v_col:v_col + HEAD_DIM] = pass_clip(dv_scr[...].T, qkv_ref[:, v_col:v_col + HEAD_DIM])
    gown_ref[...] = qkv_ref[own, :]
    gfar_ref[...] = qkv_ref[far, :]


def head_specs(half, slot, wide):
    table = pl.BlockSpec((2 * half, HEAD_DIM), lambda n: (0, 0))
    part = pl.BlockSpec((half, wide), lambda n: (0, n))
    full = pl.BlockSpec((half, slot), lambda n: (0, n))
    lse = pl.BlockSpec((2 * half, wide), lambda n: (0, n))
    return table, part, full, lse


def attn_fwd(qkv_own, qkv_far, cos_t, sin_t, kv_loc):
    half = qkv_own.shape[0]
    slot = qkv_own.shape[1] // kv_loc
    groups = slot // HEAD_DIM - 2
    wide = groups * HEAD_DIM
    table, part, full, lse = head_specs(half, slot, wide)
    rows = jax.ShapeDtypeStruct((half, kv_loc * wide), jnp.bfloat16)
    return pl.pallas_call(
        functools.partial(attn_fwd_kernel, groups),
        grid=(kv_loc,),
        in_specs=[full, full, table, table],
        out_specs=[part, part, lse],
        out_shape=[rows, rows, jax.ShapeDtypeStruct((2 * half, kv_loc * wide), jnp.float32)],
        scratch_shapes=[pltpu.VMEM((2 * half, slot), jnp.bfloat16), pltpu.VMEM((2 * half, wide), jnp.bfloat16)] + [pltpu.VMEM((2 * half, HEAD_DIM), jnp.bfloat16)] * 2,
        compiler_params=pltpu.CompilerParams(vmem_limit_bytes=48 * 2 ** 20),
        cost_estimate=pl.CostEstimate(flops=12 * 10 ** 9, bytes_accessed=14 * 10 ** 6, transcendentals=0),
        name="attn_fwd",
    )(qkv_own, qkv_far, cos_t, sin_t)


def attn_bwd(qkv_own, qkv_far, attn_own, attn_far, dattn_own, dattn_far, lse_t, cos_t, sin_t, kv_loc):
    half = qkv_own.shape[0]
    slot = qkv_own.shape[1] // kv_loc
    groups = slot // HEAD_DIM - 2
    wide = groups * HEAD_DIM
    table, part, full, lse = head_specs(half, slot, wide)
    return pl.pallas_call(
        functools.partial(attn_bwd_kernel, groups),
        grid=(kv_loc,),
        in_specs=[full, full, part, part, part, part, lse, table, table],
        out_specs=[full, full],
        out_shape=[jax.ShapeDtypeStruct(qkv_own.shape, jnp.bfloat16)] * 2,
        scratch_shapes=[pltpu.VMEM((2 * half, slot), jnp.bfloat16)] + [pltpu.VMEM((2 * half, wide), jnp.bfloat16)] * 2 + [pltpu.VMEM((2 * half, HEAD_DIM), jnp.bfloat16)] * 2 + [pltpu.VMEM((HEAD_DIM, 2 * half), jnp.float32)] * 2,
        compiler_params=pltpu.CompilerParams(vmem_limit_bytes=56 * 2 ** 20),
        cost_estimate=pl.CostEstimate(flops=25 * 10 ** 9, bytes_accessed=22 * 10 ** 6, transcendentals=0),
        name="attn_bwd",
    )(qkv_own, qkv_far, attn_own, attn_far, dattn_own, dattn_far, lse_t, cos_t, sin_t)


def dw_qkv_kernel(n_rows, *refs):
    acts, grads, out_ref = refs[:n_rows], refs[n_rows:-1], refs[-1]
    slot = out_ref.shape[2]
    for n in range(out_ref.shape[1]):
        cols = slice(n * slot, (n + 1) * slot)
        acc = sum(dot(a[...], g[:, cols], TN) for a, g in zip(acts, grads))
        out_ref[:, n, :] = acc.astype(jnp.bfloat16)


def dw_qkv(acts, grads, kv_loc, tile=512):
    rows, d_model = acts[0].shape
    width = grads[0].shape[1]
    slot = width // kv_loc
    whole = pl.BlockSpec((rows, width), lambda i: (0, 0))
    part = pl.BlockSpec((rows, tile), lambda i: (0, i))
    return pl.pallas_call(
        functools.partial(dw_qkv_kernel, len(acts)),
        grid=(d_model // tile,),
        in_specs=[part] * len(acts) + [whole] * len(grads),
        out_specs=pl.BlockSpec((tile, kv_loc, slot), lambda i: (i, 0, 0)),
        out_shape=jax.ShapeDtypeStruct((d_model, kv_loc, slot), jnp.bfloat16),
        compiler_params=pltpu.CompilerParams(vmem_limit_bytes=60 * 2 ** 20),
        cost_estimate=pl.CostEstimate(flops=51 * 10 ** 9, bytes_accessed=60 * 10 ** 6, transcendentals=0),
        name="dw_qkv",
    )(*acts, *grads)


def dw_out_kernel(n_rows, *refs):
    acts, grads, out_ref = refs[:n_rows], refs[n_rows:-1], refs[-1]
    out_ref[...] = sum(dot(a[...], g[...], TN) for a, g in zip(acts, grads)).astype(jnp.bfloat16)


def dw_out(acts, grads, tile=512):
    rows, width = acts[0].shape
    d_model = grads[0].shape[-1]
    whole = pl.BlockSpec((rows, width), lambda i: (0, 0))
    part = pl.BlockSpec((rows, tile), lambda i: (0, i))
    return pl.pallas_call(
        functools.partial(dw_out_kernel, len(acts)),
        grid=(d_model // tile,),
        in_specs=[whole] * len(acts) + [part] * len(grads),
        out_specs=pl.BlockSpec((width, tile), lambda i: (0, i)),
        out_shape=jax.ShapeDtypeStruct((width, d_model), jnp.bfloat16),
        compiler_params=pltpu.CompilerParams(vmem_limit_bytes=60 * 2 ** 20),
        cost_estimate=pl.CostEstimate(flops=39 * 10 ** 9, bytes_accessed=50 * 10 ** 6, transcendentals=0),
        name="dw_out",
    )(*acts, *grads)


def normalized(x_f32):
    centered = x_f32 - jnp.mean(x_f32, axis=-1, keepdims=True)
    rstd = lax.rsqrt(jnp.mean(centered * centered, axis=-1, keepdims=True) + LN_EPS)
    return centered * rstd, rstd


def norm_fwd_kernel(x_ref, gain_ref, h_ref):
    hat, _ = normalized(x_ref[0].astype(jnp.float32))
    h_ref[...] = (hat * gain_ref[...]).astype(jnp.bfloat16)


def norm_fwd(x_seq, gain, b, tile=64):
    _, rows, d_model = x_seq.shape
    return pl.pallas_call(
        norm_fwd_kernel,
        grid=(rows // tile,),
        in_specs=[pl.BlockSpec((1, tile, d_model), lambda i: (b, i, 0)), pl.BlockSpec((1, d_model), lambda i: (0, 0))],
        out_specs=pl.BlockSpec((tile, d_model), lambda i: (i, 0)),
        out_shape=jax.ShapeDtypeStruct((rows, d_model), jnp.bfloat16),
        cost_estimate=pl.CostEstimate(flops=2 * 10 ** 9, bytes_accessed=7 * 10 ** 6, transcendentals=0),
        name="norm_fwd",
    )(x_seq, gain)


def residual_kernel(x_ref, near_ref, far_ref, *rest):
    total = near_ref[...].astype(jnp.float32) + far_ref[...].astype(jnp.float32)
    rest[-1][0] = (x_ref[0].astype(jnp.float32) + total.astype(jnp.bfloat16).astype(jnp.float32)).astype(jnp.bfloat16)


def norm_bwd_kernel(x_ref, dy_ref, gain_ref, near_ref, far_ref, *rest):
    dx_ref, dgain_ref = rest[-2:]
    hat, rstd = normalized(x_ref[0].astype(jnp.float32))
    dh = (near_ref[...].astype(jnp.float32) + far_ref[...].astype(jnp.float32)).astype(jnp.bfloat16).astype(jnp.float32)

    @pl.when(pl.program_id(0) == 0)
    def _():
        dgain_ref[...] = jnp.zeros_like(dgain_ref)

    dgain_ref[...] += jnp.sum(dh * hat, axis=0, keepdims=True)
    dhat = dh * gain_ref[...]
    inner = dhat - jnp.mean(dhat, axis=-1, keepdims=True) - hat * jnp.mean(dhat * hat, axis=-1, keepdims=True)
    dx_ref[0] = (dy_ref[0].astype(jnp.float32) + inner * rstd).astype(jnp.bfloat16)


def residual(x_seq, near, far, b, held, tile=64):
    _, rows, d_model = x_seq.shape
    whole = pl.BlockSpec((1, tile, d_model), lambda i: (b, i, 0))
    part = pl.BlockSpec((tile, d_model), lambda i: (i, 0))
    keep = [] if held is None else [held]
    return pl.pallas_call(
        residual_kernel,
        grid=(rows // tile,),
        in_specs=[whole, part, part] + [pl.BlockSpec(memory_space=pl.ANY)] * len(keep),
        out_specs=whole,
        out_shape=jax.ShapeDtypeStruct(x_seq.shape, jnp.bfloat16),
        input_output_aliases={3: 0} if keep else {},
        cost_estimate=pl.CostEstimate(flops=2 * 10 ** 9, bytes_accessed=13 * 10 ** 6, transcendentals=0),
        name="residual",
    )(x_seq, near, far, *keep)


def norm_bwd(x_seq, y_grad, gain, near, far, b, held, tile=64):
    _, rows, d_model = x_seq.shape
    whole = pl.BlockSpec((1, tile, d_model), lambda i: (b, i, 0))
    part = pl.BlockSpec((tile, d_model), lambda i: (i, 0))
    row = pl.BlockSpec((1, d_model), lambda i: (0, 0))
    keep = [] if held is None else [held]
    return pl.pallas_call(
        norm_bwd_kernel,
        grid=(rows // tile,),
        in_specs=[whole, whole, row, part, part] + [pl.BlockSpec(memory_space=pl.ANY)] * len(keep),
        out_specs=[whole, row],
        out_shape=[jax.ShapeDtypeStruct(x_seq.shape, jnp.bfloat16), jax.ShapeDtypeStruct((1, d_model), jnp.float32)],
        input_output_aliases={5: 0} if keep else {},
        cost_estimate=pl.CostEstimate(flops=4 * 10 ** 9, bytes_accessed=16 * 10 ** 6, transcendentals=0),
        name="norm_bwd",
    )(x_seq, y_grad, gain, near, far, *keep)


def solution(mesh):
    n_tp = mesh.shape["tp"]
    pairs = [[i, i + 1] for i in range(0, n_tp, 2)]

    def swap(value, bit):
        return lax.ppermute(value, "tp", [(i, i ^ bit) for i in range(n_tp)])

    def pair_gather(value):
        return lax.all_gather(value, "tp", axis_index_groups=pairs, axis=0, tiled=True)

    def pair_scatter(value):
        return lax.psum_scatter(value, "tp", axis_index_groups=pairs, scatter_dimension=0, tiled=True)

    def staged_step(x_seq, ln_gain, w_qkv, w_out, y_grad):
        kv_loc = w_qkv.shape[1]
        gain = ln_gain.astype(jnp.float32)[None, :]
        token = [None]

        def run(fn, lead, *rest):
            if token[0] is not None:
                lead, _ = lax.optimization_barrier((lead, token[0]))
            result = fn(lead, *rest)
            token[0] = jax.tree.leaves(result)[0]
            return result

        def matmul(dims):
            return lambda a, b: dot(a, b, dims).astype(jnp.bfloat16)

        cos_t, sin_t = rope_tables(x_seq.shape[1] * n_tp)
        h0 = run(lambda x: norm_fwd(x, gain, 0), x_seq)
        hx0 = swap(h0, 2)
        h1 = run(lambda x: norm_fwd(x, gain, 1), x_seq)
        hx1 = swap(h1, 2)
        dy0, dy1, _ = lax.optimization_barrier((y_grad[0], y_grad[1], h1))
        dyx0 = swap(dy0, 2)
        dyx1 = swap(dy1, 2)
        h_own0, h_own1 = pair_gather(h0), pair_gather(h1)
        dy_own0, dy_own1 = pair_gather(dy0), pair_gather(dy1)
        w_flat = run(lambda w: lax.optimization_barrier(w.reshape(w.shape[0], -1)), w_qkv)
        qkv_own0 = run(matmul(NN), h_own0, w_flat)
        qkv_own1 = run(matmul(NN), h_own1, w_flat)
        h_far0 = pair_gather(hx0)
        dattn_own0 = run(matmul(NT), dy_own0, w_out)
        qkv_far0 = run(matmul(NN), h_far0, w_flat)
        attn_own0, attn_far0, lse0 = run(lambda far: attn_fwd(qkv_own0, far, cos_t, sin_t, kv_loc), qkv_far0)
        o_far0 = run(matmul(NN), attn_far0, w_out)
        h_far1 = pair_gather(hx1)
        os_far0 = pair_scatter(o_far0)
        o_near0 = run(matmul(NN), attn_own0, w_out)
        ox0 = swap(os_far0, 2)
        os_near0 = pair_scatter(o_near0)
        dattn_own1 = run(matmul(NT), dy_own1, w_out)
        qkv_far1 = run(matmul(NN), h_far1, w_flat)
        attn_own1, attn_far1, lse1 = run(lambda far: attn_fwd(qkv_own1, far, cos_t, sin_t, kv_loc), qkv_far1)
        dy_far0 = pair_gather(dyx0)
        o_far1 = run(matmul(NN), attn_far1, w_out)
        os_far1 = pair_scatter(o_far1)
        dattn_far0 = run(matmul(NT), dy_far0, w_out)
        ox1 = swap(os_far1, 2)
        dq_own0, dq_far0 = run(lambda d: attn_bwd(qkv_own0, qkv_far0, attn_own0, attn_far0, dattn_own0, d, lse0, cos_t, sin_t, kv_loc), dattn_far0)
        dy_far1 = pair_gather(dyx1)
        dh_far0 = run(matmul(NT), dq_far0, w_flat)
        dhs_far0 = pair_scatter(dh_far0)
        o_near1 = run(matmul(NN), attn_own1, w_out)
        dhx0 = swap(dhs_far0, 2)
        os_near1 = pair_scatter(o_near1)
        dattn_far1 = run(matmul(NT), dy_far1, w_out)
        dq_own1, dq_far1 = run(lambda d: attn_bwd(qkv_own1, qkv_far1, attn_own1, attn_far1, dattn_own1, d, lse1, cos_t, sin_t, kv_loc), dattn_far1)
        dh_far1 = run(matmul(NT), dq_far1, w_flat)
        dhs_far1 = pair_scatter(dh_far1)
        dh_near0 = run(matmul(NT), dq_own0, w_flat)
        dhx1 = swap(dhs_far1, 2)
        dhs_near0 = pair_scatter(dh_near0)
        dh_near1 = run(matmul(NT), dq_own1, w_flat)
        dhs_near1 = pair_scatter(dh_near1)
        wout_grad = run(lambda a: dw_out([a, attn_far0, attn_own1, attn_far1], [dy_own0, dy_far0, dy_own1, dy_far1]), attn_own0)
        y_out = run(lambda near: residual(x_seq, near, ox0, 0, None), os_near0)
        y_out = run(lambda near: residual(x_seq, near, ox1, 1, y_out), os_near1)
        wqkv_grad = run(lambda h: dw_qkv([h, h_far0, h_own1, h_far1], [dq_own0, dq_far0, dq_own1, dq_far1], kv_loc), h_own0)
        x_grad, gain0 = run(lambda near: norm_bwd(x_seq, y_grad, gain, near, dhx0, 0, None), dhs_near0)
        x_grad, gain1 = run(lambda near: norm_bwd(x_seq, y_grad, gain, near, dhx1, 1, x_grad), dhs_near1)
        gain_part = gain0 + gain1
        gain_part = gain_part + swap(gain_part, 1)
        gain_grad = (gain_part + swap(gain_part, 2)).astype(jnp.bfloat16)[0]
        return y_out, x_grad, gain_grad, wqkv_grad, wout_grad

    specs_in = (P('dp', 'tp', None), P(None), P(None, 'tp', None), P('tp', None), P('dp', 'tp', None))
    specs_out = (P('dp', 'tp', None), P('dp', 'tp', None), P('dp'), P('dp', 'tp', None), P(('dp', 'tp'), None))
    return jax.shard_map(staged_step, mesh=mesh, in_specs=specs_in, out_specs=specs_out, check_vma=False)
```

profile of v0, /device:TPU:0, one launch (start us, length us, event | category | flops | bytes accessed | tf_op | source)
XLA Modules:
  0.0 1033.6 jit_solution(17413515362683880995)
XLA Ops:
  30.9 68.3 %collective-permute-done.1 = bf16[256,6144]{1,0:T(8,128)(2,1)} collective-permute-done((bf16[256,6144]{1,0:T(8,128)(2,1)S(1)}, bf16[256,6144]{1,0:T(8,128)(2,1)}, u32[]{:S(2)}, u32[]{:S(2)}) %collective-permute-start.1) | collective-permute-done | bytes 3145760 | tf_op jit(solution)/shard_map/ppermute | solution.py:329
  102.8 67.7 %collective-permute-done = bf16[256,6144]{1,0:T(8,128)(2,1)} collective-permute-done((bf16[256,6144]{1,0:T(8,128)(2,1)S(1)}, bf16[256,6144]{1,0:T(8,128)(2,1)}, u32[]{:S(2)}, u32[]{:S(2)}) %collective-permute-start) | collective-permute-done | bytes 3145760 | tf_op jit(solution)/shard_map/ppermute | solution.py:329
  172.1 67.2 %collective-permute-done.2 = bf16[256,6144]{1,0:T(8,128)(2,1)S(1)} collective-permute-done((bf16[256,6144]{1,0:T(8,128)(2,1)}, bf16[256,6144]{1,0:T(8,128)(2,1)S(1)}, u32[]{:S(2)}, u32[]{:S(2)}) %collective-permute-start.2) | collective-permute-done | bytes 3145760 | tf_op jit(solution)/shard_map/ppermute | solution.py:329
  242.3 25.3 %copy.12 = bf16[768,8,2,1024]{3,1,2,0:T(8,128)(2,1)} copy(bf16[768,8,2,1024]{3,2,1,0:T(2,128)(2,1)} %bitcast.39) | data formatting | bytes 50331648
  269.9 39.1 %collective-permute-done.3 = bf16[256,6144]{1,0:T(8,128)(2,1)} collective-permute-done((bf16[256,6144]{1,0:T(8,128)(2,1)}, bf16[256,6144]{1,0:T(8,128)(2,1)}, u32[]{:S(2)}, u32[]{:S(2)}) %collective-permute-start.3) | collective-permute-done | bytes 3145760 | tf_op jit(solution)/shard_map/ppermute | solution.py:329
  309.4 22.3 %convolution_convert_fusion.11.own_ref = bf16[512,2048]{1,0:T(8,128)(2,1)} fusion(bf16[512,6144]{1,0:T(8,128)(2,1)} %all-gather.11.cloned.1.call-done.refs_0_, bf16[6144,2048]{1,0:T(8,128)(2,1)} %bitcast.40), kind=kOutput, calls=%fused_computation.13 | convolution fusion | flops 12885950464 | bytes 33554432 | tf_op jit(solution)/shard_map/dot_general | solution.py:22
  331.7 20.7 %convolution_convert_fusion.10.own_ref = bf16[512,2048]{1,0:T(8,128)(2,1)} fusion(bf16[512,6144]{1,0:T(8,128)(2,1)} %all-gather.9.cloned.1.call-done.refs_2_, bf16[6144,2048]{1,0:T(8,128)(2,1)} %bitcast.41), kind=kOutput, calls=%fused_computation.12 | convolution fusion | flops 12885950464 | bytes 33554432 | tf_op jit(solution)/shard_map/dot_general | solution.py:22
  352.4 17.0 %convolution_convert_fusion.15.down_ref = bf16[512,1536]{1,0:T(8,128)(2,1)} fusion(bf16[512,6144]{1,0:T(8,128)(2,1)} %all-gather.19.cloned.1.call-done.refs_4_, bf16[1536,6144]{1,0:T(8,128)(2,1)} %param.8), kind=kOutput, calls=%fused_computation.17 | convolution fusion | flops 9664462848 | bytes 26738688 | tf_op jit(solution)/shard_map/dot_general | solution.py:22
  369.4 20.7 %convolution_convert_fusion.9.far_ref = bf16[512,2048]{1,0:T(8,128)(2,1)} fusion(bf16[512,6144]{1,0:T(8,128)(2,1)} %all-gather.17.cloned.1.call-done.refs_1_, bf16[6144,2048]{1,0:T(8,128)(2,1)} %bitcast.42), kind=kOutput, calls=%fused_computation.11 | convolution fusion | flops 12885950464 | bytes 33554432 | tf_op jit(solution)/shard_map/dot_general | solution.py:22
  390.1 31.7 %attn_fwd.2 = (bf16[512,1536]{1,0:T(8,128)(2,1)S(1)}, bf16[512,1536]{1,0:T(8,128)(2,1)S(1)}, f32[1024,1536]{1,0:T(8,128)}) custom-call(bf16[512,2048]{1,0:T(8,128)(2,1)} %convolution_convert_fusion.11.own_ref, bf16[512,2048]{1,0:T(8,128)(2,1)} %convolution_convert_fusion.9.far_ref, f32[1024,128]{1,0:T(8,128)S(1)} %get-tuple-element.94.cos_ref, ...), custom_call_target="tpu_custom_call" | custom-call | flops 12000000000 | bytes 14000000 | tf_op jit(solution)/shard_map/attn_fwd/pallas_call | solution.py:164
  471.3 20.9 %convolution_convert_fusion.8.far_ref = bf16[512,2048]{1,0:T(8,128)(2,1)} fusion(bf16[512,6144]{1,0:T(8,128)(2,1)} %all-gather.13.cloned.1.call-done.refs_3_, bf16[6144,2048]{1,0:T(8,128)(2,1)} %bitcast.43), kind=kOutput, calls=%fused_computation.10 | convolution fusion | flops 12885950464 | bytes 33554432 | tf_op jit(solution)/shard_map/dot_general | solution.py:22
  492.3 31.7 %attn_fwd.3 = (bf16[512,1536]{1,0:T(8,128)(2,1)S(1)}, bf16[512,1536]{1,0:T(8,128)(2,1)S(1)}, f32[1024,1536]{1,0:T(8,128)}) custom-call(bf16[512,2048]{1,0:T(8,128)(2,1)} %convolution_convert_fusion.10.own_ref, bf16[512,2048]{1,0:T(8,128)(2,1)} %convolution_convert_fusion.8.far_ref, f32[1024,128]{1,0:T(8,128)S(1)} %get-tuple-element.94.cos_ref, ...), custom_call_target="tpu_custom_call" | custom-call | flops 12000000000 | bytes 14000000 | tf_op jit(solution)/shard_map/attn_fwd/pallas_call | solution.py:164
  541.3 19.7 %convolution_convert_fusion.13.dfar_ref = bf16[512,1536]{1,0:T(8,128)(2,1)} fusion(bf16[512,6144]{1,0:T(8,128)(2,1)} %all-gather.21.cloned.1.call-done.refs_5_, bf16[1536,6144]{1,0:T(8,128)(2,1)} %param.8), kind=kOutput, calls=%fused_computation.15 | convolution fusion | flops 9664462848 | bytes 26738688 | tf_op jit(solution)/shard_map/dot_general | solution.py:22
  561.0 36.2 %attn_bwd.2 = (bf16[512,2048]{1,0:T(8,128)(2,1)}, bf16[512,2048]{1,0:T(8,128)(2,1)}) custom-call(bf16[512,2048]{1,0:T(8,128)(2,1)} %convolution_convert_fusion.11.own_ref, bf16[512,2048]{1,0:T(8,128)(2,1)} %convolution_convert_fusion.9.far_ref, bf16[512,1536]{1,0:T(8,128)(2,1)} %copy-done.2, bf16[512,1536]{1,0:T(8,128)(2,1)} %copy-done.3, ...), custom_call_target="tpu_custom_call" | custom-call | flops 24999999488 | bytes 22000000 | tf_op jit(solution)/shard_map/attn_bwd/pallas_call | solution.py:183
  597.2 19.0 %convolution_convert_fusion.3 = bf16[512,6144]{1,0:T(8,128)(2,1)} fusion(bf16[512,2048]{1,0:T(8,128)(2,1)} %get-tuple-element.70.refs_5_, bf16[6144,2048]{1,0:T(8,128)(2,1)} %bitcast.44), kind=kOutput, calls=%fused_computation.3 | convolution fusion | flops 12888047616 | bytes 33554432 | tf_op jit(solution)/shard_map/dot_general | solution.py:22
  649.5 34.1 %attn_bwd.3 = (bf16[512,2048]{1,0:T(8,128)(2,1)}, bf16[512,2048]{1,0:T(8,128)(2,1)}) custom-call(bf16[512,2048]{1,0:T(8,128)(2,1)} %convolution_convert_fusion.10.own_ref, bf16[512,2048]{1,0:T(8,128)(2,1)} %convolution_convert_fusion.8.far_ref, bf16[512,1536]{1,0:T(8,128)(2,1)} %copy-done.4, bf16[512,1536]{1,0:T(8,128)(2,1)} %copy-done.5, ...), custom_call_target="tpu_custom_call" | custom-call | flops 24999999488 | bytes 22000000 | tf_op jit(solution)/shard_map/attn_bwd/pallas_call | solution.py:183
  683.6 19.1 %convolution_convert_fusion.2 = bf16[512,6144]{1,0:T(8,128)(2,1)} fusion(bf16[512,2048]{1,0:T(8,128)(2,1)} %get-tuple-element.76.refs_7_, bf16[6144,2048]{1,0:T(8,128)(2,1)} %bitcast.45), kind=kOutput, calls=%fused_computation.2 | convolution fusion | flops 12888047616 | bytes 33554432 | tf_op jit(solution)/shard_map/dot_general | solution.py:22
  704.3 18.9 %convolution_convert_fusion.1 = bf16[512,6144]{1,0:T(8,128)(2,1)} fusion(bf16[512,2048]{1,0:T(8,128)(2,1)S(1)} %copy-done.11, bf16[6144,2048]{1,0:T(8,128)(2,1)} %bitcast.46), kind=kOutput, calls=%fused_computation.1 | convolution fusion | flops 12888047616 | bytes 33554432 | tf_op jit(solution)/shard_map/dot_general | solution.py:22
  725.6 19.3 %convolution_convert_fusion = bf16[512,6144]{1,0:T(8,128)(2,1)} fusion(bf16[512,2048]{1,0:T(8,128)(2,1)S(1)} %copy-done.12, bf16[6144,2048]{1,0:T(8,128)(2,1)} %bitcast.47), kind=kOutput, calls=%fused_computation | convolution fusion | flops 12888047616 | bytes 33554432 | tf_op jit(solution)/shard_map/dot_general | solution.py:22
  747.0 46.8 %dw_out.1 = bf16[1536,6144]{1,0:T(8,128)(2,1)} custom-call(bf16[512,1536]{1,0:T(8,128)(2,1)} %copy-done.2, bf16[512,1536]{1,0:T(8,128)(2,1)} %copy-done.3, bf16[512,1536]{1,0:T(8,128)(2,1)} %copy-done.4, bf16[512,1536]{1,0:T(8,128)(2,1)} %copy-done.5, bf16[512,6144]{1,0:T(8,128)(2,1)} %all-gather.19.cloned.1.call-done.refs_4_, ...), custom_call_target="tpu_custom_call" | custom-call | flops 38999998464 | bytes 50000000 | tf_op jit(solution)/shard_map/dw_out/pallas_call | solution.py:233
  795.9 20.4 %collective-permute-done.4.far_ref = bf16[256,6144]{1,0:T(8,128)(2,1)} collective-permute-done((bf16[256,6144]{1,0:T(8,128)(2,1)}, bf16[256,6144]{1,0:T(8,128)(2,1)}, u32[]{:S(2)}, u32[]{:S(2)}) %collective-permute-start.4) | collective-permute-done | bytes 3145760 | tf_op jit(solution)/shard_map/ppermute | solution.py:329
  822.5 61.2 %collective-permute-done.5.far_ref = bf16[256,6144]{1,0:T(8,128)(2,1)} collective-permute-done((bf16[256,6144]{1,0:T(8,128)(2,1)}, bf16[256,6144]{1,0:T(8,128)(2,1)}, u32[]{:S(2)}, u32[]{:S(2)}) %collective-permute-start.5) | collective-permute-done | bytes 3145760 | tf_op jit(solution)/shard_map/ppermute | solution.py:329
  889.9 63.9 %dw_qkv.1 = bf16[6144,2,1024]{2,1,0:T(2,128)(2,1)} custom-call(bf16[512,6144]{1,0:T(8,128)(2,1)} %all-gather.11.cloned.1.call-done.refs_0_, bf16[512,6144]{1,0:T(8,128)(2,1)} %all-gather.17.cloned.1.call-done.refs_1_, bf16[512,6144]{1,0:T(8,128)(2,1)} %all-gather.9.cloned.1.call-done.refs_2_, bf16[512,6144]{1,0:T(8,128)(2,1)} %all-gather.13.cloned.1.call-done.refs_3_, ...), custom_call_target="tpu_custom_call" | custom-call | flops 51000000512 | bytes 60000000 | tf_op jit(solution)/shard_map/dw_qkv/pallas_call | solution.py:211
  965.7 41.3 %collective-permute-done.7.far_ref = bf16[256,6144]{1,0:T(8,128)(2,1)S(1)} collective-permute-done((bf16[256,6144]{1,0:T(8,128)(2,1)}, bf16[256,6144]{1,0:T(8,128)(2,1)S(1)}, u32[]{:S(2)}, u32[]{:S(2)}) %collective-permute-start.7) | collective-permute-done | bytes 3145760 | tf_op jit(solution)/shard_map/ppermute | solution.py:329
  (107 shorter events, 186.6 us)
Async XLA Ops:
  7.2 302.2 %all-gather.11.cloned.1.call-start = ((), (), s32[]{:S(2)}) async-start(), calls=%async_computation.9 | async-start | bytes 9437184 | tf_op jit(solution)/shard_map/all_gather | solution.py:332
  14.1 317.6 %all-gather.9.cloned.1.call-start = ((), (), s32[]{:S(2)}) async-start(), calls=%async_computation.8 | async-start | bytes 9437184 | tf_op jit(solution)/shard_map/all_gather | solution.py:332
  19.8 332.6 %all-gather.19.cloned.1.call-start = ((), (), s32[]{:S(2)}) async-start(), calls=%async_computation.13 | async-start | bytes 9437184 | tf_op jit(solution)/shard_map/all_gather | solution.py:332
  27.8 341.6 %all-gather.17.cloned.1.call-start = ((), (), s32[]{:S(2)}) async-start(), calls=%async_computation.12 | async-start | bytes 9437184 | tf_op jit(solution)/shard_map/all_gather | solution.py:332
  27.9 71.3 %collective-permute-start.1 = (bf16[256,6144]{1,0:T(8,128)(2,1)S(1)}, bf16[256,6144]{1,0:T(8,128)(2,1)}, u32[]{:S(2)}, u32[]{:S(2)}) collective-permute-start(bf16[256,6144]{1,0:T(8,128)(2,1)S(1)} %copy-done.6), channel_id=1, source_target_pairs={{0,2},{1,3},{2,0},{3,1},{4,6},{5,7},{6,4},{7,5}} | collective-permute-start | bytes 9437192 | tf_op jit(solution)/shard_map/ppermute | solution.py:329
  99.2 355.4 %all-gather.15.cloned.1.call-start = ((), (), s32[]{:S(2)}) async-start(), calls=%async_computation.11 | async-start | bytes 9437184 | tf_op jit(solution)/shard_map/all_gather | solution.py:332
  99.8 371.5 %all-gather.13.cloned.1.call-start = ((), (), s32[]{:S(2)}) async-start(), calls=%async_computation.10 | async-start | bytes 9437184 | tf_op jit(solution)/shard_map/all_gather | solution.py:332
  101.1 69.4 %collective-permute-start = (bf16[256,6144]{1,0:T(8,128)(2,1)S(1)}, bf16[256,6144]{1,0:T(8,128)(2,1)}, u32[]{:S(2)}, u32[]{:S(2)}) collective-permute-start(bf16[256,6144]{1,0:T(8,128)(2,1)S(1)} %copy-done.7), channel_id=1, source_target_pairs={{0,2},{1,3},{2,0},{3,1},{4,6},{5,7},{6,4},{7,5}} | collective-permute-start | bytes 9437192 | tf_op jit(solution)/shard_map/ppermute | solution.py:329
  170.6 370.7 %all-gather.21.cloned.1.call-start = ((), (), s32[]{:S(2)}) async-start(), calls=%async_computation.14 | async-start | bytes 9437184 | tf_op jit(solution)/shard_map/all_gather | solution.py:332
  170.6 68.7 %collective-permute-start.2 = (bf16[256,6144]{1,0:T(8,128)(2,1)}, bf16[256,6144]{1,0:T(8,128)(2,1)S(1)}, u32[]{:S(2)}, u32[]{:S(2)}) collective-permute-start(bf16[256,6144]{1,0:T(8,128)(2,1)} %get-tuple-element.52), channel_id=1, source_target_pairs={{0,2},{1,3},{2,0},{3,1},{4,6},{5,7},{6,4},{7,5}} | collective-permute-start | bytes 9437192 | tf_op jit(solution)/shard_map/ppermute | solution.py:329
  241.0 391.9 %all-gather.23.cloned.1.call-start = ((), (), s32[]{:S(2)}) async-start(), calls=%async_computation.17 | async-start | bytes 9437184 | tf_op jit(solution)/shard_map/all_gather | solution.py:332
  241.1 68.0 %collective-permute-start.3 = (bf16[256,6144]{1,0:T(8,128)(2,1)}, bf16[256,6144]{1,0:T(8,128)(2,1)}, u32[]{:S(2)}, u32[]{:S(2)}) collective-permute-start(bf16[256,6144]{1,0:T(8,128)(2,1)} %get-tuple-element.51), channel_id=1, source_target_pairs={{0,2},{1,3},{2,0},{3,1},{4,6},{5,7},{6,4},{7,5}} | collective-permute-start | bytes 9437192 | tf_op jit(solution)/shard_map/ppermute | solution.py:329
  309.1 435.9 %reduce-scatter.13.cloned.1.call-start = ((), (), s32[]{:S(2)}) async-start(), calls=%async_computation.18 | async-start | bytes 9437184 | tf_op jit(solution)/shard_map/reduce_scatter | solution.py:335
  438.6 306.5 %reduce-scatter.15.cloned.1.call-start = ((), (), s32[]{:S(2)}) async-start(), calls=%async_computation.19 | async-start | bytes 9437184 | tf_op jit(solution)/shard_map/reduce_scatter | solution.py:335
  540.5 253.3 %reduce-scatter.11.cloned.1.call-start = ((), (), s32[]{:S(2)}) async-start(), calls=%async_computation.16 | async-start | bytes 9437184 | tf_op jit(solution)/shard_map/reduce_scatter | solution.py:335
  541.3 252.6 %reduce-scatter.21.cloned.1.call-start = ((), (), s32[]{:S(2)}) async-start(), calls=%async_computation.22 | async-start | bytes 9437184 | tf_op jit(solution)/shard_map/reduce_scatter | solution.py:335
  616.2 177.8 %reduce-scatter.23.cloned.1.call-start = ((), (), s32[]{:S(2)}) async-start(), calls=%async_computation.23 | async-start | bytes 9437184 | tf_op jit(solution)/shard_map/reduce_scatter | solution.py:335
  702.7 119.8 %reduce-scatter.9.cloned.1.call-start = ((), (), s32[]{:S(2)}) async-start(), calls=%async_computation.15 | async-start | bytes 9437184 | tf_op jit(solution)/shard_map/reduce_scatter | solution.py:335
  703.3 250.5 %reduce-scatter.19.cloned.1.call-start = ((), (), s32[]{:S(2)}) async-start(), calls=%async_computation.21 | async-start | bytes 9437184 | tf_op jit(solution)/shard_map/reduce_scatter | solution.py:335
  723.2 242.5 %reduce-scatter.17.cloned.1.call-start = ((), (), s32[]{:S(2)}) async-start(), calls=%async_computation.20 | async-start | bytes 9437184 | tf_op jit(solution)/shard_map/reduce_scatter | solution.py:335
  745.0 71.3 %collective-permute-start.4 = (bf16[256,6144]{1,0:T(8,128)(2,1)}, bf16[256,6144]{1,0:T(8,128)(2,1)}, u32[]{:S(2)}, u32[]{:S(2)}) collective-permute-start(bf16[256,6144]{1,0:T(8,128)(2,1)} %reduce-scatter.13.cloned.1.call-done), channel_id=1, source_target_pairs={{0,2},{1,3},{2,0},{3,1},{4,6},{5,7},{6,4},{7,5}} | collective-permute-start | bytes 9437192 | tf_op jit(solution)/shard_map/ppermute | solution.py:329
  745.0 138.7 %collective-permute-start.5 = (bf16[256,6144]{1,0:T(8,128)(2,1)}, bf16[256,6144]{1,0:T(8,128)(2,1)}, u32[]{:S(2)}, u32[]{:S(2)}) collective-permute-start(bf16[256,6144]{1,0:T(8,128)(2,1)} %reduce-scatter.15.cloned.1.call-done), channel_id=1, source_target_pairs={{0,2},{1,3},{2,0},{3,1},{4,6},{5,7},{6,4},{7,5}} | collective-permute-start | bytes 9437192 | tf_op jit(solution)/shard_map/ppermute | solution.py:329
  793.8 159.9 %collective-permute-start.6 = (bf16[256,6144]{1,0:T(8,128)(2,1)}, bf16[256,6144]{1,0:T(8,128)(2,1)}, u32[]{:S(2)}, u32[]{:S(2)}) collective-permute-start(bf16[256,6144]{1,0:T(8,128)(2,1)} %reduce-scatter.21.cloned.1.call-done), channel_id=1, source_target_pairs={{0,2},{1,3},{2,0},{3,1},{4,6},{5,7},{6,4},{7,5}} | collective-permute-start | bytes 9437192 | tf_op jit(solution)/shard_map/ppermute | solution.py:329
  793.9 213.1 %collective-permute-start.7 = (bf16[256,6144]{1,0:T(8,128)(2,1)}, bf16[256,6144]{1,0:T(8,128)(2,1)S(1)}, u32[]{:S(2)}, u32[]{:S(2)}) collective-permute-start(bf16[256,6144]{1,0:T(8,128)(2,1)} %reduce-scatter.23.cloned.1.call-done), channel_id=1, source_target_pairs={{0,2},{1,3},{2,0},{3,1},{4,6},{5,7},{6,4},{7,5}} | collective-permute-start | bytes 9437192 | tf_op jit(solution)/shard_map/ppermute | solution.py:329
  (15 other events, 632.9 us)
Sparse Core Ops, SparseCore 0:
  14.2 16.7 all-gather.10
  33.1 15.1 all-gather.8
  50.4 15.1 all-gather.18
  99.4 15.1 all-gather.16
  116.0 15.1 all-gather.14
  170.7 14.9 all-gather.12
  241.2 14.7 all-gather.20
  309.2 14.5 all-gather.22
  438.7 11.1 reduce-scatter.12
  540.6 10.6 reduce-scatter.14
  553.6 13.2 reduce-scatter.10
  616.3 9.8 reduce-scatter.20
  702.8 9.8 reduce-scatter.22
  714.8 13.2 reduce-scatter.8
  730.3 13.2 reduce-scatter.18
  745.7 13.2 reduce-scatter.16
where the time goes:
time: 1040 us; the launch traced here: 1030 us
  waiting for transfers between devices  371 us (36%)
  matrix products  295 us (28%)
  Pallas kernels  291 us (28%)
  local copies, waits for them, and re-layouts  43.4 us (4%)
  between operations  14.6 us (1%)
  starting transfers between devices  14 us (1%)
    ppermute x10, waiting for transfers between devices, swap(): return lax.ppermute(value, 'tp', [(i, i ^ bit) for i in range(n_tp)])  369 us
    dot_general x16, matrix products, dot(): return lax.dot_general(a, b, dims, preferred_element_type=jnp.float32)  295 us
    pallas_call x2, Pallas kernels, attn_bwd(): pl.pallas_call(functools.partial(attn_bwd_kernel, groups), grid=(kv_loc,)...  70.2 us
    pallas_call x1, Pallas kernels, dw_qkv(): pl.pallas_call(functools.partial(dw_qkv_kernel, len(acts)), grid=(d_model...  63.9 us
    pallas_call x2, Pallas kernels, attn_fwd(): pl.pallas_call(functools.partial(attn_fwd_kernel, groups), grid=(kv_loc,)...  63.3 us
    pallas_call x1, Pallas kernels, dw_out(): pl.pallas_call(functools.partial(dw_out_kernel, len(acts)), grid=(d_model...  46.8 us
    unnamed x27, local copies, waits for them, and re-layouts  35.4 us
    pallas_call x2, Pallas kernels, norm_bwd(): pl.pallas_call(norm_bwd_kernel, grid=(rows // tile,), in_specs=[whole, wh...  23.4 us
  transfers between devices with their start and end apart: 26, of which 9 were waited for; matrix products, arithmetic and copies ran while one was open for 32% of the time, Pallas kernels for 27%

commit v1 on v0

--- a/solution.py
+++ b/solution.py
@@ -66,7 +66,7 @@
     return pl.ds(pl.multiple_of(start * size, size), size)
 
 
-def attn_fwd_kernel(groups, own_ref, far_ref, cos_ref, sin_ref, oown_ref, ofar_ref, lse_ref, qkv_ref, out_ref, k_scr, v_scr):
+def attn_fwd_kernel(groups, own_ref, far_ref, cos_ref, sin_ref, oown_ref, ofar_ref, lse_ref, qkv_ref, out_ref, k_scr, v_scr, s_scr, p_scr):
     half = own_ref.shape[0]
     own, far = half_rows(True, half), half_rows(False, half)
     qkv_ref[own, :] = own_ref[...]
@@ -74,24 +74,49 @@
     seq_len = qkv_ref.shape[0]
     k_col = groups * HEAD_DIM
     k_scr[...] = rotate(clipped(qkv_ref[:, k_col:k_col + HEAD_DIM]), cos_ref[...], sin_ref[...])
-    v_scr[...] = clipped(qkv_ref[:, k_col + HEAD_DIM:k_col + 2 * HEAD_DIM]).astype(jnp.bfloat16)
-    mask = diagonal_mask()
+    v_scr[...] = clipped(qkv_ref[:, k_col + HEAD_DIM:k_col + 2 * HEAD_DIM]).T.astype(jnp.bfloat16)
+    row = lax.broadcasted_iota(jnp.int32, (TILE_Q, TILE_Q), 0)
+    col = lax.broadcasted_iota(jnp.int32, (TILE_Q, TILE_Q), 1)
+    mask = row <= col
     coef = HEAD_DIM ** -0.5 * LOG2E
 
     def head(g, carry):
         cols = pl.ds(pl.multiple_of(g * HEAD_DIM, HEAD_DIM), HEAD_DIM)
-        for qi in range(seq_len // TILE_Q):
+
+        def scored(qi):
             rows = slice(qi * TILE_Q, (qi + 1) * TILE_Q)
-            width = (qi + 1) * TILE_Q
             query = rotate(clipped(qkv_ref[rows, cols]), cos_ref[rows, :], sin_ref[rows, :])
-            scores = mask_scores(dot(query, k_scr[:width, :], NT), width, mask)
-            peak = jnp.max(scores, axis=1, keepdims=True)
-            prob = jnp.exp2((scores - peak) * coef)
-            total = jnp.sum(prob, axis=1, keepdims=True)
-            prob = (prob * (1.0 / total)).astype(jnp.bfloat16)
-            out_ref[rows, cols] = dot(prob, v_scr[:width, :], NN).astype(jnp.bfloat16)
-            lse = peak * coef + jnp.log2(total)
-            lse_ref[rows, cols] = jnp.broadcast_to(lse, (TILE_Q, HEAD_DIM))
+            peak = None
+            for kj in range(qi + 1):
+                keys = slice(kj * TILE_Q, (kj + 1) * TILE_Q)
+                scores = dot(k_scr[keys, :], query, NT)
+                if kj == qi:
+                    scores = jnp.where(mask, scores, NEG_BIG)
+                s_scr[qi % 2, keys, :] = scores
+                part = jnp.max(scores.reshape(TILE_Q // 8, 8, TILE_Q), axis=0)
+                peak = part if peak is None else jnp.maximum(peak, part)
+            return jnp.max(peak, axis=0, keepdims=True) * coef
+
+        def mixed(qi, shift):
+            rows = slice(qi * TILE_Q, (qi + 1) * TILE_Q)
+            total = None
+            for kj in range(qi + 1):
+                keys = slice(kj * TILE_Q, (kj + 1) * TILE_Q)
+                prob = jnp.exp2(s_scr[qi % 2, keys, :] * coef - shift)
+                p_scr[qi % 2, keys, :] = prob.astype(jnp.bfloat16)
+                part = jnp.sum(prob.reshape(TILE_Q // 8, 8, TILE_Q), axis=0)
+                total = part if total is None else total + part
+            total = jnp.sum(total, axis=0, keepdims=True)
+            out = dot(v_scr[:, :(qi + 1) * TILE_Q], p_scr[qi % 2, :(qi + 1) * TILE_Q, :], NN)
+            out_ref[rows, cols] = (out * (1.0 / total)).T.astype(jnp.bfloat16)
+            lse_ref[rows, cols] = jnp.broadcast_to(shift + jnp.log2(total), (HEAD_DIM, TILE_Q)).T
+
+        tiles = seq_len // TILE_Q
+        shift = scored(0)
+        for qi in range(tiles):
+            later = scored(qi + 1) if qi + 1 < tiles else None
+            mixed(qi, shift)
+            shift = later
         return carry
 
     lax.fori_loop(0, groups, head, 0)
@@ -167,7 +192,7 @@
         in_specs=[full, full, table, table],
         out_specs=[part, part, lse],
         out_shape=[rows, rows, jax.ShapeDtypeStruct((2 * half, kv_loc * wide), jnp.float32)],
-        scratch_shapes=[pltpu.VMEM((2 * half, slot), jnp.bfloat16), pltpu.VMEM((2 * half, wide), jnp.bfloat16)] + [pltpu.VMEM((2 * half, HEAD_DIM), jnp.bfloat16)] * 2,
+        scratch_shapes=[pltpu.VMEM((2 * half, slot), jnp.bfloat16), pltpu.VMEM((2 * half, wide), jnp.bfloat16), pltpu.VMEM((2 * half, HEAD_DIM), jnp.bfloat16), pltpu.VMEM((HEAD_DIM, 2 * half), jnp.bfloat16), pltpu.VMEM((2, 2 * half, TILE_Q), jnp.float32), pltpu.VMEM((2, 2 * half, TILE_Q), jnp.bfloat16)],
         compiler_params=pltpu.CompilerParams(vmem_limit_bytes=48 * 2 ** 20),
         cost_estimate=pl.CostEstimate(flops=12 * 10 ** 9, bytes_accessed=14 * 10 ** 6, transcendentals=0),
         name="attn_fwd",
@@ -227,19 +252,18 @@
 
 def dw_out(acts, grads, tile=512):
     rows, width = acts[0].shape
-    d_model = grads[0].shape[-1]
+    d_model = grads[0][1].shape[-1]
     whole = pl.BlockSpec((rows, width), lambda i: (0, 0))
-    part = pl.BlockSpec((rows, tile), lambda i: (0, i))
     return pl.pallas_call(
         functools.partial(dw_out_kernel, len(acts)),
         grid=(d_model // tile,),
-        in_specs=[whole] * len(acts) + [part] * len(grads),
+        in_specs=[whole] * len(acts) + [part_spec(g, b, (rows, tile), lambda i: (0, i)) for b, g in grads],
         out_specs=pl.BlockSpec((width, tile), lambda i: (0, i)),
         out_shape=jax.ShapeDtypeStruct((width, d_model), jnp.bfloat16),
         compiler_params=pltpu.CompilerParams(vmem_limit_bytes=60 * 2 ** 20),
         cost_estimate=pl.CostEstimate(flops=39 * 10 ** 9, bytes_accessed=50 * 10 ** 6, transcendentals=0),
         name="dw_out",
-    )(*acts, *grads)
+    )(*acts, *[g for _, g in grads])
 
 
 def normalized(x_f32):
@@ -250,7 +274,7 @@
 
 def norm_fwd_kernel(x_ref, gain_ref, h_ref):
     hat, _ = normalized(x_ref[0].astype(jnp.float32))
-    h_ref[...] = (hat * gain_ref[...]).astype(jnp.bfloat16)
+    h_ref[...] = (hat * gain_ref[...].astype(jnp.float32)).astype(jnp.bfloat16)
 
 
 def norm_fwd(x_seq, gain, b, tile=64):
@@ -272,18 +296,28 @@
 
 
 def norm_bwd_kernel(x_ref, dy_ref, gain_ref, near_ref, far_ref, *rest):
-    dx_ref, dgain_ref = rest[-2:]
-    hat, rstd = normalized(x_ref[0].astype(jnp.float32))
-    dh = (near_ref[...].astype(jnp.float32) + far_ref[...].astype(jnp.float32)).astype(jnp.bfloat16).astype(jnp.float32)
+    dx_ref, dgain_ref, sum_ref = rest[-3:]
 
     @pl.when(pl.program_id(0) == 0)
     def _():
-        dgain_ref[...] = jnp.zeros_like(dgain_ref)
-
-    dgain_ref[...] += jnp.sum(dh * hat, axis=0, keepdims=True)
-    dhat = dh * gain_ref[...]
-    inner = dhat - jnp.mean(dhat, axis=-1, keepdims=True) - hat * jnp.mean(dhat * hat, axis=-1, keepdims=True)
-    dx_ref[0] = (dy_ref[0].astype(jnp.float32) + inner * rstd).astype(jnp.bfloat16)
+        sum_ref[...] = jnp.zeros_like(sum_ref)
+
+    def group(i, carry):
+        rows = pl.ds(pl.multiple_of(i * 16, 16), 16)
+        hat, rstd = normalized(x_ref[0, rows, :].astype(jnp.float32))
+        dh = (near_ref[rows, :].astype(jnp.float32) + far_ref[rows, :].astype(jnp.float32)).astype(jnp.bfloat16).astype(jnp.float32)
+        prod = dh * hat
+        sum_ref[...] += prod[:8] + prod[8:]
+        dhat = dh * gain_ref[...].astype(jnp.float32)
+        inner = dhat - jnp.mean(dhat, axis=-1, keepdims=True) - hat * jnp.mean(dhat * hat, axis=-1, keepdims=True)
+        dx_ref[0, rows, :] = (dy_ref[0, rows, :].astype(jnp.float32) + inner * rstd).astype(jnp.bfloat16)
+        return carry
+
+    lax.fori_loop(0, x_ref.shape[1] // 16, group, 0, unroll=2)
+
+    @pl.when(pl.program_id(0) == pl.num_programs(0) - 1)
+    def _():
+        dgain_ref[...] = jnp.sum(sum_ref[...], axis=0, keepdims=True)
 
 
 def residual(x_seq, near, far, b, held, tile=64):
@@ -303,24 +337,92 @@
     )(x_seq, near, far, *keep)
 
 
-def norm_bwd(x_seq, y_grad, gain, near, far, b, held, tile=64):
-    _, rows, d_model = x_seq.shape
-    whole = pl.BlockSpec((1, tile, d_model), lambda i: (b, i, 0))
-    part = pl.BlockSpec((tile, d_model), lambda i: (i, 0))
+def norm_bwd(x_seq, y_grad, gain, near, far, b, base, held, tile=64):
+    _, _, d_model = x_seq.shape
+    first = base // tile
+    whole = pl.BlockSpec((1, tile, d_model), lambda i: (b, first + i, 0))
+    part = pl.BlockSpec((tile, d_model), lambda i: (first + i, 0))
+    piece = pl.BlockSpec((tile, d_model), lambda i: (i, 0))
     row = pl.BlockSpec((1, d_model), lambda i: (0, 0))
     keep = [] if held is None else [held]
     return pl.pallas_call(
         norm_bwd_kernel,
-        grid=(rows // tile,),
-        in_specs=[whole, whole, row, part, part] + [pl.BlockSpec(memory_space=pl.ANY)] * len(keep),
+        grid=(far.shape[0] // tile,),
+        in_specs=[whole, whole, row, part, piece] + [pl.BlockSpec(memory_space=pl.ANY)] * len(keep),
         out_specs=[whole, row],
         out_shape=[jax.ShapeDtypeStruct(x_seq.shape, jnp.bfloat16), jax.ShapeDtypeStruct((1, d_model), jnp.float32)],
         input_output_aliases={5: 0} if keep else {},
+        scratch_shapes=[pltpu.VMEM((8, d_model), jnp.float32)],
         cost_estimate=pl.CostEstimate(flops=4 * 10 ** 9, bytes_accessed=16 * 10 ** 6, transcendentals=0),
         name="norm_bwd",
     )(x_seq, y_grad, gain, near, far, *keep)
 
 
+def proj_deep_kernel(n_parts, dims, *refs):
+    parts, w_ref, outs, accs = refs[:n_parts], refs[n_parts], refs[n_parts + 1:2 * n_parts + 1], refs[2 * n_parts + 1:]
+    step, last = pl.program_id(0), pl.num_programs(0) - 1
+
+    @pl.when(step == 0)
+    def _():
+        for a, acc in zip(parts, accs):
+            acc[...] = dot(a[...], w_ref[...], dims)
+
+    @pl.when((step > 0) & (step < last))
+    def _():
+        for a, acc in zip(parts, accs):
+            acc[...] += dot(a[...], w_ref[...], dims)
+
+    @pl.when(step == last)
+    def _():
+        for a, acc, out in zip(parts, accs, outs):
+            out[...] = (acc[...] + dot(a[...], w_ref[...], dims)).astype(jnp.bfloat16)
+
+
+def part_spec(a, b, block, index):
+    if a.ndim == 2:
+        return pl.BlockSpec(block, index)
+    return pl.BlockSpec((None,) + block, lambda i: (b,) + index(i))
+
+
+def proj_deep(parts, w, dims, tile=1024):
+    rows, depth = parts[0].shape[-2:]
+    width = w.shape[0] if dims is NT else w.shape[1]
+    w_spec = pl.BlockSpec((width, tile), lambda i: (0, i)) if dims is NT else pl.BlockSpec((tile, width), lambda i: (i, 0))
+    return pl.pallas_call(
+        functools.partial(proj_deep_kernel, len(parts), dims),
+        grid=(depth // tile,),
+        in_specs=[part_spec(a, b, (rows, tile), lambda i: (0, i)) for b, a in enumerate(parts)] + [w_spec],
+        out_specs=[pl.BlockSpec((rows, width), lambda i: (0, 0))] * len(parts),
+        out_shape=[jax.ShapeDtypeStruct((rows, width), jnp.bfloat16)] * len(parts),
+        scratch_shapes=[pltpu.VMEM((rows, width), jnp.float32)] * len(parts),
+        compiler_params=pltpu.CompilerParams(vmem_limit_bytes=60 * 2 ** 20),
+        cost_estimate=pl.CostEstimate(flops=2 * len(parts) * rows * depth * width, bytes_accessed=2 * depth * width, transcendentals=0),
+        name="proj_deep",
+    )(*parts, w)
+
+
+def proj_wide_kernel(n_parts, dims, *refs):
+    w_ref = refs[n_parts]
+    for a, out in zip(refs[:n_parts], refs[n_parts + 1:]):
+        out[...] = dot(a[...], w_ref[...], dims).astype(jnp.bfloat16)
+
+
+def proj_wide(parts, w, dims, tile=1024):
+    rows, depth = parts[0].shape
+    width = w.shape[0] if dims is NT else w.shape[1]
+    w_spec = pl.BlockSpec((tile, depth), lambda i: (i, 0)) if dims is NT else pl.BlockSpec((depth, tile), lambda i: (0, i))
+    return pl.pallas_call(
+        functools.partial(proj_wide_kernel, len(parts), dims),
+        grid=(width // tile,),
+        in_specs=[pl.BlockSpec((rows, depth), lambda i: (0, 0))] * len(parts) + [w_spec],
+        out_specs=[pl.BlockSpec((rows, tile), lambda i: (0, i))] * len(parts),
+        out_shape=[jax.ShapeDtypeStruct((rows, width), jnp.bfloat16)] * len(parts),
+        compiler_params=pltpu.CompilerParams(vmem_limit_bytes=60 * 2 ** 20),
+        cost_estimate=pl.CostEstimate(flops=2 * len(parts) * rows * depth * width, bytes_accessed=2 * depth * width, transcendentals=0),
+        name="proj_wide",
+    )(*parts, w)
+
+
 def solution(mesh):
     n_tp = mesh.shape["tp"]
     pairs = [[i, i + 1] for i in range(0, n_tp, 2)]
@@ -328,15 +430,15 @@
     def swap(value, bit):
         return lax.ppermute(value, "tp", [(i, i ^ bit) for i in range(n_tp)])
 
-    def pair_gather(value):
-        return lax.all_gather(value, "tp", axis_index_groups=pairs, axis=0, tiled=True)
+    def pair_gather(value, axis=0):
+        return lax.all_gather(value, "tp", axis_index_groups=pairs, axis=axis, tiled=True)
 
     def pair_scatter(value):
         return lax.psum_scatter(value, "tp", axis_index_groups=pairs, scatter_dimension=0, tiled=True)
 
     def staged_step(x_seq, ln_gain, w_qkv, w_out, y_grad):
         kv_loc = w_qkv.shape[1]
-        gain = ln_gain.astype(jnp.float32)[None, :]
+        gain = ln_gain[None, :]
         token = [None]
 
         def run(fn, lead, *rest):
@@ -345,9 +447,6 @@
             result = fn(lead, *rest)
             token[0] = jax.tree.leaves(result)[0]
             return result
-
-        def matmul(dims):
-            return lambda a, b: dot(a, b, dims).astype(jnp.bfloat16)
 
         cos_t, sin_t = rope_tables(x_seq.shape[1] * n_tp)
         h0 = run(lambda x: norm_fwd(x, gain, 0), x_seq)
@@ -358,53 +457,44 @@
         dyx0 = swap(dy0, 2)
         dyx1 = swap(dy1, 2)
         h_own0, h_own1 = pair_gather(h0), pair_gather(h1)
-        dy_own0, dy_own1 = pair_gather(dy0), pair_gather(dy1)
+        dy_own = pair_gather(y_grad, 1)
         w_flat = run(lambda w: lax.optimization_barrier(w.reshape(w.shape[0], -1)), w_qkv)
-        qkv_own0 = run(matmul(NN), h_own0, w_flat)
-        qkv_own1 = run(matmul(NN), h_own1, w_flat)
+        qkv_own0, qkv_own1 = run(lambda h: proj_deep([h, h_own1], w_flat, NN), h_own0)
         h_far0 = pair_gather(hx0)
-        dattn_own0 = run(matmul(NT), dy_own0, w_out)
-        qkv_far0 = run(matmul(NN), h_far0, w_flat)
+        dattn_own0, dattn_own1 = run(lambda d: proj_deep([d, d], w_out, NT), dy_own)
+        (qkv_far0,) = run(lambda h: proj_deep([h], w_flat, NN), h_far0)
         attn_own0, attn_far0, lse0 = run(lambda far: attn_fwd(qkv_own0, far, cos_t, sin_t, kv_loc), qkv_far0)
-        o_far0 = run(matmul(NN), attn_far0, w_out)
         h_far1 = pair_gather(hx1)
-        os_far0 = pair_scatter(o_far0)
-        o_near0 = run(matmul(NN), attn_own0, w_out)
+        o_far0, o_near0 = run(lambda a: proj_wide([a, attn_own0], w_out, NN), attn_far0)
+        os_far0, os_near0 = pair_scatter(o_far0), pair_scatter(o_near0)
+        (qkv_far1,) = run(lambda h: proj_deep([h], w_flat, NN), h_far1)
         ox0 = swap(os_far0, 2)
-        os_near0 = pair_scatter(o_near0)
-        dattn_own1 = run(matmul(NT), dy_own1, w_out)
-        qkv_far1 = run(matmul(NN), h_far1, w_flat)
         attn_own1, attn_far1, lse1 = run(lambda far: attn_fwd(qkv_own1, far, cos_t, sin_t, kv_loc), qkv_far1)
         dy_far0 = pair_gather(dyx0)
-        o_far1 = run(matmul(NN), attn_far1, w_out)
-        os_far1 = pair_scatter(o_far1)
-        dattn_far0 = run(matmul(NT), dy_far0, w_out)
+        o_far1, o_near1 = run(lambda a: proj_wide([a, attn_own1], w_out, NN), attn_far1)
+        os_far1, os_near1 = pair_scatter(o_far1), pair_scatter(o_near1)
+        (dattn_far0,) = run(lambda d: proj_deep([d], w_out, NT), dy_far0)
         ox1 = swap(os_far1, 2)
         dq_own0, dq_far0 = run(lambda d: attn_bwd(qkv_own0, qkv_far0, attn_own0, attn_far0, dattn_own0, d, lse0, cos_t, sin_t, kv_loc), dattn_far0)
         dy_far1 = pair_gather(dyx1)
-        dh_far0 = run(matmul(NT), dq_far0, w_flat)
-        dhs_far0 = pair_scatter(dh_far0)
-        o_near1 = run(matmul(NN), attn_own1, w_out)
+        dh_far0, dh_near0 = run(lambda d: proj_wide([d, dq_own0], w_flat, NT), dq_far0)
+        dhs_far0, dhs_near0 = pair_scatter(dh_far0), pair_scatter(dh_near0)
+        (dattn_far1,) = run(lambda d: proj_deep([d], w_out, NT), dy_far1)
         dhx0 = swap(dhs_far0, 2)
-        os_near1 = pair_scatter(o_near1)
-        dattn_far1 = run(matmul(NT), dy_far1, w_out)
         dq_own1, dq_far1 = run(lambda d: attn_bwd(qkv_own1, qkv_far1, attn_own1, attn_far1, dattn_own1, d, lse1, cos_t, sin_t, kv_loc), dattn_far1)
-        dh_far1 = run(matmul(NT), dq_far1, w_flat)
-        dhs_far1 = pair_scatter(dh_far1)
-        dh_near0 = run(matmul(NT), dq_own0, w_flat)
-        dhx1 = swap(dhs_far1, 2)
-        dhs_near0 = pair_scatter(dh_near0)
-        dh_near1 = run(matmul(NT), dq_own1, w_flat)
-        dhs_near1 = pair_scatter(dh_near1)
-        wout_grad = run(lambda a: dw_out([a, attn_far0, attn_own1, attn_far1], [dy_own0, dy_far0, dy_own1, dy_far1]), attn_own0)
+        dh_far1, dh_near1 = run(lambda d: proj_wide([d, dq_own1], w_flat, NT), dq_far1)
+        dhs_far1, dhs_near1 = pair_scatter(dh_far1), pair_scatter(dh_near1)
+        wout_grad = run(lambda a: dw_out([a, attn_far0, attn_own1, attn_far1], [(0, dy_own), (0, dy_far0), (1, dy_own), (0, dy_far1)]), attn_own0)
+        cut = dhs_far1.shape[0] // 2
+        dhx1a, dhx1b = swap(dhs_far1[:cut], 2), swap(dhs_far1[cut:], 2)
         y_out = run(lambda near: residual(x_seq, near, ox0, 0, None), os_near0)
         y_out = run(lambda near: residual(x_seq, near, ox1, 1, y_out), os_near1)
         wqkv_grad = run(lambda h: dw_qkv([h, h_far0, h_own1, h_far1], [dq_own0, dq_far0, dq_own1, dq_far1], kv_loc), h_own0)
-        x_grad, gain0 = run(lambda near: norm_bwd(x_seq, y_grad, gain, near, dhx0, 0, None), dhs_near0)
-        x_grad, gain1 = run(lambda near: norm_bwd(x_seq, y_grad, gain, near, dhx1, 1, x_grad), dhs_near1)
-        gain_part = gain0 + gain1
-        gain_part = gain_part + swap(gain_part, 1)
-        gain_grad = (gain_part + swap(gain_part, 2)).astype(jnp.bfloat16)[0]
+        x_grad, gain0 = run(lambda near: norm_bwd(x_seq, y_grad, gain, near, dhx0, 0, 0, None), dhs_near0)
+        x_grad, gain1 = run(lambda near: norm_bwd(x_seq, y_grad, gain, near, dhx1a, 1, 0, x_grad), dhs_near1)
+        x_grad, gain2 = run(lambda near: norm_bwd(x_seq, y_grad, gain, near, dhx1b, 1, cut, x_grad), dhs_near1)
+        mine = gain0 + gain1 + gain2
+        gain_grad = (mine + swap(mine, 1) + swap(mine, 2) + swap(mine, 3)).astype(jnp.bfloat16)[0]
         return y_out, x_grad, gain_grad, wqkv_grad, wout_grad
 
     specs_in = (P('dp', 'tp', None), P(None), P(None, 'tp', None), P('tp', None), P('dp', 'tp', None))

time: 1040 us -> 983 us (0.945)
  matrix products: 295 us -> 0 us
  Pallas kernels: 291 us -> 517 us
    dot_general x16 -> x0, matrix products: 295 us -> none  [dot(): return lax.dot_general(a, b, dims, preferred_element_type=jnp.float32)]
    pallas_call x2 -> x13, Pallas kernels: 23.4 us -> 268 us  [the longest x6 129 us: proj_deep(): pl.pallas_call(functools.partial(proj_deep_kernel, len(parts), dims), gri...]
    pallas_call x2, Pallas kernels: 63.3 us -> 42.7 us  [attn_fwd(): pl.pallas_call(functools.partial(attn_fwd_kernel, groups), grid=(kv_loc,)...]
    ppermute x10 -> x12, waiting for transfers between devices: 369 us -> 376 us  [swap(): return lax.ppermute(value, 'tp', [(i, i ^ bit) for i in range(n_tp)])]
    unnamed x27 -> x25, local copies, waits for them, and re-layouts: 35.4 us -> 36.8 us
  transfers between devices with their start and end apart: 26 -> 27, of which waited for: 9 -> 9; matrix products, arithmetic and copies ran while one was open for 32% -> 4% of each run, Pallas kernels for 27% -> 52%
where the time goes in v1:
time: 983 us; the launch traced here: 977 us
  Pallas kernels  517 us (53%)
  waiting for transfers between devices  380 us (39%)
  local copies, waits for them, and re-layouts  48.1 us (5%)
  starting transfers between devices  14.6 us (1%)
  between operations  14.3 us (1%)
    ppermute x12, waiting for transfers between devices, swap(): return lax.ppermute(value, 'tp', [(i, i ^ bit) for i in range(n_tp)])  376 us
    pallas_call x6, Pallas kernels, proj_deep(): pl.pallas_call(functools.partial(proj_deep_kernel, len(parts), dims), gri...  129 us
    pallas_call x4, Pallas kernels, proj_wide(): pl.pallas_call(functools.partial(proj_wide_kernel, len(parts), dims), gri...  113 us
    pallas_call x2, Pallas kernels, attn_bwd(): pl.pallas_call(functools.partial(attn_bwd_kernel, groups), grid=(kv_loc,)...  70 us
    pallas_call x1, Pallas kernels, dw_qkv(): pl.pallas_call(functools.partial(dw_qkv_kernel, len(acts)), grid=(d_model...  63.9 us
    pallas_call x1, Pallas kernels, dw_out(): pl.pallas_call(functools.partial(dw_out_kernel, len(acts)), grid=(d_model...  48.8 us
    pallas_call x2, Pallas kernels, attn_fwd(): pl.pallas_call(functools.partial(attn_fwd_kernel, groups), grid=(kv_loc,)...  42.7 us
    unnamed x25, local copies, waits for them, and re-layouts  36.8 us
  transfers between devices with their start and end apart: 27, of which 9 were waited for; matrix products, arithmetic and copies ran while one was open for 4% of the time, Pallas kernels for 52%

profile of v1, /device:TPU:0, one launch (start us, length us, event | category | flops | bytes accessed | tf_op | source)
XLA Modules:
  0.0 977.5 jit_solution(640301142854089183)
XLA Ops:
  25.5 68.2 %collective-permute-done.1 = bf16[256,6144]{1,0:T(8,128)(2,1)} collective-permute-done((bf16[256,6144]{1,0:T(8,128)(2,1)S(1)}, bf16[256,6144]{1,0:T(8,128)(2,1)}, u32[]{:S(2)}, u32[]{:S(2)}) %collective-permute-start.1) | collective-permute-done | bytes 3145760 | tf_op jit(solution)/shard_map/ppermute | solution.py:431
  97.4 67.6 %collective-permute-done = bf16[256,6144]{1,0:T(8,128)(2,1)} collective-permute-done((bf16[256,6144]{1,0:T(8,128)(2,1)S(1)}, bf16[256,6144]{1,0:T(8,128)(2,1)}, u32[]{:S(2)}, u32[]{:S(2)}) %collective-permute-start) | collective-permute-done | bytes 3145760 | tf_op jit(solution)/shard_map/ppermute | solution.py:431
  171.6 66.9 %collective-permute-done.3 = bf16[256,6144]{1,0:T(8,128)(2,1)S(1)} collective-permute-done((bf16[256,6144]{1,0:T(8,128)(2,1)S(1)}, bf16[256,6144]{1,0:T(8,128)(2,1)S(1)}, u32[]{:S(2)}, u32[]{:S(2)}) %collective-permute-start.3) | collective-permute-done | bytes 3145760 | tf_op jit(solution)/shard_map/ppermute | solution.py:431
  241.5 25.4 %copy.13 = bf16[768,8,2,1024]{3,1,2,0:T(8,128)(2,1)} copy(bf16[768,8,2,1024]{3,2,1,0:T(2,128)(2,1)} %bitcast.6) | data formatting | bytes 50331648
  269.2 39.0 %collective-permute-done.2 = bf16[256,6144]{1,0:T(8,128)(2,1)} collective-permute-done((bf16[256,6144]{1,0:T(8,128)(2,1)}, bf16[256,6144]{1,0:T(8,128)(2,1)}, u32[]{:S(2)}, u32[]{:S(2)}) %collective-permute-start.2) | collective-permute-done | bytes 3145760 | tf_op jit(solution)/shard_map/ppermute | solution.py:431
  308.6 32.2 %proj_deep.6 = (bf16[512,2048]{1,0:T(8,128)(2,1)}, bf16[512,2048]{1,0:T(8,128)(2,1)}) custom-call(bf16[512,6144]{1,0:T(8,128)(2,1)} %all-gather.8.cloned.1.call-done.refs_0_, bf16[512,6144]{1,0:T(8,128)(2,1)} %all-gather.10.cloned.1.call-done.refs_1_.refs_2_, bf16[6144,2048]{1,0:T(8,128)(2,1)} %bitcast.7), custom_call_target="tpu_custom_call" | custom-call | flops 25769803776 | bytes 25165824 | tf_op jit(solution)/shard_map/proj_deep/pallas_call | solution.py:391
  340.8 25.6 %proj_deep.7 = (bf16[512,1536]{1,0:T(8,128)(2,1)}, bf16[512,1536]{1,0:T(8,128)(2,1)}) custom-call(bf16[2,512,6144]{2,1,0:T(8,128)(2,1)} %all-gather.16.cloned.1.call-done.refs_0_.refs_1_.refs_4_.refs_6_, bf16[2,512,6144]{2,1,0:T(8,128)(2,1)} %all-gather.16.cloned.1.call-done.refs_0_.refs_1_.refs_4_.refs_6_, bf16[1536,6144]{1,0:T(8,128)(2,1)} %refs_1_.3), custom_call_target="tpu_custom_call" | custom-call | flops 19327352832 | bytes 18874368 | tf_op jit(solution)/shard_map/proj_deep/pallas_call | solution.py:391
  366.4 18.5 %proj_deep.8.far_ref = bf16[512,2048]{1,0:T(8,128)(2,1)} custom-call(bf16[512,6144]{1,0:T(8,128)(2,1)} %all-gather.14.cloned.1.call-done.refs_0_.refs_1_, bf16[6144,2048]{1,0:T(8,128)(2,1)} %bitcast.8), custom_call_target="tpu_custom_call" | custom-call | flops 12884901888 | bytes 25165824 | tf_op jit(solution)/shard_map/proj_deep/pallas_call | solution.py:391
  384.9 21.3 %attn_fwd.2 = (bf16[512,1536]{1,0:T(8,128)(2,1)S(1)}, bf16[512,1536]{1,0:T(8,128)(2,1)S(1)}, f32[1024,1536]{1,0:T(8,128)}) custom-call(bf16[512,2048]{1,0:T(8,128)(2,1)} %get-tuple-element.60.own_ref, bf16[512,2048]{1,0:T(8,128)(2,1)} %proj_deep.8.far_ref, f32[1024,128]{1,0:T(8,128)S(1)} %get-tuple-element.114.cos_ref, ...), custom_call_target="tpu_custom_call" | custom-call | flops 12000000000 | bytes 14000000 | tf_op jit(solution)/shard_map/attn_fwd/pallas_call | solution.py:189
  408.5 24.5 %proj_wide.4 = (bf16[512,6144]{1,0:T(8,128)(2,1)}, bf16[512,6144]{1,0:T(8,128)(2,1)}) custom-call(bf16[512,1536]{1,0:T(8,128)(2,1)} %copy-done.3, bf16[512,1536]{1,0:T(8,128)(2,1)} %copy-done.2, bf16[1536,6144]{1,0:T(8,128)(2,1)} %refs_1_.3), custom_call_target="tpu_custom_call" | custom-call | flops 19327352832 | bytes 18874368 | tf_op jit(solution)/shard_map/proj_wide/pallas_call | solution.py:414
  433.1 19.8 %proj_deep.9.far_ref = bf16[512,2048]{1,0:T(8,128)(2,1)} custom-call(bf16[512,6144]{1,0:T(8,128)(2,1)} %all-gather.12.cloned.1.call-done.refs_0_.refs_3_, bf16[6144,2048]{1,0:T(8,128)(2,1)} %bitcast.9), custom_call_target="tpu_custom_call" | custom-call | flops 12884901888 | bytes 25165824 | tf_op jit(solution)/shard_map/proj_deep/pallas_call | solution.py:391
  452.9 21.3 %attn_fwd.3 = (bf16[512,1536]{1,0:T(8,128)(2,1)S(1)}, bf16[512,1536]{1,0:T(8,128)(2,1)S(1)}, f32[1024,1536]{1,0:T(8,128)}) custom-call(bf16[512,2048]{1,0:T(8,128)(2,1)} %get-tuple-element.59.own_ref, bf16[512,2048]{1,0:T(8,128)(2,1)} %proj_deep.9.far_ref, f32[1024,128]{1,0:T(8,128)S(1)} %get-tuple-element.114.cos_ref, ...), custom_call_target="tpu_custom_call" | custom-call | flops 12000000000 | bytes 14000000 | tf_op jit(solution)/shard_map/attn_fwd/pallas_call | solution.py:189
  476.6 24.6 %proj_wide.5 = (bf16[512,6144]{1,0:T(8,128)(2,1)}, bf16[512,6144]{1,0:T(8,128)(2,1)}) custom-call(bf16[512,1536]{1,0:T(8,128)(2,1)} %copy-done.5, bf16[512,1536]{1,0:T(8,128)(2,1)} %copy-done.4, bf16[1536,6144]{1,0:T(8,128)(2,1)} %refs_1_.3), custom_call_target="tpu_custom_call" | custom-call | flops 19327352832 | bytes 18874368 | tf_op jit(solution)/shard_map/proj_wide/pallas_call | solution.py:414
  501.9 17.0 %proj_deep.10.dfar_ref = bf16[512,1536]{1,0:T(8,128)(2,1)} custom-call(bf16[512,6144]{1,0:T(8,128)(2,1)} %all-gather.20.cloned.1.call-done.refs_0_.refs_5_, bf16[1536,6144]{1,0:T(8,128)(2,1)} %refs_1_.3), custom_call_target="tpu_custom_call" | custom-call | flops 9663676416 | bytes 18874368 | tf_op jit(solution)/shard_map/proj_deep/pallas_call | solution.py:391
  518.9 35.9 %attn_bwd.2 = (bf16[512,2048]{1,0:T(8,128)(2,1)}, bf16[512,2048]{1,0:T(8,128)(2,1)}) custom-call(bf16[512,2048]{1,0:T(8,128)(2,1)} %get-tuple-element.60.own_ref, bf16[512,2048]{1,0:T(8,128)(2,1)} %proj_deep.8.far_ref, bf16[512,1536]{1,0:T(8,128)(2,1)} %copy-done.2, bf16[512,1536]{1,0:T(8,128)(2,1)} %copy-done.3, ...), custom_call_target="tpu_custom_call" | custom-call | flops 24999999488 | bytes 22000000 | tf_op jit(solution)/shard_map/attn_bwd/pallas_call | solution.py:208
  554.8 31.8 %proj_wide.6 = (bf16[512,6144]{1,0:T(8,128)(2,1)}, bf16[512,6144]{1,0:T(8,128)(2,1)}) custom-call(bf16[512,2048]{1,0:T(8,128)(2,1)} %get-tuple-element.84.refs_0_.refs_5_, bf16[512,2048]{1,0:T(8,128)(2,1)} %get-tuple-element.83.refs_1_.refs_4_, bf16[6144,2048]{1,0:T(8,128)(2,1)} %bitcast.10), custom_call_target="tpu_custom_call" | custom-call | flops 25769803776 | bytes 25165824 | tf_op jit(solution)/shard_map/proj_wide/pallas_call | solution.py:414
  586.6 15.5 %proj_deep.11.dfar_ref = bf16[512,1536]{1,0:T(8,128)(2,1)} custom-call(bf16[512,6144]{1,0:T(8,128)(2,1)} %all-gather.18.cloned.1.call-done.refs_0_.refs_7_, bf16[1536,6144]{1,0:T(8,128)(2,1)} %refs_1_.3), custom_call_target="tpu_custom_call" | custom-call | flops 9663676416 | bytes 18874368 | tf_op jit(solution)/shard_map/proj_deep/pallas_call | solution.py:391
  602.1 34.1 %attn_bwd.3 = (bf16[512,2048]{1,0:T(8,128)(2,1)}, bf16[512,2048]{1,0:T(8,128)(2,1)}) custom-call(bf16[512,2048]{1,0:T(8,128)(2,1)} %get-tuple-element.59.own_ref, bf16[512,2048]{1,0:T(8,128)(2,1)} %proj_deep.9.far_ref, bf16[512,1536]{1,0:T(8,128)(2,1)} %copy-done.4, bf16[512,1536]{1,0:T(8,128)(2,1)} %copy-done.5, ...), custom_call_target="tpu_custom_call" | custom-call | flops 24999999488 | bytes 22000000 | tf_op jit(solution)/shard_map/attn_bwd/pallas_call | solution.py:208
  636.2 31.8 %proj_wide.7 = (bf16[512,6144]{1,0:T(8,128)(2,1)}, bf16[512,6144]{1,0:T(8,128)(2,1)}) custom-call(bf16[512,2048]{1,0:T(8,128)(2,1)} %get-tuple-element.90.refs_0_.refs_7_, bf16[512,2048]{1,0:T(8,128)(2,1)} %get-tuple-element.89.refs_1_.refs_6_, bf16[6144,2048]{1,0:T(8,128)(2,1)} %bitcast.11), custom_call_target="tpu_custom_call" | custom-call | flops 25769803776 | bytes 25165824 | tf_op jit(solution)/shard_map/proj_wide/pallas_call | solution.py:414
  672.6 48.8 %dw_out.1 = bf16[1536,6144]{1,0:T(8,128)(2,1)} custom-call(bf16[512,1536]{1,0:T(8,128)(2,1)} %copy-done.2, bf16[512,1536]{1,0:T(8,128)(2,1)} %copy-done.3, bf16[512,1536]{1,0:T(8,128)(2,1)} %copy-done.4, bf16[512,1536]{1,0:T(8,128)(2,1)} %copy-done.5, bf16[2,512,6144]{2,1,0:T(8,128)(2,1)} %all-gather.16.cloned.1.call-done.refs_0_.refs_1_.refs_4_.refs_6_, ...), custom_call_target="tpu_custom_call" | custom-call | flops 38999998464 | bytes 50000000 | tf_op jit(solution)/shard_map/dw_out/pallas_call | solution.py:257
  728.3 13.5 %collective-permute-done.4.far_ref = bf16[256,6144]{1,0:T(8,128)(2,1)} collective-permute-done((bf16[256,6144]{1,0:T(8,128)(2,1)}, bf16[256,6144]{1,0:T(8,128)(2,1)}, u32[]{:S(2)}, u32[]{:S(2)}) %collective-permute-start.4) | collective-permute-done | bytes 3145760 | tf_op jit(solution)/shard_map/ppermute | solution.py:431
  748.0 61.1 %collective-permute-done.5.far_ref = bf16[256,6144]{1,0:T(8,128)(2,1)S(1)} collective-permute-done((bf16[256,6144]{1,0:T(8,128)(2,1)}, bf16[256,6144]{1,0:T(8,128)(2,1)S(1)}, u32[]{:S(2)}, u32[]{:S(2)}) %collective-permute-start.5) | collective-permute-done | bytes 3145760 | tf_op jit(solution)/shard_map/ppermute | solution.py:431
  817.0 63.9 %dw_qkv.1 = bf16[6144,2,1024]{2,1,0:T(2,128)(2,1)} custom-call(bf16[512,6144]{1,0:T(8,128)(2,1)} %all-gather.8.cloned.1.call-done.refs_0_, bf16[512,6144]{1,0:T(8,128)(2,1)} %all-gather.14.cloned.1.call-done.refs_0_.refs_1_, bf16[512,6144]{1,0:T(8,128)(2,1)} %all-gather.10.cloned.1.call-done.refs_1_.refs_2_, ...), custom_call_target="tpu_custom_call" | custom-call | flops 51000000512 | bytes 60000000 | tf_op jit(solution)/shard_map/dw_qkv/pallas_call | solution.py:236
  880.8 58.0 %collective-permute-done.6.far_ref = bf16[256,6144]{1,0:T(8,128)(2,1)} collective-permute-done((bf16[256,6144]{1,0:T(8,128)(2,1)}, bf16[256,6144]{1,0:T(8,128)(2,1)}, u32[]{:S(2)}, u32[]{:S(2)}) %collective-permute-start.6) | collective-permute-done | bytes 3145760 | tf_op jit(solution)/shard_map/ppermute | solution.py:431
  (101 shorter events, 97.0 us)
Async XLA Ops:
  7.2 301.4 %all-gather.8.cloned.1.call-start = ((), (), s32[]{:S(2)}) async-start(), calls=%async_computation.8 | async-start | bytes 9437184 | tf_op jit(solution)/shard_map/all_gather | solution.py:434
  14.1 294.4 %all-gather.10.cloned.1.call-start = ((), (), s32[]{:S(2)}) async-start(), calls=%async_computation.9 | async-start | bytes 9437184 | tf_op jit(solution)/shard_map/all_gather | solution.py:434
  19.8 320.9 %all-gather.16.cloned.1.call-start = ((), (), s32[]{:S(2)}) async-start(), calls=%async_computation.12 | async-start | bytes 18874368 | tf_op jit(solution)/shard_map/all_gather | solution.py:434
  20.6 345.8 %all-gather.14.cloned.1.call-start = ((), (), s32[]{:S(2)}) async-start(), calls=%async_computation.11 | async-start | bytes 9437184 | tf_op jit(solution)/shard_map/all_gather | solution.py:434
  22.2 71.5 %collective-permute-start.1 = (bf16[256,6144]{1,0:T(8,128)(2,1)S(1)}, bf16[256,6144]{1,0:T(8,128)(2,1)}, u32[]{:S(2)}, u32[]{:S(2)}) collective-permute-start(bf16[256,6144]{1,0:T(8,128)(2,1)S(1)} %copy-done.6), channel_id=1, source_target_pairs={{0,2},{1,3},{2,0},{3,1},{4,6},{5,7},{6,4},{7,5}} | collective-permute-start | bytes 9437192 | tf_op jit(solution)/shard_map/ppermute | solution.py:431
  93.8 339.4 %all-gather.12.cloned.1.call-start = ((), (), s32[]{:S(2)}) async-start(), calls=%async_computation.10 | async-start | bytes 9437184 | tf_op jit(solution)/shard_map/all_gather | solution.py:434
  95.6 69.4 %collective-permute-start = (bf16[256,6144]{1,0:T(8,128)(2,1)S(1)}, bf16[256,6144]{1,0:T(8,128)(2,1)}, u32[]{:S(2)}, u32[]{:S(2)}) collective-permute-start(bf16[256,6144]{1,0:T(8,128)(2,1)S(1)} %copy-done.7), channel_id=1, source_target_pairs={{0,2},{1,3},{2,0},{3,1},{4,6},{5,7},{6,4},{7,5}} | collective-permute-start | bytes 9437192 | tf_op jit(solution)/shard_map/ppermute | solution.py:431
  165.0 336.9 %all-gather.20.cloned.1.call-start = ((), (), s32[]{:S(2)}) async-start(), calls=%async_computation.16 | async-start | bytes 9437184 | tf_op jit(solution)/shard_map/all_gather | solution.py:434
  170.1 68.4 %collective-permute-start.3 = (bf16[256,6144]{1,0:T(8,128)(2,1)S(1)}, bf16[256,6144]{1,0:T(8,128)(2,1)S(1)}, u32[]{:S(2)}, u32[]{:S(2)}) collective-permute-start(bf16[256,6144]{1,0:T(8,128)(2,1)S(1)} %get-tuple-element.78), channel_id=1, source_target_pairs={{0,2},{1,3},{2,0},{3,1},{4,6},{5,7},{6,4},{7,5}} | collective-permute-start | bytes 9437192 | tf_op jit(solution)/shard_map/ppermute | solution.py:431
  240.2 346.4 %all-gather.18.cloned.1.call-start = ((), (), s32[]{:S(2)}) async-start(), calls=%async_computation.15 | async-start | bytes 9437184 | tf_op jit(solution)/shard_map/all_gather | solution.py:434
  240.3 67.9 %collective-permute-start.2 = (bf16[256,6144]{1,0:T(8,128)(2,1)}, bf16[256,6144]{1,0:T(8,128)(2,1)}, u32[]{:S(2)}, u32[]{:S(2)}) collective-permute-start(bf16[256,6144]{1,0:T(8,128)(2,1)} %get-tuple-element.77), channel_id=1, source_target_pairs={{0,2},{1,3},{2,0},{3,1},{4,6},{5,7},{6,4},{7,5}} | collective-permute-start | bytes 9437192 | tf_op jit(solution)/shard_map/ppermute | solution.py:431
  308.2 362.3 %reduce-scatter.13.cloned.1.call-start = ((), (), s32[]{:S(2)}) async-start(), calls=%async_computation.17 | async-start | bytes 9437184 | tf_op jit(solution)/shard_map/reduce_scatter | solution.py:437
  433.0 237.9 %reduce-scatter.15.cloned.1.call-start = ((), (), s32[]{:S(2)}) async-start(), calls=%async_computation.18 | async-start | bytes 9437184 | tf_op jit(solution)/shard_map/reduce_scatter | solution.py:437
  501.2 220.1 %reduce-scatter.11.cloned.1.call-start = ((), (), s32[]{:S(2)}) async-start(), calls=%async_computation.14 | async-start | bytes 9437184 | tf_op jit(solution)/shard_map/reduce_scatter | solution.py:437
  501.8 219.6 %reduce-scatter.23.cloned.1.call-start = ((), (), s32[]{:S(2)}) async-start(), calls=%async_computation.22 | async-start | bytes 9437184 | tf_op jit(solution)/shard_map/reduce_scatter | solution.py:437
  668.0 60.3 %reduce-scatter.21.cloned.1.call-start = ((), (), s32[]{:S(2)}) async-start(), calls=%async_computation.21 | async-start | bytes 9437184 | tf_op jit(solution)/shard_map/reduce_scatter | solution.py:437
  668.6 79.4 %reduce-scatter.9.cloned.1.call-start = ((), (), s32[]{:S(2)}) async-start(), calls=%async_computation.13 | async-start | bytes 9437184 | tf_op jit(solution)/shard_map/reduce_scatter | solution.py:437
  669.3 211.5 %reduce-scatter.19.cloned.1.call-start = ((), (), s32[]{:S(2)}) async-start(), calls=%async_computation.20 | async-start | bytes 9437184 | tf_op jit(solution)/shard_map/reduce_scatter | solution.py:437
  669.9 280.8 %reduce-scatter.17.cloned.1.call-start = ((), (), s32[]{:S(2)}) async-start(), calls=%async_computation.19 | async-start | bytes 9437184 | tf_op jit(solution)/shard_map/reduce_scatter | solution.py:437
  670.5 71.3 %collective-permute-start.4 = (bf16[256,6144]{1,0:T(8,128)(2,1)}, bf16[256,6144]{1,0:T(8,128)(2,1)}, u32[]{:S(2)}, u32[]{:S(2)}) collective-permute-start(bf16[256,6144]{1,0:T(8,128)(2,1)} %reduce-scatter.13.cloned.1.call-done), channel_id=1, source_target_pairs={{0,2},{1,3},{2,0},{3,1},{4,6},{5,7},{6,4},{7,5}} | collective-permute-start | bytes 9437192 | tf_op jit(solution)/shard_map/ppermute | solution.py:431
  670.9 138.2 %collective-permute-start.5 = (bf16[256,6144]{1,0:T(8,128)(2,1)}, bf16[256,6144]{1,0:T(8,128)(2,1)S(1)}, u32[]{:S(2)}, u32[]{:S(2)}) collective-permute-start(bf16[256,6144]{1,0:T(8,128)(2,1)} %reduce-scatter.15.cloned.1.call-done), channel_id=1, source_target_pairs={{0,2},{1,3},{2,0},{3,1},{4,6},{5,7},{6,4},{7,5}} | collective-permute-start | bytes 9437192 | tf_op jit(solution)/shard_map/ppermute | solution.py:431
  726.3 231.6 %collective-permute-start.8 = (bf16[128,6144]{1,0:T(8,128)(2,1)}, bf16[128,6144]{1,0:T(8,128)(2,1)}, u32[]{:S(2)}, u32[]{:S(2)}) collective-permute-start(bf16[128,6144]{1,0:T(8,128)(2,1)} %get-tuple-element.109), channel_id=1, source_target_pairs={{0,2},{1,3},{2,0},{3,1},{4,6},{5,7},{6,4},{7,5}} | collective-permute-start | bytes 4718600 | tf_op jit(solution)/shard_map/ppermute | solution.py:431
  726.3 224.4 %collective-permute-start.7 = (bf16[128,6144]{1,0:T(8,128)(2,1)}, bf16[128,6144]{1,0:T(8,128)(2,1)}, u32[]{:S(2)}, u32[]{:S(2)}) collective-permute-start(bf16[128,6144]{1,0:T(8,128)(2,1)} %get-tuple-element.110), channel_id=1, source_target_pairs={{0,2},{1,3},{2,0},{3,1},{4,6},{5,7},{6,4},{7,5}} | collective-permute-start | bytes 4718600 | tf_op jit(solution)/shard_map/ppermute | solution.py:431
  728.3 210.5 %collective-permute-start.6 = (bf16[256,6144]{1,0:T(8,128)(2,1)}, bf16[256,6144]{1,0:T(8,128)(2,1)}, u32[]{:S(2)}, u32[]{:S(2)}) collective-permute-start(bf16[256,6144]{1,0:T(8,128)(2,1)} %reduce-scatter.21.cloned.1.call-done), channel_id=1, source_target_pairs={{0,2},{1,3},{2,0},{3,1},{4,6},{5,7},{6,4},{7,5}} | collective-permute-start | bytes 9437192 | tf_op jit(solution)/shard_map/ppermute | solution.py:431
  (15 other events, 405.2 us)
Sparse Core Ops, SparseCore 0:
  14.3 16.7 all-gather.7
  33.2 15.1 all-gather.9
  49.9 22.8 all-gather.15
  93.9 15.2 all-gather.13
  165.1 14.9 all-gather.11
  240.3 14.6 all-gather.19
  308.3 14.3 all-gather.17
  433.2 11.5 reduce-scatter.12
  501.3 11.6 reduce-scatter.14
  515.2 13.2 reduce-scatter.10
  668.1 11.1 reduce-scatter.22
  681.4 13.2 reduce-scatter.20
  697.0 13.2 reduce-scatter.8
  712.4 13.2 reduce-scatter.18
  727.9 13.2 reduce-scatter.16

commit v2 on v1

--- a/solution.py
+++ b/solution.py
@@ -51,13 +51,6 @@
     row = lax.broadcasted_iota(jnp.int32, (TILE_Q, TILE_Q), 0)
     col = lax.broadcasted_iota(jnp.int32, (TILE_Q, TILE_Q), 1)
     return row >= col
-
-
-def mask_scores(scores, width, mask):
-    tail = jnp.where(mask, scores[:, width - TILE_Q:], NEG_BIG)
-    if width == TILE_Q:
-        return tail
-    return jnp.concatenate([scores[:, :width - TILE_Q], tail], axis=1)
 
 
 def half_rows(own, size):
@@ -124,7 +117,7 @@
     ofar_ref[...] = out_ref[far, :]
 
 
-def attn_bwd_kernel(groups, own_ref, far_ref, aown_ref, afar_ref, down_ref, dfar_ref, lse_ref, cos_ref, sin_ref, gown_ref, gfar_ref, qkv_ref, attn_ref, dattn_ref, k_scr, v_scr, dk_scr, dv_scr):
+def attn_bwd_kernel(groups, own_ref, far_ref, aown_ref, afar_ref, down_ref, dfar_ref, lse_ref, cos_ref, sin_ref, gown_ref, gfar_ref, qkv_ref, attn_ref, dattn_ref, k_scr, v_scr, dk_scr, dv_scr, q_scr, p_scr, s_scr):
     half = own_ref.shape[0]
     own, far = half_rows(True, half), half_rows(False, half)
     for dst, near, away in ((qkv_ref, own_ref, far_ref), (attn_ref, aown_ref, afar_ref), (dattn_ref, down_ref, dfar_ref)):
@@ -143,24 +136,39 @@
 
     def head(g, carry):
         cols = pl.ds(pl.multiple_of(g * HEAD_DIM, HEAD_DIM), HEAD_DIM)
-        for qi in range(seq_len // TILE_Q):
+
+        def scored(qi):
+            rows = slice(qi * TILE_Q, (qi + 1) * TILE_Q)
+            query = rotate(clipped(qkv_ref[rows, cols]), cos_ref[rows, :], sin_ref[rows, :])
+            q_scr[qi % 2] = query
+            dout = dattn_ref[rows, cols]
+            delta = jnp.sum(dout.astype(jnp.float32) * attn_ref[rows, cols].astype(jnp.float32), axis=1, keepdims=True)
+            lse = jnp.concatenate([lse_ref[rows, cols]] * (TILE_Q // HEAD_DIM), axis=1)
+            for kj in range(qi + 1):
+                keys = slice(kj * TILE_Q, (kj + 1) * TILE_Q)
+                scores = dot(query, k_scr[keys, :], NT)
+                if kj == qi:
+                    scores = jnp.where(mask, scores, NEG_BIG)
+                prob = jnp.exp2(scores * coef - lse)
+                dprob = dot(dout, v_scr[keys, :], NT).astype(jnp.bfloat16).astype(jnp.float32)
+                p_scr[qi % 2, :, keys] = prob.astype(jnp.bfloat16)
+                s_scr[qi % 2, :, keys] = (prob * (dprob - delta)).astype(jnp.bfloat16)
+
+        def mixed(qi):
             rows = slice(qi * TILE_Q, (qi + 1) * TILE_Q)
             width = (qi + 1) * TILE_Q
-            raw = qkv_ref[rows, cols]
-            cos_t, sin_t = cos_ref[rows, :], sin_ref[rows, :]
-            query = rotate(clipped(raw), cos_t, sin_t)
-            dout = dattn_ref[rows, cols]
-            delta = jnp.sum(dout.astype(jnp.float32) * attn_ref[rows, cols].astype(jnp.float32), axis=1, keepdims=True)
-            scores = mask_scores(dot(query, k_scr[:width, :], NT), width, mask)
-            lse = jnp.concatenate([lse_ref[rows, cols]] * (width // HEAD_DIM), axis=1)
-            prob = jnp.exp2(scores * coef - lse)
-            dprob = dot(dout, v_scr[:width, :], NT).astype(jnp.bfloat16).astype(jnp.float32)
-            dscore = (prob * (dprob - delta)).astype(jnp.bfloat16)
-            prob = prob.astype(jnp.bfloat16)
-            dv_scr[:, :width] += dot(dout, prob, TN)
-            dk_scr[:, :width] += dot(query, dscore, TN)
+            dscore = s_scr[qi % 2, :, :width]
+            dv_scr[:, :width] += dot(dattn_ref[rows, cols], p_scr[qi % 2, :, :width], TN)
+            dk_scr[:, :width] += dot(q_scr[qi % 2], dscore, TN)
             dquery = dot(dscore, k_scr[:width, :], NN) * scale
-            qkv_ref[rows, cols] = pass_clip(unrotate(dquery, cos_t, sin_t), raw)
+            qkv_ref[rows, cols] = pass_clip(unrotate(dquery, cos_ref[rows, :], sin_ref[rows, :]), qkv_ref[rows, cols])
+
+        tiles = seq_len // TILE_Q
+        scored(0)
+        for qi in range(tiles):
+            if qi + 1 < tiles:
+                scored(qi + 1)
+            mixed(qi)
         return carry
 
     lax.fori_loop(0, groups, head, 0)
@@ -193,7 +201,7 @@
         out_specs=[part, part, lse],
         out_shape=[rows, rows, jax.ShapeDtypeStruct((2 * half, kv_loc * wide), jnp.float32)],
         scratch_shapes=[pltpu.VMEM((2 * half, slot), jnp.bfloat16), pltpu.VMEM((2 * half, wide), jnp.bfloat16), pltpu.VMEM((2 * half, HEAD_DIM), jnp.bfloat16), pltpu.VMEM((HEAD_DIM, 2 * half), jnp.bfloat16), pltpu.VMEM((2, 2 * half, TILE_Q), jnp.float32), pltpu.VMEM((2, 2 * half, TILE_Q), jnp.bfloat16)],
-        compiler_params=pltpu.CompilerParams(vmem_limit_bytes=48 * 2 ** 20),
+        compiler_params=pltpu.CompilerParams(vmem_limit_bytes=62 * 2 ** 20),
         cost_estimate=pl.CostEstimate(flops=12 * 10 ** 9, bytes_accessed=14 * 10 ** 6, transcendentals=0),
         name="attn_fwd",
     )(qkv_own, qkv_far, cos_t, sin_t)
@@ -211,8 +219,8 @@
         in_specs=[full, full, part, part, part, part, lse, table, table],
         out_specs=[full, full],
         out_shape=[jax.ShapeDtypeStruct(qkv_own.shape, jnp.bfloat16)] * 2,
-        scratch_shapes=[pltpu.VMEM((2 * half, slot), jnp.bfloat16)] + [pltpu.VMEM((2 * half, wide), jnp.bfloat16)] * 2 + [pltpu.VMEM((2 * half, HEAD_DIM), jnp.bfloat16)] * 2 + [pltpu.VMEM((HEAD_DIM, 2 * half), jnp.float32)] * 2,
-        compiler_params=pltpu.CompilerParams(vmem_limit_bytes=56 * 2 ** 20),
+        scratch_shapes=[pltpu.VMEM((2 * half, slot), jnp.bfloat16)] + [pltpu.VMEM((2 * half, wide), jnp.bfloat16)] * 2 + [pltpu.VMEM((2 * half, HEAD_DIM), jnp.bfloat16)] * 2 + [pltpu.VMEM((HEAD_DIM, 2 * half), jnp.float32)] * 2 + [pltpu.VMEM((2, TILE_Q, HEAD_DIM), jnp.bfloat16)] + [pltpu.VMEM((2, TILE_Q, 2 * half), jnp.bfloat16)] * 2,
+        compiler_params=pltpu.CompilerParams(vmem_limit_bytes=62 * 2 ** 20),
         cost_estimate=pl.CostEstimate(flops=25 * 10 ** 9, bytes_accessed=22 * 10 ** 6, transcendentals=0),
         name="attn_bwd",
     )(qkv_own, qkv_far, attn_own, attn_far, dattn_own, dattn_far, lse_t, cos_t, sin_t)
@@ -239,7 +247,7 @@
         in_specs=[part] * len(acts) + [whole] * len(grads),
         out_specs=pl.BlockSpec((tile, kv_loc, slot), lambda i: (i, 0, 0)),
         out_shape=jax.ShapeDtypeStruct((d_model, kv_loc, slot), jnp.bfloat16),
-        compiler_params=pltpu.CompilerParams(vmem_limit_bytes=60 * 2 ** 20),
+        compiler_params=pltpu.CompilerParams(vmem_limit_bytes=62 * 2 ** 20),
         cost_estimate=pl.CostEstimate(flops=51 * 10 ** 9, bytes_accessed=60 * 10 ** 6, transcendentals=0),
         name="dw_qkv",
     )(*acts, *grads)
@@ -260,21 +268,25 @@
         in_specs=[whole] * len(acts) + [part_spec(g, b, (rows, tile), lambda i: (0, i)) for b, g in grads],
         out_specs=pl.BlockSpec((width, tile), lambda i: (0, i)),
         out_shape=jax.ShapeDtypeStruct((width, d_model), jnp.bfloat16),
-        compiler_params=pltpu.CompilerParams(vmem_limit_bytes=60 * 2 ** 20),
+        compiler_params=pltpu.CompilerParams(vmem_limit_bytes=62 * 2 ** 20),
         cost_estimate=pl.CostEstimate(flops=39 * 10 ** 9, bytes_accessed=50 * 10 ** 6, transcendentals=0),
         name="dw_out",
     )(*acts, *[g for _, g in grads])
 
 
-def normalized(x_f32):
-    centered = x_f32 - jnp.mean(x_f32, axis=-1, keepdims=True)
-    rstd = lax.rsqrt(jnp.mean(centered * centered, axis=-1, keepdims=True) + LN_EPS)
-    return centered * rstd, rstd
-
-
-def norm_fwd_kernel(x_ref, gain_ref, h_ref):
-    hat, _ = normalized(x_ref[0].astype(jnp.float32))
-    h_ref[...] = (hat * gain_ref[...].astype(jnp.float32)).astype(jnp.bfloat16)
+def norm_fwd_kernel(x_ref, gain_ref, h_ref, stat_ref):
+    def group(i, carry):
+        rows = pl.ds(pl.multiple_of(i * 16, 16), 16)
+        x_f32 = x_ref[0, rows, :].astype(jnp.float32)
+        mean = jnp.mean(x_f32, axis=-1, keepdims=True)
+        centered = x_f32 - mean
+        rstd = lax.rsqrt(jnp.mean(centered * centered, axis=-1, keepdims=True) + LN_EPS)
+        h_ref[rows, :] = (centered * rstd * gain_ref[...].astype(jnp.float32)).astype(jnp.bfloat16)
+        stat_ref[rows, :HEAD_DIM] = jnp.broadcast_to(mean, (16, HEAD_DIM))
+        stat_ref[rows, HEAD_DIM:] = jnp.broadcast_to(rstd, (16, HEAD_DIM))
+        return carry
+
+    lax.fori_loop(0, x_ref.shape[1] // 16, group, 0, unroll=2)
 
 
 def norm_fwd(x_seq, gain, b, tile=64):
@@ -283,19 +295,21 @@
         norm_fwd_kernel,
         grid=(rows // tile,),
         in_specs=[pl.BlockSpec((1, tile, d_model), lambda i: (b, i, 0)), pl.BlockSpec((1, d_model), lambda i: (0, 0))],
-        out_specs=pl.BlockSpec((tile, d_model), lambda i: (i, 0)),
-        out_shape=jax.ShapeDtypeStruct((rows, d_model), jnp.bfloat16),
+        out_specs=[pl.BlockSpec((tile, d_model), lambda i: (i, 0)), pl.BlockSpec((tile, 2 * HEAD_DIM), lambda i: (i, 0))],
+        out_shape=[jax.ShapeDtypeStruct((rows, d_model), jnp.bfloat16), jax.ShapeDtypeStruct((rows, 2 * HEAD_DIM), jnp.float32)],
+        compiler_params=pltpu.CompilerParams(vmem_limit_bytes=62 * 2 ** 20),
         cost_estimate=pl.CostEstimate(flops=2 * 10 ** 9, bytes_accessed=7 * 10 ** 6, transcendentals=0),
         name="norm_fwd",
     )(x_seq, gain)
 
 
-def residual_kernel(x_ref, near_ref, far_ref, *rest):
-    total = near_ref[...].astype(jnp.float32) + far_ref[...].astype(jnp.float32)
-    rest[-1][0] = (x_ref[0].astype(jnp.float32) + total.astype(jnp.bfloat16).astype(jnp.float32)).astype(jnp.bfloat16)
-
-
-def norm_bwd_kernel(x_ref, dy_ref, gain_ref, near_ref, far_ref, *rest):
+def residual_kernel(x_ref, near0_ref, near1_ref, far0_ref, far1_ref, out_ref):
+    for b, (near, far) in enumerate(((near0_ref, far0_ref), (near1_ref, far1_ref))):
+        total = (near[...].astype(jnp.float32) + far[...].astype(jnp.float32)).astype(jnp.bfloat16)
+        out_ref[b] = (x_ref[b].astype(jnp.float32) + total.astype(jnp.float32)).astype(jnp.bfloat16)
+
+
+def norm_bwd_kernel(x_ref, dy_ref, gain_ref, near_ref, far_ref, stat_ref, *rest):
     dx_ref, dgain_ref, sum_ref = rest[-3:]
 
     @pl.when(pl.program_id(0) == 0)
@@ -304,7 +318,8 @@
 
     def group(i, carry):
         rows = pl.ds(pl.multiple_of(i * 16, 16), 16)
-        hat, rstd = normalized(x_ref[0, rows, :].astype(jnp.float32))
+        mean, rstd = stat_ref[rows, :1], stat_ref[rows, HEAD_DIM:HEAD_DIM + 1]
+        hat = (x_ref[0, rows, :].astype(jnp.float32) - mean) * rstd
         dh = (near_ref[rows, :].astype(jnp.float32) + far_ref[rows, :].astype(jnp.float32)).astype(jnp.bfloat16).astype(jnp.float32)
         prod = dh * hat
         sum_ref[...] += prod[:8] + prod[8:]
@@ -320,24 +335,23 @@
         dgain_ref[...] = jnp.sum(sum_ref[...], axis=0, keepdims=True)
 
 
-def residual(x_seq, near, far, b, held, tile=64):
-    _, rows, d_model = x_seq.shape
-    whole = pl.BlockSpec((1, tile, d_model), lambda i: (b, i, 0))
+def residual(x_seq, nears, fars, tile=64):
+    batch, rows, d_model = x_seq.shape
+    whole = pl.BlockSpec((batch, tile, d_model), lambda i: (0, i, 0))
     part = pl.BlockSpec((tile, d_model), lambda i: (i, 0))
-    keep = [] if held is None else [held]
     return pl.pallas_call(
         residual_kernel,
         grid=(rows // tile,),
-        in_specs=[whole, part, part] + [pl.BlockSpec(memory_space=pl.ANY)] * len(keep),
+        in_specs=[whole] + [part] * 4,
         out_specs=whole,
         out_shape=jax.ShapeDtypeStruct(x_seq.shape, jnp.bfloat16),
-        input_output_aliases={3: 0} if keep else {},
-        cost_estimate=pl.CostEstimate(flops=2 * 10 ** 9, bytes_accessed=13 * 10 ** 6, transcendentals=0),
+        compiler_params=pltpu.CompilerParams(vmem_limit_bytes=62 * 2 ** 20),
+        cost_estimate=pl.CostEstimate(flops=4 * 10 ** 9, bytes_accessed=26 * 10 ** 6, transcendentals=0),
         name="residual",
-    )(x_seq, near, far, *keep)
-
-
-def norm_bwd(x_seq, y_grad, gain, near, far, b, base, held, tile=64):
+    )(x_seq, *nears, *fars)
+
+
+def norm_bwd(x_seq, y_grad, gain, near, far, stat, b, base, held, tile=64):
     _, _, d_model = x_seq.shape
     first = base // tile
     whole = pl.BlockSpec((1, tile, d_model), lambda i: (b, first + i, 0))
@@ -348,14 +362,15 @@
     return pl.pallas_call(
         norm_bwd_kernel,
         grid=(far.shape[0] // tile,),
-        in_specs=[whole, whole, row, part, piece] + [pl.BlockSpec(memory_space=pl.ANY)] * len(keep),
+        in_specs=[whole, whole, row, part, piece, pl.BlockSpec((tile, 2 * HEAD_DIM), lambda i: (first + i, 0))] + [pl.BlockSpec(memory_space=pl.ANY)] * len(keep),
         out_specs=[whole, row],
         out_shape=[jax.ShapeDtypeStruct(x_seq.shape, jnp.bfloat16), jax.ShapeDtypeStruct((1, d_model), jnp.float32)],
-        input_output_aliases={5: 0} if keep else {},
+        input_output_aliases={6: 0} if keep else {},
         scratch_shapes=[pltpu.VMEM((8, d_model), jnp.float32)],
+        compiler_params=pltpu.CompilerParams(vmem_limit_bytes=62 * 2 ** 20),
         cost_estimate=pl.CostEstimate(flops=4 * 10 ** 9, bytes_accessed=16 * 10 ** 6, transcendentals=0),
         name="norm_bwd",
-    )(x_seq, y_grad, gain, near, far, *keep)
+    )(x_seq, y_grad, gain, near, far, stat, *keep)
 
 
 def proj_deep_kernel(n_parts, dims, *refs):
@@ -395,7 +410,7 @@
         out_specs=[pl.BlockSpec((rows, width), lambda i: (0, 0))] * len(parts),
         out_shape=[jax.ShapeDtypeStruct((rows, width), jnp.bfloat16)] * len(parts),
         scratch_shapes=[pltpu.VMEM((rows, width), jnp.float32)] * len(parts),
-        compiler_params=pltpu.CompilerParams(vmem_limit_bytes=60 * 2 ** 20),
+        compiler_params=pltpu.CompilerParams(vmem_limit_bytes=62 * 2 ** 20),
         cost_estimate=pl.CostEstimate(flops=2 * len(parts) * rows * depth * width, bytes_accessed=2 * depth * width, transcendentals=0),
         name="proj_deep",
     )(*parts, w)
@@ -417,7 +432,7 @@
         in_specs=[pl.BlockSpec((rows, depth), lambda i: (0, 0))] * len(parts) + [w_spec],
         out_specs=[pl.BlockSpec((rows, tile), lambda i: (0, i))] * len(parts),
         out_shape=[jax.ShapeDtypeStruct((rows, width), jnp.bfloat16)] * len(parts),
-        compiler_params=pltpu.CompilerParams(vmem_limit_bytes=60 * 2 ** 20),
+        compiler_params=pltpu.CompilerParams(vmem_limit_bytes=62 * 2 ** 20),
         cost_estimate=pl.CostEstimate(flops=2 * len(parts) * rows * depth * width, bytes_accessed=2 * depth * width, transcendentals=0),
         name="proj_wide",
     )(*parts, w)
@@ -449,9 +464,9 @@
             return result
 
         cos_t, sin_t = rope_tables(x_seq.shape[1] * n_tp)
-        h0 = run(lambda x: norm_fwd(x, gain, 0), x_seq)
+        h0, stat0 = run(lambda x: norm_fwd(x, gain, 0), x_seq)
         hx0 = swap(h0, 2)
-        h1 = run(lambda x: norm_fwd(x, gain, 1), x_seq)
+        h1, stat1 = run(lambda x: norm_fwd(x, gain, 1), x_seq)
         hx1 = swap(h1, 2)
         dy0, dy1, _ = lax.optimization_barrier((y_grad[0], y_grad[1], h1))
         dyx0 = swap(dy0, 2)
@@ -487,12 +502,11 @@
         wout_grad = run(lambda a: dw_out([a, attn_far0, attn_own1, attn_far1], [(0, dy_own), (0, dy_far0), (1, dy_own), (0, dy_far1)]), attn_own0)
         cut = dhs_far1.shape[0] // 2
         dhx1a, dhx1b = swap(dhs_far1[:cut], 2), swap(dhs_far1[cut:], 2)
-        y_out = run(lambda near: residual(x_seq, near, ox0, 0, None), os_near0)
-        y_out = run(lambda near: residual(x_seq, near, ox1, 1, y_out), os_near1)
+        y_out = run(lambda near: residual(x_seq, [near, os_near1], [ox0, ox1]), os_near0)
         wqkv_grad = run(lambda h: dw_qkv([h, h_far0, h_own1, h_far1], [dq_own0, dq_far0, dq_own1, dq_far1], kv_loc), h_own0)
-        x_grad, gain0 = run(lambda near: norm_bwd(x_seq, y_grad, gain, near, dhx0, 0, 0, None), dhs_near0)
-        x_grad, gain1 = run(lambda near: norm_bwd(x_seq, y_grad, gain, near, dhx1a, 1, 0, x_grad), dhs_near1)
-        x_grad, gain2 = run(lambda near: norm_bwd(x_seq, y_grad, gain, near, dhx1b, 1, cut, x_grad), dhs_near1)
+        x_grad, gain0 = run(lambda near: norm_bwd(x_seq, y_grad, gain, near, dhx0, stat0, 0, 0, None), dhs_near0)
+        x_grad, gain1 = run(lambda near: norm_bwd(x_seq, y_grad, gain, near, dhx1a, stat1, 1, 0, x_grad), dhs_near1)
+        x_grad, gain2 = run(lambda near: norm_bwd(x_seq, y_grad, gain, near, dhx1b, stat1, 1, cut, x_grad), dhs_near1)
         mine = gain0 + gain1 + gain2
         gain_grad = (mine + swap(mine, 1) + swap(mine, 2) + swap(mine, 3)).astype(jnp.bfloat16)[0]
         return y_out, x_grad, gain_grad, wqkv_grad, wout_grad

time: 983 us -> 973 us (0.990)
  Pallas kernels: 517 us -> 506 us
    unnamed x25 -> x15, local copies, waits for them, and re-layouts: 36.8 us -> 33.3 us
  transfers between devices with their start and end apart: 27 -> 27, of which waited for: 9 -> 9; matrix products, arithmetic and copies ran while one was open for 4% -> 4% of each run, Pallas kernels for 52% -> 51%
where the time goes in v2:
time: 973 us; the launch traced here: 968 us
  Pallas kernels  506 us (52%)
  waiting for transfers between devices  383 us (39%)
  local copies, waits for them, and re-layouts  44.5 us (5%)
  starting transfers between devices  14.6 us (2%)
  between operations  14.3 us (1%)
    ppermute x12, waiting for transfers between devices, swap(): return lax.ppermute(value, 'tp', [(i, i ^ bit) for i in range(n_tp)])  380 us
    pallas_call x6, Pallas kernels, proj_deep(): pl.pallas_call(functools.partial(proj_deep_kernel, len(parts), dims), gri...  129 us
    pallas_call x4, Pallas kernels, proj_wide(): pl.pallas_call(functools.partial(proj_wide_kernel, len(parts), dims), gri...  113 us
    pallas_call x1, Pallas kernels, dw_qkv(): pl.pallas_call(functools.partial(dw_qkv_kernel, len(acts)), grid=(d_model...  63.9 us
    pallas_call x2, Pallas kernels, attn_bwd(): pl.pallas_call(functools.partial(attn_bwd_kernel, groups), grid=(kv_loc,)...  63.3 us
    pallas_call x1, Pallas kernels, dw_out(): pl.pallas_call(functools.partial(dw_out_kernel, len(acts)), grid=(d_model...  48.8 us
    pallas_call x2, Pallas kernels, attn_fwd(): pl.pallas_call(functools.partial(attn_fwd_kernel, groups), grid=(kv_loc,)...  43.6 us
    unnamed x15, local copies, waits for them, and re-layouts  33.3 us
  transfers between devices with their start and end apart: 27, of which 9 were waited for; matrix products, arithmetic and copies ran while one was open for 4% of the time, Pallas kernels for 51%

profile of v2, /device:TPU:0, one launch (start us, length us, event | category | flops | bytes accessed | tf_op | source)
XLA Modules:
  0.0 967.9 jit_solution(8312929884797985634)
XLA Ops:
  26.1 68.2 %collective-permute-done = bf16[256,6144]{1,0:T(8,128)(2,1)} collective-permute-done((bf16[256,6144]{1,0:T(8,128)(2,1)S(1)}, bf16[256,6144]{1,0:T(8,128)(2,1)}, u32[]{:S(2)}, u32[]{:S(2)}) %collective-permute-start) | collective-permute-done | bytes 3145760 | tf_op jit(solution)/shard_map/ppermute | solution.py:446
  97.9 67.6 %collective-permute-done.1 = bf16[256,6144]{1,0:T(8,128)(2,1)} collective-permute-done((bf16[256,6144]{1,0:T(8,128)(2,1)S(1)}, bf16[256,6144]{1,0:T(8,128)(2,1)}, u32[]{:S(2)}, u32[]{:S(2)}) %collective-permute-start.1) | collective-permute-done | bytes 3145760 | tf_op jit(solution)/shard_map/ppermute | solution.py:446
  172.1 66.9 %collective-permute-done.3 = bf16[256,6144]{1,0:T(8,128)(2,1)S(1)} collective-permute-done((bf16[256,6144]{1,0:T(8,128)(2,1)S(1)}, bf16[256,6144]{1,0:T(8,128)(2,1)S(1)}, u32[]{:S(2)}, u32[]{:S(2)}) %collective-permute-start.3) | collective-permute-done | bytes 3145760 | tf_op jit(solution)/shard_map/ppermute | solution.py:446
  242.0 25.3 %copy.12 = bf16[768,8,2,1024]{3,1,2,0:T(8,128)(2,1)} copy(bf16[768,8,2,1024]{3,2,1,0:T(2,128)(2,1)} %bitcast.6) | data formatting | bytes 50331648
  270.7 37.9 %collective-permute-done.2 = bf16[256,6144]{1,0:T(8,128)(2,1)S(1)} collective-permute-done((bf16[256,6144]{1,0:T(8,128)(2,1)}, bf16[256,6144]{1,0:T(8,128)(2,1)S(1)}, u32[]{:S(2)}, u32[]{:S(2)}) %collective-permute-start.2) | collective-permute-done | bytes 3145760 | tf_op jit(solution)/shard_map/ppermute | solution.py:446
  310.7 32.2 %proj_deep.6 = (bf16[512,2048]{1,0:T(8,128)(2,1)}, bf16[512,2048]{1,0:T(8,128)(2,1)}) custom-call(bf16[512,6144]{1,0:T(8,128)(2,1)} %all-gather.8.cloned.1.call-done.refs_0_, bf16[512,6144]{1,0:T(8,128)(2,1)} %all-gather.10.cloned.1.call-done.refs_1_.refs_2_, bf16[6144,2048]{1,0:T(8,128)(2,1)} %bitcast.7), custom_call_target="tpu_custom_call" | custom-call | flops 25769803776 | bytes 25165824 | tf_op jit(solution)/shard_map/proj_deep/pallas_call | solution.py:406
  342.9 25.6 %proj_deep.7 = (bf16[512,1536]{1,0:T(8,128)(2,1)}, bf16[512,1536]{1,0:T(8,128)(2,1)}) custom-call(bf16[2,512,6144]{2,1,0:T(8,128)(2,1)} %all-gather.14.cloned.1.call-done.refs_0_.refs_1_.refs_4_.refs_6_, bf16[2,512,6144]{2,1,0:T(8,128)(2,1)} %all-gather.14.cloned.1.call-done.refs_0_.refs_1_.refs_4_.refs_6_, bf16[1536,6144]{1,0:T(8,128)(2,1)} %refs_1_.3), custom_call_target="tpu_custom_call" | custom-call | flops 19327352832 | bytes 18874368 | tf_op jit(solution)/shard_map/proj_deep/pallas_call | solution.py:406
  368.5 18.5 %proj_deep.8.far_ref = bf16[512,2048]{1,0:T(8,128)(2,1)} custom-call(bf16[512,6144]{1,0:T(8,128)(2,1)} %all-gather.12.cloned.1.call-done.refs_0_.refs_1_, bf16[6144,2048]{1,0:T(8,128)(2,1)} %bitcast.8), custom_call_target="tpu_custom_call" | custom-call | flops 12884901888 | bytes 25165824 | tf_op jit(solution)/shard_map/proj_deep/pallas_call | solution.py:406
  387.0 21.8 %attn_fwd.2 = (bf16[512,1536]{1,0:T(8,128)(2,1)}, bf16[512,1536]{1,0:T(8,128)(2,1)}, f32[1024,1536]{1,0:T(8,128)}) custom-call(bf16[512,2048]{1,0:T(8,128)(2,1)} %get-tuple-element.64.own_ref, bf16[512,2048]{1,0:T(8,128)(2,1)} %proj_deep.8.far_ref, f32[1024,128]{1,0:T(8,128)} %get-tuple-element.120.cos_ref, f32[1024,128]{1,0:T(8,128)} %get-tuple-element.121.sin_ref), custom_call_target="tpu_custom_call" | custom-call | flops 12000000000 | bytes 14000000 | tf_op jit(solution)/shard_map/attn_fwd/pallas_call | solution.py:197
  408.8 24.5 %proj_wide.4 = (bf16[512,6144]{1,0:T(8,128)(2,1)}, bf16[512,6144]{1,0:T(8,128)(2,1)}) custom-call(bf16[512,1536]{1,0:T(8,128)(2,1)} %get-tuple-element.71.refs_0_.afar_ref.refs_1_, bf16[512,1536]{1,0:T(8,128)(2,1)} %get-tuple-element.96.refs_1_.aown_ref.refs_0_, bf16[1536,6144]{1,0:T(8,128)(2,1)} %refs_1_.3), custom_call_target="tpu_custom_call" | custom-call | flops 19327352832 | bytes 18874368 | tf_op jit(solution)/shard_map/proj_wide/pallas_call | solution.py:429
  433.4 19.8 %proj_deep.9.far_ref = bf16[512,2048]{1,0:T(8,128)(2,1)} custom-call(bf16[512,6144]{1,0:T(8,128)(2,1)} %all-gather.16.cloned.1.call-done.refs_0_.refs_3_, bf16[6144,2048]{1,0:T(8,128)(2,1)} %bitcast.9), custom_call_target="tpu_custom_call" | custom-call | flops 12884901888 | bytes 25165824 | tf_op jit(solution)/shard_map/proj_deep/pallas_call | solution.py:406
  453.2 21.8 %attn_fwd.3 = (bf16[512,1536]{1,0:T(8,128)(2,1)}, bf16[512,1536]{1,0:T(8,128)(2,1)}, f32[1024,1536]{1,0:T(8,128)}) custom-call(bf16[512,2048]{1,0:T(8,128)(2,1)} %get-tuple-element.73.own_ref, bf16[512,2048]{1,0:T(8,128)(2,1)} %proj_deep.9.far_ref, f32[1024,128]{1,0:T(8,128)} %get-tuple-element.120.cos_ref, f32[1024,128]{1,0:T(8,128)} %get-tuple-element.121.sin_ref), custom_call_target="tpu_custom_call" | custom-call | flops 12000000000 | bytes 14000000 | tf_op jit(solution)/shard_map/attn_fwd/pallas_call | solution.py:197
  475.0 24.5 %proj_wide.5 = (bf16[512,6144]{1,0:T(8,128)(2,1)}, bf16[512,6144]{1,0:T(8,128)(2,1)}) custom-call(bf16[512,1536]{1,0:T(8,128)(2,1)} %get-tuple-element.82.refs_0_.afar_ref.refs_3_, bf16[512,1536]{1,0:T(8,128)(2,1)} %get-tuple-element.77.refs_1_.aown_ref.refs_2_, bf16[1536,6144]{1,0:T(8,128)(2,1)} %refs_1_.3), custom_call_target="tpu_custom_call" | custom-call | flops 19327352832 | bytes 18874368 | tf_op jit(solution)/shard_map/proj_wide/pallas_call | solution.py:429
  500.2 17.1 %proj_deep.10.dfar_ref = bf16[512,1536]{1,0:T(8,128)(2,1)} custom-call(bf16[512,6144]{1,0:T(8,128)(2,1)} %all-gather.20.cloned.1.call-done.refs_0_.refs_5_, bf16[1536,6144]{1,0:T(8,128)(2,1)} %refs_1_.3), custom_call_target="tpu_custom_call" | custom-call | flops 9663676416 | bytes 18874368 | tf_op jit(solution)/shard_map/proj_deep/pallas_call | solution.py:406
  517.2 32.6 %attn_bwd.2 = (bf16[512,2048]{1,0:T(8,128)(2,1)}, bf16[512,2048]{1,0:T(8,128)(2,1)}) custom-call(bf16[512,2048]{1,0:T(8,128)(2,1)} %get-tuple-element.64.own_ref, bf16[512,2048]{1,0:T(8,128)(2,1)} %proj_deep.8.far_ref, bf16[512,1536]{1,0:T(8,128)(2,1)} %get-tuple-element.96.refs_1_.aown_ref.refs_0_, ...), custom_call_target="tpu_custom_call" | custom-call | flops 24999999488 | bytes 22000000 | tf_op jit(solution)/shard_map/attn_bwd/pallas_call | solution.py:216
  549.9 31.8 %proj_wide.6 = (bf16[512,6144]{1,0:T(8,128)(2,1)}, bf16[512,6144]{1,0:T(8,128)(2,1)}) custom-call(bf16[512,2048]{1,0:T(8,128)(2,1)} %get-tuple-element.88.refs_0_.refs_5_, bf16[512,2048]{1,0:T(8,128)(2,1)} %get-tuple-element.87.refs_1_.refs_4_, bf16[6144,2048]{1,0:T(8,128)(2,1)} %bitcast.10), custom_call_target="tpu_custom_call" | custom-call | flops 25769803776 | bytes 25165824 | tf_op jit(solution)/shard_map/proj_wide/pallas_call | solution.py:429
  581.7 15.5 %proj_deep.11.dfar_ref = bf16[512,1536]{1,0:T(8,128)(2,1)} custom-call(bf16[512,6144]{1,0:T(8,128)(2,1)} %all-gather.18.cloned.1.call-done.refs_0_.refs_7_, bf16[1536,6144]{1,0:T(8,128)(2,1)} %refs_1_.3), custom_call_target="tpu_custom_call" | custom-call | flops 9663676416 | bytes 18874368 | tf_op jit(solution)/shard_map/proj_deep/pallas_call | solution.py:406
  597.1 30.7 %attn_bwd.3 = (bf16[512,2048]{1,0:T(8,128)(2,1)}, bf16[512,2048]{1,0:T(8,128)(2,1)}) custom-call(bf16[512,2048]{1,0:T(8,128)(2,1)} %get-tuple-element.73.own_ref, bf16[512,2048]{1,0:T(8,128)(2,1)} %proj_deep.9.far_ref, bf16[512,1536]{1,0:T(8,128)(2,1)} %get-tuple-element.77.refs_1_.aown_ref.refs_2_, ...), custom_call_target="tpu_custom_call" | custom-call | flops 24999999488 | bytes 22000000 | tf_op jit(solution)/shard_map/attn_bwd/pallas_call | solution.py:216
  627.9 31.8 %proj_wide.7 = (bf16[512,6144]{1,0:T(8,128)(2,1)}, bf16[512,6144]{1,0:T(8,128)(2,1)}) custom-call(bf16[512,2048]{1,0:T(8,128)(2,1)} %get-tuple-element.94.refs_0_.refs_7_, bf16[512,2048]{1,0:T(8,128)(2,1)} %get-tuple-element.93.refs_1_.refs_6_, bf16[6144,2048]{1,0:T(8,128)(2,1)} %bitcast.11), custom_call_target="tpu_custom_call" | custom-call | flops 25769803776 | bytes 25165824 | tf_op jit(solution)/shard_map/proj_wide/pallas_call | solution.py:429
  664.2 48.8 %dw_out.1 = bf16[1536,6144]{1,0:T(8,128)(2,1)} custom-call(bf16[512,1536]{1,0:T(8,128)(2,1)} %get-tuple-element.96.refs_1_.aown_ref.refs_0_, bf16[512,1536]{1,0:T(8,128)(2,1)} %get-tuple-element.71.refs_0_.afar_ref.refs_1_, bf16[512,1536]{1,0:T(8,128)(2,1)} %get-tuple-element.77.refs_1_.aown_ref.refs_2_, ...), custom_call_target="tpu_custom_call" | custom-call | flops 38999998464 | bytes 50000000 | tf_op jit(solution)/shard_map/dw_out/pallas_call | solution.py:265
  719.9 13.6 %collective-permute-done.4.far0_ref = bf16[256,6144]{1,0:T(8,128)(2,1)} collective-permute-done((bf16[256,6144]{1,0:T(8,128)(2,1)}, bf16[256,6144]{1,0:T(8,128)(2,1)}, u32[]{:S(2)}, u32[]{:S(2)}) %collective-permute-start.4) | collective-permute-done | bytes 3145760 | tf_op jit(solution)/shard_map/ppermute | solution.py:446
  733.5 67.4 %collective-permute-done.5.far1_ref = bf16[256,6144]{1,0:T(8,128)(2,1)} collective-permute-done((bf16[256,6144]{1,0:T(8,128)(2,1)}, bf16[256,6144]{1,0:T(8,128)(2,1)}, u32[]{:S(2)}, u32[]{:S(2)}) %collective-permute-start.5) | collective-permute-done | bytes 3145760 | tf_op jit(solution)/shard_map/ppermute | solution.py:446
  810.7 63.9 %dw_qkv.1 = bf16[6144,2,1024]{2,1,0:T(2,128)(2,1)} custom-call(bf16[512,6144]{1,0:T(8,128)(2,1)} %all-gather.8.cloned.1.call-done.refs_0_, bf16[512,6144]{1,0:T(8,128)(2,1)} %all-gather.12.cloned.1.call-done.refs_0_.refs_1_, bf16[512,6144]{1,0:T(8,128)(2,1)} %all-gather.10.cloned.1.call-done.refs_1_.refs_2_, ...), custom_call_target="tpu_custom_call" | custom-call | flops 51000000512 | bytes 60000000 | tf_op jit(solution)/shard_map/dw_qkv/pallas_call | solution.py:244
  874.6 55.8 %collective-permute-done.6.far_ref = bf16[256,6144]{1,0:T(8,128)(2,1)} collective-permute-done((bf16[256,6144]{1,0:T(8,128)(2,1)}, bf16[256,6144]{1,0:T(8,128)(2,1)}, u32[]{:S(2)}, u32[]{:S(2)}) %collective-permute-start.6) | collective-permute-done | bytes 3145760 | tf_op jit(solution)/shard_map/ppermute | solution.py:446
  (90 shorter events, 90.0 us)
Async XLA Ops:
  7.2 303.5 %all-gather.8.cloned.1.call-start = ((), (), s32[]{:S(2)}) async-start(), calls=%async_computation.8 | async-start | bytes 9437184 | tf_op jit(solution)/shard_map/all_gather | solution.py:449
  14.4 296.3 %all-gather.10.cloned.1.call-start = ((), (), s32[]{:S(2)}) async-start(), calls=%async_computation.9 | async-start | bytes 9437184 | tf_op jit(solution)/shard_map/all_gather | solution.py:449
  20.3 322.6 %all-gather.14.cloned.1.call-start = ((), (), s32[]{:S(2)}) async-start(), calls=%async_computation.11 | async-start | bytes 18874368 | tf_op jit(solution)/shard_map/all_gather | solution.py:449
  21.1 347.4 %all-gather.12.cloned.1.call-start = ((), (), s32[]{:S(2)}) async-start(), calls=%async_computation.10 | async-start | bytes 9437184 | tf_op jit(solution)/shard_map/all_gather | solution.py:449
  22.7 71.6 %collective-permute-start = (bf16[256,6144]{1,0:T(8,128)(2,1)S(1)}, bf16[256,6144]{1,0:T(8,128)(2,1)}, u32[]{:S(2)}, u32[]{:S(2)}) collective-permute-start(bf16[256,6144]{1,0:T(8,128)(2,1)S(1)} %copy-done), channel_id=1, source_target_pairs={{0,2},{1,3},{2,0},{3,1},{4,6},{5,7},{6,4},{7,5}} | collective-permute-start | bytes 9437192 | tf_op jit(solution)/shard_map/ppermute | solution.py:446
  94.3 339.1 %all-gather.16.cloned.1.call-start = ((), (), s32[]{:S(2)}) async-start(), calls=%async_computation.13 | async-start | bytes 9437184 | tf_op jit(solution)/shard_map/all_gather | solution.py:449
  96.1 69.4 %collective-permute-start.1 = (bf16[256,6144]{1,0:T(8,128)(2,1)S(1)}, bf16[256,6144]{1,0:T(8,128)(2,1)}, u32[]{:S(2)}, u32[]{:S(2)}) collective-permute-start(bf16[256,6144]{1,0:T(8,128)(2,1)S(1)} %copy-done.3), channel_id=1, source_target_pairs={{0,2},{1,3},{2,0},{3,1},{4,6},{5,7},{6,4},{7,5}} | collective-permute-start | bytes 9437192 | tf_op jit(solution)/shard_map/ppermute | solution.py:446
  165.5 334.7 %all-gather.20.cloned.1.call-start = ((), (), s32[]{:S(2)}) async-start(), calls=%async_computation.15 | async-start | bytes 9437184 | tf_op jit(solution)/shard_map/all_gather | solution.py:449
  170.6 68.4 %collective-permute-start.3 = (bf16[256,6144]{1,0:T(8,128)(2,1)S(1)}, bf16[256,6144]{1,0:T(8,128)(2,1)S(1)}, u32[]{:S(2)}, u32[]{:S(2)}) collective-permute-start(bf16[256,6144]{1,0:T(8,128)(2,1)S(1)} %get-tuple-element.81), channel_id=1, source_target_pairs={{0,2},{1,3},{2,0},{3,1},{4,6},{5,7},{6,4},{7,5}} | collective-permute-start | bytes 9437192 | tf_op jit(solution)/shard_map/ppermute | solution.py:446
  240.8 340.9 %all-gather.18.cloned.1.call-start = ((), (), s32[]{:S(2)}) async-start(), calls=%async_computation.14 | async-start | bytes 9437184 | tf_op jit(solution)/shard_map/all_gather | solution.py:449
  240.8 67.8 %collective-permute-start.2 = (bf16[256,6144]{1,0:T(8,128)(2,1)}, bf16[256,6144]{1,0:T(8,128)(2,1)S(1)}, u32[]{:S(2)}, u32[]{:S(2)}) collective-permute-start(bf16[256,6144]{1,0:T(8,128)(2,1)} %get-tuple-element.80), channel_id=1, source_target_pairs={{0,2},{1,3},{2,0},{3,1},{4,6},{5,7},{6,4},{7,5}} | collective-permute-start | bytes 9437192 | tf_op jit(solution)/shard_map/ppermute | solution.py:446
  310.3 351.9 %reduce-scatter.13.cloned.1.call-start = ((), (), s32[]{:S(2)}) async-start(), calls=%async_computation.17 | async-start | bytes 9437184 | tf_op jit(solution)/shard_map/reduce_scatter | solution.py:452
  433.3 229.3 %reduce-scatter.15.cloned.1.call-start = ((), (), s32[]{:S(2)}) async-start(), calls=%async_computation.18 | async-start | bytes 9437184 | tf_op jit(solution)/shard_map/reduce_scatter | solution.py:452
  499.5 213.5 %reduce-scatter.9.cloned.1.call-start = ((), (), s32[]{:S(2)}) async-start(), calls=%async_computation.12 | async-start | bytes 9437184 | tf_op jit(solution)/shard_map/reduce_scatter | solution.py:452
  500.1 212.9 %reduce-scatter.23.cloned.1.call-start = ((), (), s32[]{:S(2)}) async-start(), calls=%async_computation.22 | async-start | bytes 9437184 | tf_op jit(solution)/shard_map/reduce_scatter | solution.py:452
  659.7 60.2 %reduce-scatter.21.cloned.1.call-start = ((), (), s32[]{:S(2)}) async-start(), calls=%async_computation.21 | async-start | bytes 9437184 | tf_op jit(solution)/shard_map/reduce_scatter | solution.py:452
  660.2 59.6 %reduce-scatter.11.cloned.1.call-start = ((), (), s32[]{:S(2)}) async-start(), calls=%async_computation.16 | async-start | bytes 9437184 | tf_op jit(solution)/shard_map/reduce_scatter | solution.py:452
  661.0 213.6 %reduce-scatter.19.cloned.1.call-start = ((), (), s32[]{:S(2)}) async-start(), calls=%async_computation.20 | async-start | bytes 9437184 | tf_op jit(solution)/shard_map/reduce_scatter | solution.py:452
  661.6 279.6 %reduce-scatter.17.cloned.1.call-start = ((), (), s32[]{:S(2)}) async-start(), calls=%async_computation.19 | async-start | bytes 9437184 | tf_op jit(solution)/shard_map/reduce_scatter | solution.py:452
  662.2 71.3 %collective-permute-start.4 = (bf16[256,6144]{1,0:T(8,128)(2,1)}, bf16[256,6144]{1,0:T(8,128)(2,1)}, u32[]{:S(2)}, u32[]{:S(2)}) collective-permute-start(bf16[256,6144]{1,0:T(8,128)(2,1)} %reduce-scatter.13.cloned.1.call-done), channel_id=1, source_target_pairs={{0,2},{1,3},{2,0},{3,1},{4,6},{5,7},{6,4},{7,5}} | collective-permute-start | bytes 9437192 | tf_op jit(solution)/shard_map/ppermute | solution.py:446
  662.6 138.3 %collective-permute-start.5 = (bf16[256,6144]{1,0:T(8,128)(2,1)}, bf16[256,6144]{1,0:T(8,128)(2,1)}, u32[]{:S(2)}, u32[]{:S(2)}) collective-permute-start(bf16[256,6144]{1,0:T(8,128)(2,1)} %reduce-scatter.15.cloned.1.call-done), channel_id=1, source_target_pairs={{0,2},{1,3},{2,0},{3,1},{4,6},{5,7},{6,4},{7,5}} | collective-permute-start | bytes 9437192 | tf_op jit(solution)/shard_map/ppermute | solution.py:446
  717.8 230.1 %collective-permute-start.8 = (bf16[128,6144]{1,0:T(8,128)(2,1)}, bf16[128,6144]{1,0:T(8,128)(2,1)S(1)}, u32[]{:S(2)}, u32[]{:S(2)}) collective-permute-start(bf16[128,6144]{1,0:T(8,128)(2,1)} %get-tuple-element.115), channel_id=1, source_target_pairs={{0,2},{1,3},{2,0},{3,1},{4,6},{5,7},{6,4},{7,5}} | collective-permute-start | bytes 4718600 | tf_op jit(solution)/shard_map/ppermute | solution.py:446
  717.8 223.3 %collective-permute-start.7 = (bf16[128,6144]{1,0:T(8,128)(2,1)}, bf16[128,6144]{1,0:T(8,128)(2,1)}, u32[]{:S(2)}, u32[]{:S(2)}) collective-permute-start(bf16[128,6144]{1,0:T(8,128)(2,1)} %get-tuple-element.116), channel_id=1, source_target_pairs={{0,2},{1,3},{2,0},{3,1},{4,6},{5,7},{6,4},{7,5}} | collective-permute-start | bytes 4718600 | tf_op jit(solution)/shard_map/ppermute | solution.py:446
  719.8 210.6 %collective-permute-start.6 = (bf16[256,6144]{1,0:T(8,128)(2,1)}, bf16[256,6144]{1,0:T(8,128)(2,1)}, u32[]{:S(2)}, u32[]{:S(2)}) collective-permute-start(bf16[256,6144]{1,0:T(8,128)(2,1)} %reduce-scatter.21.cloned.1.call-done), channel_id=1, source_target_pairs={{0,2},{1,3},{2,0},{3,1},{4,6},{5,7},{6,4},{7,5}} | collective-permute-start | bytes 9437192 | tf_op jit(solution)/shard_map/ppermute | solution.py:446
  (10 other events, 35.1 us)
Sparse Core Ops, SparseCore 0:
  14.5 16.7 all-gather.7
  33.4 15.1 all-gather.9
  50.1 22.8 all-gather.13
  94.4 15.2 all-gather.11
  165.6 14.9 all-gather.15
  240.9 14.6 all-gather.19
  310.4 14.3 all-gather.17
  433.4 11.5 reduce-scatter.12
  499.6 11.6 reduce-scatter.14
  513.5 13.2 reduce-scatter.8
  659.8 11.0 reduce-scatter.22
  673.0 13.2 reduce-scatter.20
  688.6 13.2 reduce-scatter.10
  704.1 13.2 reduce-scatter.18
  719.5 13.2 reduce-scatter.16

commit v3 on v2

--- a/solution.py
+++ b/solution.py
@@ -18,13 +18,36 @@
 NN = (((1,), (0,)), ((), ()))
 
 
+GRANT = pltpu.CompilerParams(vmem_limit_bytes=62 * 2 ** 20)
+
+
+def cost(gigaflops, megabytes):
+    return pl.CostEstimate(flops=gigaflops * 10 ** 9, bytes_accessed=megabytes * 10 ** 6, transcendentals=0)
+
+
+def matmul_cost(rows, depth, width):
+    return pl.CostEstimate(flops=2 * rows * depth * width, bytes_accessed=2 * depth * width, transcendentals=0)
+
+
+def along_rows(rows, columns):
+    return pl.BlockSpec((rows, columns), lambda i: (i, 0))
+
+
+def along_columns(rows, columns):
+    return pl.BlockSpec((rows, columns), lambda i: (0, i))
+
+
+def held_whole(rows, columns):
+    return pl.BlockSpec((rows, columns), lambda i: (0, 0))
+
+
 def dot(a, b, dims):
     return lax.dot_general(a, b, dims, preferred_element_type=jnp.float32)
 
 
-def rope_tables(seq_len):
+def rope_tables(positions):
     inv_freq = 1.0 / (ROPE_THETA ** (jnp.arange(0, HEAD_DIM, 2, dtype=jnp.float32) / HEAD_DIM))
-    angles = jnp.arange(seq_len, dtype=jnp.float32)[:, None] * inv_freq[None, :]
+    angles = positions[:, None] * inv_freq[None, :]
     cos_t, sin_t = jnp.cos(angles), jnp.sin(angles)
     return jnp.concatenate([cos_t, cos_t], axis=-1), jnp.concatenate([-sin_t, sin_t], axis=-1)
 
@@ -180,10 +203,10 @@
 
 
 def head_specs(half, slot, wide):
-    table = pl.BlockSpec((2 * half, HEAD_DIM), lambda n: (0, 0))
-    part = pl.BlockSpec((half, wide), lambda n: (0, n))
-    full = pl.BlockSpec((half, slot), lambda n: (0, n))
-    lse = pl.BlockSpec((2 * half, wide), lambda n: (0, n))
+    table = held_whole(2 * half, HEAD_DIM)
+    part = along_columns(half, wide)
+    full = along_columns(half, slot)
+    lse = along_columns(2 * half, wide)
     return table, part, full, lse
 
 
@@ -201,8 +224,8 @@
         out_specs=[part, part, lse],
         out_shape=[rows, rows, jax.ShapeDtypeStruct((2 * half, kv_loc * wide), jnp.float32)],
         scratch_shapes=[pltpu.VMEM((2 * half, slot), jnp.bfloat16), pltpu.VMEM((2 * half, wide), jnp.bfloat16), pltpu.VMEM((2 * half, HEAD_DIM), jnp.bfloat16), pltpu.VMEM((HEAD_DIM, 2 * half), jnp.bfloat16), pltpu.VMEM((2, 2 * half, TILE_Q), jnp.float32), pltpu.VMEM((2, 2 * half, TILE_Q), jnp.bfloat16)],
-        compiler_params=pltpu.CompilerParams(vmem_limit_bytes=62 * 2 ** 20),
-        cost_estimate=pl.CostEstimate(flops=12 * 10 ** 9, bytes_accessed=14 * 10 ** 6, transcendentals=0),
+        compiler_params=GRANT,
+        cost_estimate=cost(12, 14),
         name="attn_fwd",
     )(qkv_own, qkv_far, cos_t, sin_t)
 
@@ -220,8 +243,8 @@
         out_specs=[full, full],
         out_shape=[jax.ShapeDtypeStruct(qkv_own.shape, jnp.bfloat16)] * 2,
         scratch_shapes=[pltpu.VMEM((2 * half, slot), jnp.bfloat16)] + [pltpu.VMEM((2 * half, wide), jnp.bfloat16)] * 2 + [pltpu.VMEM((2 * half, HEAD_DIM), jnp.bfloat16)] * 2 + [pltpu.VMEM((HEAD_DIM, 2 * half), jnp.float32)] * 2 + [pltpu.VMEM((2, TILE_Q, HEAD_DIM), jnp.bfloat16)] + [pltpu.VMEM((2, TILE_Q, 2 * half), jnp.bfloat16)] * 2,
-        compiler_params=pltpu.CompilerParams(vmem_limit_bytes=62 * 2 ** 20),
-        cost_estimate=pl.CostEstimate(flops=25 * 10 ** 9, bytes_accessed=22 * 10 ** 6, transcendentals=0),
+        compiler_params=GRANT,
+        cost_estimate=cost(25, 22),
         name="attn_bwd",
     )(qkv_own, qkv_far, attn_own, attn_far, dattn_own, dattn_far, lse_t, cos_t, sin_t)
 
@@ -239,16 +262,16 @@
     rows, d_model = acts[0].shape
     width = grads[0].shape[1]
     slot = width // kv_loc
-    whole = pl.BlockSpec((rows, width), lambda i: (0, 0))
-    part = pl.BlockSpec((rows, tile), lambda i: (0, i))
+    whole = held_whole(rows, width)
+    part = along_columns(rows, tile)
     return pl.pallas_call(
         functools.partial(dw_qkv_kernel, len(acts)),
         grid=(d_model // tile,),
         in_specs=[part] * len(acts) + [whole] * len(grads),
         out_specs=pl.BlockSpec((tile, kv_loc, slot), lambda i: (i, 0, 0)),
         out_shape=jax.ShapeDtypeStruct((d_model, kv_loc, slot), jnp.bfloat16),
-        compiler_params=pltpu.CompilerParams(vmem_limit_bytes=62 * 2 ** 20),
-        cost_estimate=pl.CostEstimate(flops=51 * 10 ** 9, bytes_accessed=60 * 10 ** 6, transcendentals=0),
+        compiler_params=GRANT,
+        cost_estimate=cost(51, 60),
         name="dw_qkv",
     )(*acts, *grads)
 
@@ -261,15 +284,15 @@
 def dw_out(acts, grads, tile=512):
     rows, width = acts[0].shape
     d_model = grads[0][1].shape[-1]
-    whole = pl.BlockSpec((rows, width), lambda i: (0, 0))
+    whole = held_whole(rows, width)
     return pl.pallas_call(
         functools.partial(dw_out_kernel, len(acts)),
         grid=(d_model // tile,),
         in_specs=[whole] * len(acts) + [part_spec(g, b, (rows, tile), lambda i: (0, i)) for b, g in grads],
-        out_specs=pl.BlockSpec((width, tile), lambda i: (0, i)),
+        out_specs=along_columns(width, tile),
         out_shape=jax.ShapeDtypeStruct((width, d_model), jnp.bfloat16),
-        compiler_params=pltpu.CompilerParams(vmem_limit_bytes=62 * 2 ** 20),
-        cost_estimate=pl.CostEstimate(flops=39 * 10 ** 9, bytes_accessed=50 * 10 ** 6, transcendentals=0),
+        compiler_params=GRANT,
+        cost_estimate=cost(39, 50),
         name="dw_out",
     )(*acts, *[g for _, g in grads])
 
@@ -286,7 +309,7 @@
         stat_ref[rows, HEAD_DIM:] = jnp.broadcast_to(rstd, (16, HEAD_DIM))
         return carry
 
-    lax.fori_loop(0, x_ref.shape[1] // 16, group, 0, unroll=2)
+    lax.fori_loop(0, x_ref.shape[1] // 16, group, 0, unroll=True)
 
 
 def norm_fwd(x_seq, gain, b, tile=64):
@@ -294,19 +317,46 @@
     return pl.pallas_call(
         norm_fwd_kernel,
         grid=(rows // tile,),
-        in_specs=[pl.BlockSpec((1, tile, d_model), lambda i: (b, i, 0)), pl.BlockSpec((1, d_model), lambda i: (0, 0))],
-        out_specs=[pl.BlockSpec((tile, d_model), lambda i: (i, 0)), pl.BlockSpec((tile, 2 * HEAD_DIM), lambda i: (i, 0))],
+        in_specs=[pl.BlockSpec((1, tile, d_model), lambda i: (b, i, 0)), held_whole(1, d_model)],
+        out_specs=[along_rows(tile, d_model), along_rows(tile, 2 * HEAD_DIM)],
         out_shape=[jax.ShapeDtypeStruct((rows, d_model), jnp.bfloat16), jax.ShapeDtypeStruct((rows, 2 * HEAD_DIM), jnp.float32)],
-        compiler_params=pltpu.CompilerParams(vmem_limit_bytes=62 * 2 ** 20),
-        cost_estimate=pl.CostEstimate(flops=2 * 10 ** 9, bytes_accessed=7 * 10 ** 6, transcendentals=0),
+        compiler_params=GRANT,
+        cost_estimate=cost(2, 7),
         name="norm_fwd",
     )(x_seq, gain)
 
 
-def residual_kernel(x_ref, near0_ref, near1_ref, far0_ref, far1_ref, out_ref):
-    for b, (near, far) in enumerate(((near0_ref, far0_ref), (near1_ref, far1_ref))):
-        total = (near[...].astype(jnp.float32) + far[...].astype(jnp.float32)).astype(jnp.bfloat16)
-        out_ref[b] = (x_ref[b].astype(jnp.float32) + total.astype(jnp.float32)).astype(jnp.bfloat16)
+def norm_split_kernel(x_ref, gain_ref, dy_ref, h_ref, stat_ref, dy0_ref, dy1_ref):
+    norm_fwd_kernel(x_ref, gain_ref, h_ref, stat_ref)
+    dy0_ref[...] = dy_ref[0]
+    dy1_ref[...] = dy_ref[1]
+
+
+def norm_split(x_seq, gain, y_grad, b, lead=64):
+    _, rows, d_model = x_seq.shape
+    row = along_rows(lead, d_model)
+    return pl.pallas_call(
+        norm_split_kernel,
+        grid=(rows // lead,),
+        in_specs=[pl.BlockSpec((1, lead, d_model), lambda i: (b, i, 0)), held_whole(1, d_model), pl.BlockSpec((2, lead, d_model), lambda i: (0, i, 0))],
+        out_specs=[row, along_rows(lead, 2 * HEAD_DIM), row, row],
+        out_shape=[jax.ShapeDtypeStruct((rows, d_model), jnp.bfloat16), jax.ShapeDtypeStruct((rows, 2 * HEAD_DIM), jnp.float32), jax.ShapeDtypeStruct((rows, d_model), jnp.bfloat16), jax.ShapeDtypeStruct((rows, d_model), jnp.bfloat16)],
+        compiler_params=GRANT,
+        cost_estimate=cost(2, 19),
+        name="norm_split",
+    )(x_seq, gain, y_grad)
+
+
+def residual_kernel(split, x_ref, near0_ref, near1_ref, far0_ref, far1_ref, out_ref):
+    def add(near, far):
+        out_ref[0] = (x_ref[0].astype(jnp.float32) + (near[...] + far[...]).astype(jnp.float32)).astype(jnp.bfloat16)
+
+    pl.when(pl.program_id(0) < split)(lambda: add(near0_ref, far0_ref))
+    pl.when(pl.program_id(0) >= split)(lambda: add(near1_ref, far1_ref))
+
+
+def residual_last_kernel(x_ref, near_ref, far_ref, held_ref, out_ref):
+    out_ref[0] = (x_ref[0].astype(jnp.float32) + (near_ref[...] + far_ref[...]).astype(jnp.float32)).astype(jnp.bfloat16)
 
 
 def norm_bwd_kernel(x_ref, dy_ref, gain_ref, near_ref, far_ref, stat_ref, *rest):
@@ -320,7 +370,7 @@
         rows = pl.ds(pl.multiple_of(i * 16, 16), 16)
         mean, rstd = stat_ref[rows, :1], stat_ref[rows, HEAD_DIM:HEAD_DIM + 1]
         hat = (x_ref[0, rows, :].astype(jnp.float32) - mean) * rstd
-        dh = (near_ref[rows, :].astype(jnp.float32) + far_ref[rows, :].astype(jnp.float32)).astype(jnp.bfloat16).astype(jnp.float32)
+        dh = (near_ref[rows, :] + far_ref[rows, :]).astype(jnp.float32)
         prod = dh * hat
         sum_ref[...] += prod[:8] + prod[8:]
         dhat = dh * gain_ref[...].astype(jnp.float32)
@@ -336,19 +386,38 @@
 
 
 def residual(x_seq, nears, fars, tile=64):
-    batch, rows, d_model = x_seq.shape
-    whole = pl.BlockSpec((batch, tile, d_model), lambda i: (0, i, 0))
-    part = pl.BlockSpec((tile, d_model), lambda i: (i, 0))
-    return pl.pallas_call(
-        residual_kernel,
-        grid=(rows // tile,),
-        in_specs=[whole] + [part] * 4,
+    _, rows, d_model = x_seq.shape
+    split = rows // tile
+    whole = pl.BlockSpec((1, tile, d_model), lambda i: (i // split, lax.rem(i, split), 0))
+    first = pl.BlockSpec((tile, d_model), lambda i: (jnp.minimum(i, split - 1), 0))
+    second = pl.BlockSpec((tile, d_model), lambda i: (jnp.maximum(i - split, 0), 0))
+    return pl.pallas_call(
+        functools.partial(residual_kernel, split),
+        grid=(split + fars[1].shape[0] // tile,),
+        in_specs=[whole, first, second, first, second],
         out_specs=whole,
         out_shape=jax.ShapeDtypeStruct(x_seq.shape, jnp.bfloat16),
-        compiler_params=pltpu.CompilerParams(vmem_limit_bytes=62 * 2 ** 20),
-        cost_estimate=pl.CostEstimate(flops=4 * 10 ** 9, bytes_accessed=26 * 10 ** 6, transcendentals=0),
+        compiler_params=GRANT,
+        cost_estimate=cost(4, 26),
         name="residual",
     )(x_seq, *nears, *fars)
+
+
+def residual_last(x_seq, near, far, held, tile=32):
+    _, rows, d_model = x_seq.shape
+    base = (rows - far.shape[0]) // tile
+    whole = pl.BlockSpec((1, tile, d_model), lambda i: (1, base + i, 0))
+    return pl.pallas_call(
+        residual_last_kernel,
+        grid=(far.shape[0] // tile,),
+        in_specs=[whole, pl.BlockSpec((tile, d_model), lambda i: (base + i, 0)), along_rows(tile, d_model), pl.BlockSpec(memory_space=pl.ANY)],
+        out_specs=whole,
+        out_shape=jax.ShapeDtypeStruct(x_seq.shape, jnp.bfloat16),
+        input_output_aliases={3: 0},
+        compiler_params=GRANT,
+        cost_estimate=cost(1, 3),
+        name="residual_last",
+    )(x_seq, near, far, held)
 
 
 def norm_bwd(x_seq, y_grad, gain, near, far, stat, b, base, held, tile=64):
@@ -356,8 +425,8 @@
     first = base // tile
     whole = pl.BlockSpec((1, tile, d_model), lambda i: (b, first + i, 0))
     part = pl.BlockSpec((tile, d_model), lambda i: (first + i, 0))
-    piece = pl.BlockSpec((tile, d_model), lambda i: (i, 0))
-    row = pl.BlockSpec((1, d_model), lambda i: (0, 0))
+    piece = along_rows(tile, d_model)
+    row = held_whole(1, d_model)
     keep = [] if held is None else [held]
     return pl.pallas_call(
         norm_bwd_kernel,
@@ -367,30 +436,24 @@
         out_shape=[jax.ShapeDtypeStruct(x_seq.shape, jnp.bfloat16), jax.ShapeDtypeStruct((1, d_model), jnp.float32)],
         input_output_aliases={6: 0} if keep else {},
         scratch_shapes=[pltpu.VMEM((8, d_model), jnp.float32)],
-        compiler_params=pltpu.CompilerParams(vmem_limit_bytes=62 * 2 ** 20),
-        cost_estimate=pl.CostEstimate(flops=4 * 10 ** 9, bytes_accessed=16 * 10 ** 6, transcendentals=0),
+        compiler_params=GRANT,
+        cost_estimate=cost(4, 16),
         name="norm_bwd",
     )(x_seq, y_grad, gain, near, far, stat, *keep)
 
 
-def proj_deep_kernel(n_parts, dims, *refs):
-    parts, w_ref, outs, accs = refs[:n_parts], refs[n_parts], refs[n_parts + 1:2 * n_parts + 1], refs[2 * n_parts + 1:]
+def proj_deep_kernel(dims, a_ref, w_ref, out_ref, acc_ref):
     step, last = pl.program_id(0), pl.num_programs(0) - 1
 
     @pl.when(step == 0)
     def _():
-        for a, acc in zip(parts, accs):
-            acc[...] = dot(a[...], w_ref[...], dims)
-
-    @pl.when((step > 0) & (step < last))
-    def _():
-        for a, acc in zip(parts, accs):
-            acc[...] += dot(a[...], w_ref[...], dims)
+        acc_ref[...] = jnp.zeros_like(acc_ref)
+
+    acc_ref[...] += dot(a_ref[...], w_ref[...], dims)
 
     @pl.when(step == last)
     def _():
-        for a, acc, out in zip(parts, accs, outs):
-            out[...] = (acc[...] + dot(a[...], w_ref[...], dims)).astype(jnp.bfloat16)
+        out_ref[...] = acc_ref[...].astype(jnp.bfloat16)
 
 
 def part_spec(a, b, block, index):
@@ -399,41 +462,94 @@
     return pl.BlockSpec((None,) + block, lambda i: (b,) + index(i))
 
 
-def proj_deep(parts, w, dims, tile=1024):
-    rows, depth = parts[0].shape[-2:]
+def proj_raw_kernel(n_parts, *refs):
+    mine, theirs, w_ref = refs[:n_parts], refs[n_parts:2 * n_parts], refs[2 * n_parts]
+    outs, flat_ref = refs[2 * n_parts + 1:3 * n_parts + 1], refs[3 * n_parts + 1]
+    accs, joined = refs[3 * n_parts + 2:-1], refs[-1]
+    step, last = pl.program_id(0), pl.num_programs(0) - 1
+    core = lax.rem(lax.axis_index("tp"), 2)
+    rows = mine[0].shape[0]
+
+    @pl.when(step == 0)
+    def _():
+        for acc in accs:
+            acc[...] = jnp.zeros_like(acc)
+
+    flat_ref[...] = w_ref[...].reshape(flat_ref.shape)
+    for b in range(n_parts):
+        joined[b, pl.ds(pl.multiple_of(core * rows, rows), rows), :] = mine[b][...]
+        joined[b, pl.ds(pl.multiple_of((1 - core) * rows, rows), rows), :] = theirs[b][...]
+    for b, acc in enumerate(accs):
+        acc[...] += dot(joined[b], flat_ref[...], NN)
+
+    @pl.when(step == last)
+    def _():
+        for acc, out in zip(accs, outs):
+            out[...] = acc[...].astype(jnp.bfloat16)
+
+
+def proj_raw(mine, theirs, w, tile=512):
+    rows, depth = mine[0].shape
+    n_parts = len(mine)
+    slots, slot = w.shape[1:]
+    width = slots * slot
+    return pl.pallas_call(
+        functools.partial(proj_raw_kernel, n_parts),
+        grid=(depth // tile,),
+        in_specs=[along_columns(rows, tile)] * (2 * n_parts) + [pl.BlockSpec((tile, slots, slot), lambda i: (i, 0, 0))],
+        out_specs=[held_whole(2 * rows, width)] * n_parts + [along_rows(tile, width)],
+        out_shape=[jax.ShapeDtypeStruct((2 * rows, width), jnp.bfloat16)] * n_parts + [jax.ShapeDtypeStruct((depth, width), jnp.bfloat16)],
+        scratch_shapes=[pltpu.VMEM((2 * rows, width), jnp.float32)] * n_parts + [pltpu.VMEM((n_parts, 2 * rows, tile), jnp.bfloat16)],
+        compiler_params=GRANT,
+        cost_estimate=matmul_cost(2 * n_parts * rows, depth, width),
+        name="proj_raw",
+    )(*mine, *theirs, w)
+
+
+def proj_deep(a, w, dims, b=0, tile=1024):
+    rows, depth = a.shape[-2:]
     width = w.shape[0] if dims is NT else w.shape[1]
-    w_spec = pl.BlockSpec((width, tile), lambda i: (0, i)) if dims is NT else pl.BlockSpec((tile, width), lambda i: (i, 0))
-    return pl.pallas_call(
-        functools.partial(proj_deep_kernel, len(parts), dims),
+    return pl.pallas_call(
+        functools.partial(proj_deep_kernel, dims),
         grid=(depth // tile,),
-        in_specs=[part_spec(a, b, (rows, tile), lambda i: (0, i)) for b, a in enumerate(parts)] + [w_spec],
-        out_specs=[pl.BlockSpec((rows, width), lambda i: (0, 0))] * len(parts),
-        out_shape=[jax.ShapeDtypeStruct((rows, width), jnp.bfloat16)] * len(parts),
-        scratch_shapes=[pltpu.VMEM((rows, width), jnp.float32)] * len(parts),
-        compiler_params=pltpu.CompilerParams(vmem_limit_bytes=62 * 2 ** 20),
-        cost_estimate=pl.CostEstimate(flops=2 * len(parts) * rows * depth * width, bytes_accessed=2 * depth * width, transcendentals=0),
+        in_specs=[part_spec(a, b, (rows, tile), lambda i: (0, i)), along_columns(width, tile) if dims is NT else along_rows(tile, width)],
+        out_specs=held_whole(rows, width),
+        out_shape=jax.ShapeDtypeStruct((rows, width), jnp.bfloat16),
+        scratch_shapes=[pltpu.VMEM((rows, width), jnp.float32)],
+        compiler_params=GRANT,
+        cost_estimate=matmul_cost(rows, depth, width),
         name="proj_deep",
-    )(*parts, w)
-
-
-def proj_wide_kernel(n_parts, dims, *refs):
-    w_ref = refs[n_parts]
-    for a, out in zip(refs[:n_parts], refs[n_parts + 1:]):
+    )(a, w)
+
+
+def proj_wide_kernel(n_parts, dims, cut, *refs):
+    w_ref, outs = refs[n_parts], refs[n_parts + 1:]
+    first = dot(refs[0][...], w_ref[...], dims).astype(jnp.bfloat16)
+    half, rest = first.shape[0] // 2, outs[1:]
+    if cut == half:
+        outs[0][...] = first
+    else:
+        rest = outs[2:]
+        outs[0][:cut], outs[0][cut:] = first[:cut], first[half:half + cut]
+        outs[1][:half - cut], outs[1][half - cut:] = first[cut:half], first[half + cut:]
+    for a, out in zip(refs[1:n_parts], rest):
         out[...] = dot(a[...], w_ref[...], dims).astype(jnp.bfloat16)
 
 
-def proj_wide(parts, w, dims, tile=1024):
+def proj_wide(parts, w, dims, cut=None, tile=1024):
     rows, depth = parts[0].shape
+    cut = cut or rows // 2
     width = w.shape[0] if dims is NT else w.shape[1]
-    w_spec = pl.BlockSpec((tile, depth), lambda i: (i, 0)) if dims is NT else pl.BlockSpec((depth, tile), lambda i: (0, i))
-    return pl.pallas_call(
-        functools.partial(proj_wide_kernel, len(parts), dims),
+    w_spec = along_rows(tile, depth) if dims is NT else along_columns(depth, tile)
+    sizes = [2 * cut] + [rows - 2 * cut] * (2 * cut < rows) + [rows] * (len(parts) - 1)
+    return pl.pallas_call(
+        functools.partial(proj_wide_kernel, len(parts), dims, cut),
         grid=(width // tile,),
-        in_specs=[pl.BlockSpec((rows, depth), lambda i: (0, 0))] * len(parts) + [w_spec],
-        out_specs=[pl.BlockSpec((rows, tile), lambda i: (0, i))] * len(parts),
-        out_shape=[jax.ShapeDtypeStruct((rows, width), jnp.bfloat16)] * len(parts),
-        compiler_params=pltpu.CompilerParams(vmem_limit_bytes=62 * 2 ** 20),
-        cost_estimate=pl.CostEstimate(flops=2 * len(parts) * rows * depth * width, bytes_accessed=2 * depth * width, transcendentals=0),
+        in_specs=[held_whole(rows, depth)] * len(parts) + [w_spec],
+        out_specs=[along_columns(size, tile) for size in sizes],
+        out_shape=[jax.ShapeDtypeStruct((size, width), jnp.bfloat16) for size in sizes],
+        compiler_params=GRANT,
+        cost_estimate=matmul_cost(len(parts) * rows, depth, width),
         name="proj_wide",
     )(*parts, w)
 
@@ -463,51 +579,53 @@
             token[0] = jax.tree.leaves(result)[0]
             return result
 
-        cos_t, sin_t = rope_tables(x_seq.shape[1] * n_tp)
         h0, stat0 = run(lambda x: norm_fwd(x, gain, 0), x_seq)
         hx0 = swap(h0, 2)
-        h1, stat1 = run(lambda x: norm_fwd(x, gain, 1), x_seq)
+        hs0 = swap(h0, 1)
+        h1, stat1, dy0, dy1 = run(lambda x: norm_split(x, gain, y_grad, 1), x_seq)
+        hs1 = swap(h1, 1)
         hx1 = swap(h1, 2)
-        dy0, dy1, _ = lax.optimization_barrier((y_grad[0], y_grad[1], h1))
         dyx0 = swap(dy0, 2)
         dyx1 = swap(dy1, 2)
         h_own0, h_own1 = pair_gather(h0), pair_gather(h1)
         dy_own = pair_gather(y_grad, 1)
-        w_flat = run(lambda w: lax.optimization_barrier(w.reshape(w.shape[0], -1)), w_qkv)
-        qkv_own0, qkv_own1 = run(lambda h: proj_deep([h, h_own1], w_flat, NN), h_own0)
+        cos_t, sin_t = run(lambda p: lax.optimization_barrier(rope_tables(p)), jnp.arange(x_seq.shape[1] * n_tp, dtype=jnp.float32))
+        qkv_own0, qkv_own1, w_flat = run(lambda h: proj_raw([h, h1], [hs0, hs1], w_qkv), h0)
+        dattn_own0 = run(lambda d: proj_deep(d, w_out, NT, 0), dy_own)
         h_far0 = pair_gather(hx0)
-        dattn_own0, dattn_own1 = run(lambda d: proj_deep([d, d], w_out, NT), dy_own)
-        (qkv_far0,) = run(lambda h: proj_deep([h], w_flat, NN), h_far0)
+        dattn_own1 = run(lambda d: proj_deep(d, w_out, NT, 1), dy_own)
+        qkv_far0 = run(lambda h: proj_deep(h, w_flat, NN), h_far0)
         attn_own0, attn_far0, lse0 = run(lambda far: attn_fwd(qkv_own0, far, cos_t, sin_t, kv_loc), qkv_far0)
         h_far1 = pair_gather(hx1)
         o_far0, o_near0 = run(lambda a: proj_wide([a, attn_own0], w_out, NN), attn_far0)
         os_far0, os_near0 = pair_scatter(o_far0), pair_scatter(o_near0)
-        (qkv_far1,) = run(lambda h: proj_deep([h], w_flat, NN), h_far1)
+        qkv_far1 = run(lambda h: proj_deep(h, w_flat, NN), h_far1)
         ox0 = swap(os_far0, 2)
         attn_own1, attn_far1, lse1 = run(lambda far: attn_fwd(qkv_own1, far, cos_t, sin_t, kv_loc), qkv_far1)
         dy_far0 = pair_gather(dyx0)
-        o_far1, o_near1 = run(lambda a: proj_wide([a, attn_own1], w_out, NN), attn_far1)
-        os_far1, os_near1 = pair_scatter(o_far1), pair_scatter(o_near1)
-        (dattn_far0,) = run(lambda d: proj_deep([d], w_out, NT), dy_far0)
-        ox1 = swap(os_far1, 2)
+        cut = x_seq.shape[1] * 3 // 4
+        o_far1a, o_far1b, o_near1 = run(lambda a: proj_wide([a, attn_own1], w_out, NN, cut), attn_far1)
+        os_far1a, os_far1b = pair_scatter(o_far1a), pair_scatter(o_far1b)
+        os_near1 = pair_scatter(o_near1)
+        dattn_far0 = run(lambda d: proj_deep(d, w_out, NT), dy_far0)
+        ox1a, ox1b = swap(os_far1a, 2), swap(os_far1b, 2)
         dq_own0, dq_far0 = run(lambda d: attn_bwd(qkv_own0, qkv_far0, attn_own0, attn_far0, dattn_own0, d, lse0, cos_t, sin_t, kv_loc), dattn_far0)
         dy_far1 = pair_gather(dyx1)
         dh_far0, dh_near0 = run(lambda d: proj_wide([d, dq_own0], w_flat, NT), dq_far0)
         dhs_far0, dhs_near0 = pair_scatter(dh_far0), pair_scatter(dh_near0)
-        (dattn_far1,) = run(lambda d: proj_deep([d], w_out, NT), dy_far1)
+        dattn_far1 = run(lambda d: proj_deep(d, w_out, NT), dy_far1)
         dhx0 = swap(dhs_far0, 2)
         dq_own1, dq_far1 = run(lambda d: attn_bwd(qkv_own1, qkv_far1, attn_own1, attn_far1, dattn_own1, d, lse1, cos_t, sin_t, kv_loc), dattn_far1)
         dh_far1, dh_near1 = run(lambda d: proj_wide([d, dq_own1], w_flat, NT), dq_far1)
         dhs_far1, dhs_near1 = pair_scatter(dh_far1), pair_scatter(dh_near1)
         wout_grad = run(lambda a: dw_out([a, attn_far0, attn_own1, attn_far1], [(0, dy_own), (0, dy_far0), (1, dy_own), (0, dy_far1)]), attn_own0)
-        cut = dhs_far1.shape[0] // 2
-        dhx1a, dhx1b = swap(dhs_far1[:cut], 2), swap(dhs_far1[cut:], 2)
-        y_out = run(lambda near: residual(x_seq, [near, os_near1], [ox0, ox1]), os_near0)
+        dhx1 = swap(dhs_far1, 2)
+        y_out = run(lambda near: residual(x_seq, [near, os_near1], [ox0, ox1a]), os_near0)
         wqkv_grad = run(lambda h: dw_qkv([h, h_far0, h_own1, h_far1], [dq_own0, dq_far0, dq_own1, dq_far1], kv_loc), h_own0)
         x_grad, gain0 = run(lambda near: norm_bwd(x_seq, y_grad, gain, near, dhx0, stat0, 0, 0, None), dhs_near0)
-        x_grad, gain1 = run(lambda near: norm_bwd(x_seq, y_grad, gain, near, dhx1a, stat1, 1, 0, x_grad), dhs_near1)
-        x_grad, gain2 = run(lambda near: norm_bwd(x_seq, y_grad, gain, near, dhx1b, stat1, 1, cut, x_grad), dhs_near1)
-        mine = gain0 + gain1 + gain2
+        x_grad, gain1 = run(lambda near: norm_bwd(x_seq, y_grad, gain, near, dhx1, stat1, 1, 0, x_grad), dhs_near1)
+        y_out = run(lambda near: residual_last(x_seq, near, ox1b, y_out), os_near1)
+        mine = gain0 + gain1
         gain_grad = (mine + swap(mine, 1) + swap(mine, 2) + swap(mine, 3)).astype(jnp.bfloat16)[0]
         return y_out, x_grad, gain_grad, wqkv_grad, wout_grad
 

time: 973 us -> 977 us (level)
  local copies, waits for them, and re-layouts: 44.5 us -> 3.21 us
  waiting for transfers between devices: 383 us -> 415 us
  Pallas kernels: 506 us -> 518 us
    unnamed x15 -> x10, local copies, waits for them, and re-layouts: 33.3 us -> 2.57 us
    ppermute x12 -> x14, waiting for transfers between devices: 380 us -> 409 us  [swap(): return lax.ppermute(value, 'tp', [(i, i ^ bit) for i in range(n_tp)])]
    pallas_call x11 -> x14, Pallas kernels: 251 us -> 273 us  [the longest x4 113 us: proj_wide(): pl.pallas_call(functools.partial(proj_wide_kernel, len(parts), dims, cut)...]
    pallas_call x3 -> x2, Pallas kernels: 24.1 us -> 20.3 us  [norm_bwd(): pl.pallas_call(norm_bwd_kernel, grid=(far.shape[0] // tile,), in_specs=[w...]
  transfers between devices with their start and end apart: 27 -> 30, of which waited for: 9 -> 7; matrix products, arithmetic and copies ran while one was open for 4% -> 0% of each run, Pallas kernels for 51% -> 53%
where the time goes in v3:
time: 977 us; the launch traced here: 972 us
  Pallas kernels  518 us (53%)
  waiting for transfers between devices  415 us (42%)
  starting transfers between devices  15.8 us (2%)
  between operations  14.6 us (1%)
    ppermute x14, waiting for transfers between devices, swap(): return lax.ppermute(value, 'tp', [(i, i ^ bit) for i in range(n_tp)])  409 us
    pallas_call x4, Pallas kernels, proj_wide(): pl.pallas_call(functools.partial(proj_wide_kernel, len(parts), dims, cut)...  113 us
    pallas_call x6, Pallas kernels, proj_deep(): pl.pallas_call(functools.partial(proj_deep_kernel, dims), grid=(depth //...  102 us
    pallas_call x1, Pallas kernels, dw_qkv(): pl.pallas_call(functools.partial(dw_qkv_kernel, len(acts)), grid=(d_model...  63.9 us
    pallas_call x2, Pallas kernels, attn_bwd(): pl.pallas_call(functools.partial(attn_bwd_kernel, groups), grid=(kv_loc,)...  63.7 us
    pallas_call x1, Pallas kernels, dw_out(): pl.pallas_call(functools.partial(dw_out_kernel, len(acts)), grid=(d_model...  48.8 us
    pallas_call x2, Pallas kernels, attn_fwd(): pl.pallas_call(functools.partial(attn_fwd_kernel, groups), grid=(kv_loc,)...  43.7 us
    pallas_call x1, Pallas kernels, proj_raw(): pl.pallas_call(functools.partial(proj_raw_kernel, n_parts), grid=(depth /...  37 us
  transfers between devices with their start and end apart: 30, of which 7 were waited for; matrix products, arithmetic and copies ran while one was open for 0% of the time, Pallas kernels for 53%

profile of v3, /device:TPU:0, one launch (start us, length us, event | category | flops | bytes accessed | tf_op | source)
XLA Modules:
  0.0 972.0 jit_solution(572438285999272571)
XLA Ops:
  17.5 68.3 %collective-permute-done.3 = bf16[256,6144]{1,0:T(8,128)(2,1)S(1)} collective-permute-done((bf16[256,6144]{1,0:T(8,128)(2,1)}, bf16[256,6144]{1,0:T(8,128)(2,1)S(1)}, u32[]{:S(2)}, u32[]{:S(2)}) %collective-permute-start.3) | collective-permute-done | bytes 3145760 | tf_op jit(solution)/shard_map/ppermute | solution.py:562
  98.5 67.7 %collective-permute-done.2 = bf16[256,6144]{1,0:T(8,128)(2,1)} collective-permute-done((bf16[256,6144]{1,0:T(8,128)(2,1)}, bf16[256,6144]{1,0:T(8,128)(2,1)}, u32[]{:S(2)}, u32[]{:S(2)}) %collective-permute-start.2) | collective-permute-done | bytes 3145760 | tf_op jit(solution)/shard_map/ppermute | solution.py:562
  167.8 67.2 %collective-permute-done.5 = bf16[256,6144]{1,0:T(8,128)(2,1)} collective-permute-done((bf16[256,6144]{1,0:T(8,128)(2,1)}, bf16[256,6144]{1,0:T(8,128)(2,1)}, u32[]{:S(2)}, u32[]{:S(2)}) %collective-permute-start.5) | collective-permute-done | bytes 3145760 | tf_op jit(solution)/shard_map/ppermute | solution.py:562
  240.0 62.8 %collective-permute-done.4 = bf16[256,6144]{1,0:T(8,128)(2,1)} collective-permute-done((bf16[256,6144]{1,0:T(8,128)(2,1)}, bf16[256,6144]{1,0:T(8,128)(2,1)}, u32[]{:S(2)}, u32[]{:S(2)}) %collective-permute-start.4) | collective-permute-done | bytes 3145760 | tf_op jit(solution)/shard_map/ppermute | solution.py:562
  303.5 37.0 %proj_raw.1 = (bf16[512,2048]{1,0:T(8,128)(2,1)}, bf16[512,2048]{1,0:T(8,128)(2,1)}, bf16[6144,2048]{1,0:T(8,128)(2,1)}) custom-call(bf16[256,6144]{1,0:T(8,128)(2,1)} %get-tuple-element.65.refs_0_, bf16[256,6144]{1,0:T(8,128)(2,1)} %get-tuple-element.62.refs_1_, bf16[256,6144]{1,0:T(8,128)(2,1)} %collective-permute-done.refs_2_, ...), custom_call_target="tpu_custom_call" | custom-call | flops 25769803776 | bytes 25165824 | tf_op jit(solution)/shard_map/proj_raw/pallas_call | solution.py:496
  340.5 15.8 %proj_deep.6.down_ref = bf16[512,1536]{1,0:T(8,128)(2,1)} custom-call(bf16[2,512,6144]{2,1,0:T(8,128)(2,1)} %all-gather.12.cloned.1.call-done.a_ref.refs_4_.refs_6_, bf16[1536,6144]{1,0:T(8,128)(2,1)} %w_ref.7), custom_call_target="tpu_custom_call" | custom-call | flops 9663676416 | bytes 18874368 | tf_op jit(solution)/shard_map/proj_deep/pallas_call | solution.py:512
  356.3 15.6 %proj_deep.7.down_ref = bf16[512,1536]{1,0:T(8,128)(2,1)} custom-call(bf16[2,512,6144]{2,1,0:T(8,128)(2,1)} %all-gather.12.cloned.1.call-done.a_ref.refs_4_.refs_6_, bf16[1536,6144]{1,0:T(8,128)(2,1)} %w_ref.7), custom_call_target="tpu_custom_call" | custom-call | flops 9663676416 | bytes 18874368 | tf_op jit(solution)/shard_map/proj_deep/pallas_call | solution.py:512
  371.9 18.8 %proj_deep.8.far_ref = bf16[512,2048]{1,0:T(8,128)(2,1)} custom-call(bf16[512,6144]{1,0:T(8,128)(2,1)} %all-gather.10.cloned.1.call-done.a_ref.refs_1_, bf16[6144,2048]{1,0:T(8,128)(2,1)} %get-tuple-element.71.w_ref.refs_2_), custom_call_target="tpu_custom_call" | custom-call | flops 12884901888 | bytes 25165824 | tf_op jit(solution)/shard_map/proj_deep/pallas_call | solution.py:512
  390.7 21.8 %attn_fwd.2 = (bf16[512,1536]{1,0:T(8,128)(2,1)}, bf16[512,1536]{1,0:T(8,128)(2,1)}, f32[1024,1536]{1,0:T(8,128)}) custom-call(bf16[512,2048]{1,0:T(8,128)(2,1)} %get-tuple-element.67.own_ref, bf16[512,2048]{1,0:T(8,128)(2,1)} %proj_deep.8.far_ref, f32[1024,128]{1,0:T(8,128)} %get-tuple-element.64.cos_ref, f32[1024,128]{1,0:T(8,128)} %get-tuple-element.73.sin_ref), custom_call_target="tpu_custom_call" | custom-call | flops 12000000000 | bytes 14000000 | tf_op jit(solution)/shard_map/attn_fwd/pallas_call | solution.py:220
  412.6 24.7 %proj_wide.4 = (bf16[512,6144]{1,0:T(8,128)(2,1)}, bf16[512,6144]{1,0:T(8,128)(2,1)}) custom-call(bf16[512,1536]{1,0:T(8,128)(2,1)} %get-tuple-element.76.refs_0_.afar_ref.refs_1_, bf16[512,1536]{1,0:T(8,128)(2,1)} %get-tuple-element.102.refs_1_.aown_ref.refs_0_, bf16[1536,6144]{1,0:T(8,128)(2,1)} %w_ref.7), custom_call_target="tpu_custom_call" | custom-call | flops 19327352832 | bytes 18874368 | tf_op jit(solution)/shard_map/proj_wide/pallas_call | solution.py:545
  437.3 18.8 %proj_deep.9.far_ref = bf16[512,2048]{1,0:T(8,128)(2,1)} custom-call(bf16[512,6144]{1,0:T(8,128)(2,1)} %all-gather.8.cloned.1.call-done.a_ref.refs_3_, bf16[6144,2048]{1,0:T(8,128)(2,1)} %get-tuple-element.71.w_ref.refs_2_), custom_call_target="tpu_custom_call" | custom-call | flops 12884901888 | bytes 25165824 | tf_op jit(solution)/shard_map/proj_deep/pallas_call | solution.py:512
  456.1 21.8 %attn_fwd.3 = (bf16[512,1536]{1,0:T(8,128)(2,1)}, bf16[512,1536]{1,0:T(8,128)(2,1)}, f32[1024,1536]{1,0:T(8,128)}) custom-call(bf16[512,2048]{1,0:T(8,128)(2,1)} %get-tuple-element.66.own_ref, bf16[512,2048]{1,0:T(8,128)(2,1)} %proj_deep.9.far_ref, f32[1024,128]{1,0:T(8,128)} %get-tuple-element.64.cos_ref, f32[1024,128]{1,0:T(8,128)} %get-tuple-element.73.sin_ref), custom_call_target="tpu_custom_call" | custom-call | flops 12000000000 | bytes 14000000 | tf_op jit(solution)/shard_map/attn_fwd/pallas_call | solution.py:220
  477.9 24.5 %proj_wide.5 = (bf16[384,6144]{1,0:T(8,128)(2,1)}, bf16[128,6144]{1,0:T(8,128)(2,1)}, bf16[512,6144]{1,0:T(8,128)(2,1)}) custom-call(bf16[512,1536]{1,0:T(8,128)(2,1)} %get-tuple-element.82.refs_0_.afar_ref.refs_3_, bf16[512,1536]{1,0:T(8,128)(2,1)} %get-tuple-element.81.refs_1_.aown_ref.refs_2_, bf16[1536,6144]{1,0:T(8,128)(2,1)} %w_ref.7), custom_call_target="tpu_custom_call" | custom-call | flops 19327352832 | bytes 18874368 | tf_op jit(solution)/shard_map/proj_wide/pallas_call | solution.py:545
  504.7 16.8 %proj_deep.10.dfar_ref = bf16[512,1536]{1,0:T(8,128)(2,1)} custom-call(bf16[512,6144]{1,0:T(8,128)(2,1)} %all-gather.16.cloned.1.call-done.a_ref.refs_5_, bf16[1536,6144]{1,0:T(8,128)(2,1)} %w_ref.7), custom_call_target="tpu_custom_call" | custom-call | flops 9663676416 | bytes 18874368 | tf_op jit(solution)/shard_map/proj_deep/pallas_call | solution.py:512
  521.5 32.7 %attn_bwd.2 = (bf16[512,2048]{1,0:T(8,128)(2,1)}, bf16[512,2048]{1,0:T(8,128)(2,1)}) custom-call(bf16[512,2048]{1,0:T(8,128)(2,1)} %get-tuple-element.67.own_ref, bf16[512,2048]{1,0:T(8,128)(2,1)} %proj_deep.8.far_ref, bf16[512,1536]{1,0:T(8,128)(2,1)} %get-tuple-element.102.refs_1_.aown_ref.refs_0_, ...), custom_call_target="tpu_custom_call" | custom-call | flops 24999999488 | bytes 22000000 | tf_op jit(solution)/shard_map/attn_bwd/pallas_call | solution.py:239
  554.3 31.8 %proj_wide.6 = (bf16[512,6144]{1,0:T(8,128)(2,1)}, bf16[512,6144]{1,0:T(8,128)(2,1)}) custom-call(bf16[512,2048]{1,0:T(8,128)(2,1)} %get-tuple-element.91.refs_0_.refs_5_, bf16[512,2048]{1,0:T(8,128)(2,1)} %get-tuple-element.90.refs_1_.refs_4_, bf16[6144,2048]{1,0:T(8,128)(2,1)} %get-tuple-element.71.w_ref.refs_2_), custom_call_target="tpu_custom_call" | custom-call | flops 25769803776 | bytes 25165824 | tf_op jit(solution)/shard_map/proj_wide/pallas_call | solution.py:545
  586.1 15.6 %proj_deep.11.dfar_ref = bf16[512,1536]{1,0:T(8,128)(2,1)} custom-call(bf16[512,6144]{1,0:T(8,128)(2,1)} %all-gather.14.cloned.1.call-done.a_ref.refs_7_, bf16[1536,6144]{1,0:T(8,128)(2,1)} %w_ref.7), custom_call_target="tpu_custom_call" | custom-call | flops 9663676416 | bytes 18874368 | tf_op jit(solution)/shard_map/proj_deep/pallas_call | solution.py:512
  601.7 30.9 %attn_bwd.3 = (bf16[512,2048]{1,0:T(8,128)(2,1)}, bf16[512,2048]{1,0:T(8,128)(2,1)}) custom-call(bf16[512,2048]{1,0:T(8,128)(2,1)} %get-tuple-element.66.own_ref, bf16[512,2048]{1,0:T(8,128)(2,1)} %proj_deep.9.far_ref, bf16[512,1536]{1,0:T(8,128)(2,1)} %get-tuple-element.81.refs_1_.aown_ref.refs_2_, ...), custom_call_target="tpu_custom_call" | custom-call | flops 24999999488 | bytes 22000000 | tf_op jit(solution)/shard_map/attn_bwd/pallas_call | solution.py:239
  632.7 31.8 %proj_wide.7 = (bf16[512,6144]{1,0:T(8,128)(2,1)}, bf16[512,6144]{1,0:T(8,128)(2,1)}) custom-call(bf16[512,2048]{1,0:T(8,128)(2,1)} %get-tuple-element.97.refs_0_.refs_7_, bf16[512,2048]{1,0:T(8,128)(2,1)} %get-tuple-element.96.refs_1_.refs_6_, bf16[6144,2048]{1,0:T(8,128)(2,1)} %get-tuple-element.71.w_ref.refs_2_), custom_call_target="tpu_custom_call" | custom-call | flops 25769803776 | bytes 25165824 | tf_op jit(solution)/shard_map/proj_wide/pallas_call | solution.py:545
  670.3 48.8 %dw_out.1 = bf16[1536,6144]{1,0:T(8,128)(2,1)} custom-call(bf16[512,1536]{1,0:T(8,128)(2,1)} %get-tuple-element.102.refs_1_.aown_ref.refs_0_, bf16[512,1536]{1,0:T(8,128)(2,1)} %get-tuple-element.76.refs_0_.afar_ref.refs_1_, bf16[512,1536]{1,0:T(8,128)(2,1)} %get-tuple-element.81.refs_1_.aown_ref.refs_2_, ...), custom_call_target="tpu_custom_call" | custom-call | flops 38999998464 | bytes 50000000 | tf_op jit(solution)/shard_map/dw_out/pallas_call | solution.py:288
  722.7 67.4 %collective-permute-done.6.far0_ref = bf16[256,6144]{1,0:T(8,128)(2,1)} collective-permute-done((bf16[256,6144]{1,0:T(8,128)(2,1)}, bf16[256,6144]{1,0:T(8,128)(2,1)}, u32[]{:S(2)}, u32[]{:S(2)}) %collective-permute-start.6) | collective-permute-done | bytes 3145760 | tf_op jit(solution)/shard_map/ppermute | solution.py:562
  799.9 63.9 %dw_qkv.1 = bf16[6144,2,1024]{2,1,0:T(2,128)(2,1)} custom-call(bf16[512,6144]{1,0:T(8,128)(2,1)} %all-gather.18.cloned.1.call-done.refs_0_, bf16[512,6144]{1,0:T(8,128)(2,1)} %all-gather.10.cloned.1.call-done.a_ref.refs_1_, bf16[512,6144]{1,0:T(8,128)(2,1)} %all-gather.20.cloned.1.call-done.refs_2_, ...), custom_call_target="tpu_custom_call" | custom-call | flops 51000000512 | bytes 60000000 | tf_op jit(solution)/shard_map/dw_qkv/pallas_call | solution.py:267
  863.8 74.1 %collective-permute-done.8.far_ref = bf16[256,6144]{1,0:T(8,128)(2,1)} collective-permute-done((bf16[256,6144]{1,0:T(8,128)(2,1)}, bf16[256,6144]{1,0:T(8,128)(2,1)}, u32[]{:S(2)}, u32[]{:S(2)}) %collective-permute-start.8) | collective-permute-done | bytes 3145760 | tf_op jit(solution)/shard_map/ppermute | solution.py:562
  948.0 10.2 %norm_bwd.3 = (bf16[2,256,6144]{2,1,0:T(8,128)(2,1)}, f32[1,6144]{1,0:T(1,128)}) custom-call(bf16[2,256,6144]{2,1,0:T(8,128)(2,1)} %x_ref.10, bf16[2,256,6144]{2,1,0:T(8,128)(2,1)} %dy_ref.5, bf16[1,6144]{1,0:T(2,128)(2,1)} %broadcast_in_dim.2.gain_ref, ...), custom_call_target="tpu_custom_call", output_to_operand_aliasing={{0}: (6, {})} | custom-call | flops 4000000000 | bytes 16000000 | tf_op jit(solution)/shard_map/norm_bwd/pallas_call | solution.py:431
  (92 shorter events, 68.3 us)
Async XLA Ops:
  7.2 333.3 %all-gather.12.cloned.1.call-start = ((), (), s32[]{:S(2)}) async-start(), calls=%async_computation.11 | async-start | bytes 18874368 | tf_op jit(solution)/shard_map/all_gather | solution.py:565
  7.9 364.0 %all-gather.10.cloned.1.call-start = ((), (), s32[]{:S(2)}) async-start(), calls=%async_computation.10 | async-start | bytes 9437184 | tf_op jit(solution)/shard_map/all_gather | solution.py:565
  14.2 71.6 %collective-permute-start.3 = (bf16[256,6144]{1,0:T(8,128)(2,1)}, bf16[256,6144]{1,0:T(8,128)(2,1)S(1)}, u32[]{:S(2)}, u32[]{:S(2)}) collective-permute-start(bf16[256,6144]{1,0:T(8,128)(2,1)} %get-tuple-element.65.refs_0_), channel_id=1, source_target_pairs={{0,2},{1,3},{2,0},{3,1},{4,6},{5,7},{6,4},{7,5}} | collective-permute-start | bytes 9437192 | tf_op jit(solution)/shard_map/ppermute | solution.py:562
  87.5 349.8 %all-gather.8.cloned.1.call-start = ((), (), s32[]{:S(2)}) async-start(), calls=%async_computation.9 | async-start | bytes 9437184 | tf_op jit(solution)/shard_map/all_gather | solution.py:565
  96.7 69.5 %collective-permute-start.2 = (bf16[256,6144]{1,0:T(8,128)(2,1)}, bf16[256,6144]{1,0:T(8,128)(2,1)}, u32[]{:S(2)}, u32[]{:S(2)}) collective-permute-start(bf16[256,6144]{1,0:T(8,128)(2,1)} %get-tuple-element.62.refs_1_), channel_id=1, source_target_pairs={{0,2},{1,3},{2,0},{3,1},{4,6},{5,7},{6,4},{7,5}} | collective-permute-start | bytes 9437192 | tf_op jit(solution)/shard_map/ppermute | solution.py:562
  166.3 338.4 %all-gather.16.cloned.1.call-start = ((), (), s32[]{:S(2)}) async-start(), calls=%async_computation.14 | async-start | bytes 9437184 | tf_op jit(solution)/shard_map/all_gather | solution.py:565
  166.3 68.7 %collective-permute-start.5 = (bf16[256,6144]{1,0:T(8,128)(2,1)}, bf16[256,6144]{1,0:T(8,128)(2,1)}, u32[]{:S(2)}, u32[]{:S(2)}) collective-permute-start(bf16[256,6144]{1,0:T(8,128)(2,1)} %get-tuple-element.85), channel_id=1, source_target_pairs={{0,2},{1,3},{2,0},{3,1},{4,6},{5,7},{6,4},{7,5}} | collective-permute-start | bytes 9437192 | tf_op jit(solution)/shard_map/ppermute | solution.py:562
  235.0 351.0 %all-gather.14.cloned.1.call-start = ((), (), s32[]{:S(2)}) async-start(), calls=%async_computation.13 | async-start | bytes 9437184 | tf_op jit(solution)/shard_map/all_gather | solution.py:565
  235.1 67.8 %collective-permute-start.4 = (bf16[256,6144]{1,0:T(8,128)(2,1)}, bf16[256,6144]{1,0:T(8,128)(2,1)}, u32[]{:S(2)}, u32[]{:S(2)}) collective-permute-start(bf16[256,6144]{1,0:T(8,128)(2,1)} %get-tuple-element.84), channel_id=1, source_target_pairs={{0,2},{1,3},{2,0},{3,1},{4,6},{5,7},{6,4},{7,5}} | collective-permute-start | bytes 9437192 | tf_op jit(solution)/shard_map/ppermute | solution.py:562
  236.2 67.3 %collective-permute-start = (bf16[256,6144]{1,0:T(8,128)(2,1)S(1)}, bf16[256,6144]{1,0:T(8,128)(2,1)}, u32[]{:S(2)}, u32[]{:S(2)}) collective-permute-start(bf16[256,6144]{1,0:T(8,128)(2,1)S(1)} %copy-done), channel_id=1, source_target_pairs={{0,1},{1,0},{2,3},{3,2},{4,5},{5,4},{6,7},{7,6}} | collective-permute-start | bytes 9437192 | tf_op jit(solution)/shard_map/ppermute | solution.py:562
  236.2 67.3 %collective-permute-start.1 = (bf16[256,6144]{1,0:T(8,128)(2,1)}, bf16[256,6144]{1,0:T(8,128)(2,1)}, u32[]{:S(2)}, u32[]{:S(2)}) collective-permute-start(bf16[256,6144]{1,0:T(8,128)(2,1)} %get-tuple-element.62.refs_1_), channel_id=1, source_target_pairs={{0,1},{1,0},{2,3},{3,2},{4,5},{5,4},{6,7},{7,6}} | collective-permute-start | bytes 9437192 | tf_op jit(solution)/shard_map/ppermute | solution.py:562
  302.9 365.4 %reduce-scatter.20.cloned.1.call-start = ((), (), s32[]{:S(2)}) async-start(), calls=%async_computation.20 | async-start | bytes 7077888 | tf_op jit(solution)/shard_map/reduce_scatter | solution.py:568
  502.4 166.4 %reduce-scatter.18.cloned.1.call-start = ((), (), s32[]{:S(2)}) async-start(), calls=%async_computation.19 | async-start | bytes 9437184 | tf_op jit(solution)/shard_map/reduce_scatter | solution.py:568
  503.2 215.9 %reduce-scatter.26.cloned.1.call-start = ((), (), s32[]{:S(2)}) async-start(), calls=%async_computation.24 | async-start | bytes 2359296 | tf_op jit(solution)/shard_map/reduce_scatter | solution.py:568
  503.9 215.6 %reduce-scatter.16.cloned.1.call-start = ((), (), s32[]{:S(2)}) async-start(), calls=%async_computation.18 | async-start | bytes 9437184 | tf_op jit(solution)/shard_map/reduce_scatter | solution.py:568
  504.6 214.9 %reduce-scatter.24.cloned.1.call-start = ((), (), s32[]{:S(2)}) async-start(), calls=%async_computation.23 | async-start | bytes 9437184 | tf_op jit(solution)/shard_map/reduce_scatter | solution.py:568
  665.8 134.1 %all-gather.18.cloned.1.call-start = ((), (), s32[]{:S(2)}) async-start(), calls=%async_computation.17 | async-start | bytes 9437184 | tf_op jit(solution)/shard_map/all_gather | solution.py:565
  666.5 133.4 %all-gather.20.cloned.1.call-start = ((), (), s32[]{:S(2)}) async-start(), calls=%async_computation.21 | async-start | bytes 9437184 | tf_op jit(solution)/shard_map/all_gather | solution.py:565
  667.1 196.7 %reduce-scatter.14.cloned.1.call-start = ((), (), s32[]{:S(2)}) async-start(), calls=%async_computation.16 | async-start | bytes 9437184 | tf_op jit(solution)/shard_map/reduce_scatter | solution.py:568
  667.7 280.3 %reduce-scatter.12.cloned.1.call-start = ((), (), s32[]{:S(2)}) async-start(), calls=%async_computation.15 | async-start | bytes 9437184 | tf_op jit(solution)/shard_map/reduce_scatter | solution.py:568
  668.8 121.3 %collective-permute-start.6 = (bf16[256,6144]{1,0:T(8,128)(2,1)}, bf16[256,6144]{1,0:T(8,128)(2,1)}, u32[]{:S(2)}, u32[]{:S(2)}) collective-permute-start(bf16[256,6144]{1,0:T(8,128)(2,1)} %reduce-scatter.18.cloned.1.call-done), channel_id=1, source_target_pairs={{0,2},{1,3},{2,0},{3,1},{4,6},{5,7},{6,4},{7,5}} | collective-permute-start | bytes 9437192 | tf_op jit(solution)/shard_map/ppermute | solution.py:562
  719.1 241.8 %collective-permute-start.10 = (bf16[64,6144]{1,0:T(8,128)(2,1)}, bf16[64,6144]{1,0:T(8,128)(2,1)S(1)}, u32[]{:S(2)}, u32[]{:S(2)}) collective-permute-start(bf16[64,6144]{1,0:T(8,128)(2,1)} %reduce-scatter.26.cloned.1.call-done), channel_id=1, source_target_pairs={{0,2},{1,3},{2,0},{3,1},{4,6},{5,7},{6,4},{7,5}} | collective-permute-start | bytes 2359304 | tf_op jit(solution)/shard_map/ppermute | solution.py:562
  719.5 228.4 %collective-permute-start.9 = (bf16[256,6144]{1,0:T(8,128)(2,1)}, bf16[256,6144]{1,0:T(8,128)(2,1)}, u32[]{:S(2)}, u32[]{:S(2)}) collective-permute-start(bf16[256,6144]{1,0:T(8,128)(2,1)} %reduce-scatter.24.cloned.1.call-done), channel_id=1, source_target_pairs={{0,2},{1,3},{2,0},{3,1},{4,6},{5,7},{6,4},{7,5}} | collective-permute-start | bytes 9437192 | tf_op jit(solution)/shard_map/ppermute | solution.py:562
  721.1 216.8 %collective-permute-start.8 = (bf16[256,6144]{1,0:T(8,128)(2,1)}, bf16[256,6144]{1,0:T(8,128)(2,1)}, u32[]{:S(2)}, u32[]{:S(2)}) collective-permute-start(bf16[256,6144]{1,0:T(8,128)(2,1)} %reduce-scatter.22.cloned.1.call-done), channel_id=1, source_target_pairs={{0,2},{1,3},{2,0},{3,1},{4,6},{5,7},{6,4},{7,5}} | collective-permute-start | bytes 9437192 | tf_op jit(solution)/shard_map/ppermute | solution.py:562
  (11 other events, 267.0 us)
Sparse Core Ops, SparseCore 0:
  9.5 24.4 all-gather.11
  87.6 15.2 all-gather.9
  166.4 14.9 all-gather.7
  235.1 15.8 all-gather.15
  303.0 14.3 all-gather.13
  502.5 9.9 reduce-scatter.19
  514.7 12.5 reduce-scatter.17
  529.5 8.2 reduce-scatter.25
  540.1 12.5 reduce-scatter.15
  664.6 11.2 reduce-scatter.23
  678.2 13.3 reduce-scatter.21
  694.2 13.2 reduce-scatter.9
  709.0 16.0 all-gather.17
  726.5 15.1 all-gather.19
  743.8 12.3 reduce-scatter.13
  758.3 13.2 reduce-scatter.11

commit v4 on v3

--- a/solution.py
+++ b/solution.py
@@ -304,7 +304,7 @@
         mean = jnp.mean(x_f32, axis=-1, keepdims=True)
         centered = x_f32 - mean
         rstd = lax.rsqrt(jnp.mean(centered * centered, axis=-1, keepdims=True) + LN_EPS)
-        h_ref[rows, :] = (centered * rstd * gain_ref[...].astype(jnp.float32)).astype(jnp.bfloat16)
+        h_ref[rows, :] = (centered * rstd * gain_ref[...].astype(jnp.float32)[None, :]).astype(jnp.bfloat16)
         stat_ref[rows, :HEAD_DIM] = jnp.broadcast_to(mean, (16, HEAD_DIM))
         stat_ref[rows, HEAD_DIM:] = jnp.broadcast_to(rstd, (16, HEAD_DIM))
         return carry
@@ -317,7 +317,7 @@
     return pl.pallas_call(
         norm_fwd_kernel,
         grid=(rows // tile,),
-        in_specs=[pl.BlockSpec((1, tile, d_model), lambda i: (b, i, 0)), held_whole(1, d_model)],
+        in_specs=[pl.BlockSpec((1, tile, d_model), lambda i: (b, i, 0)), pl.BlockSpec((d_model,), lambda i: (0,))],
         out_specs=[along_rows(tile, d_model), along_rows(tile, 2 * HEAD_DIM)],
         out_shape=[jax.ShapeDtypeStruct((rows, d_model), jnp.bfloat16), jax.ShapeDtypeStruct((rows, 2 * HEAD_DIM), jnp.float32)],
         compiler_params=GRANT,
@@ -338,7 +338,7 @@
     return pl.pallas_call(
         norm_split_kernel,
         grid=(rows // lead,),
-        in_specs=[pl.BlockSpec((1, lead, d_model), lambda i: (b, i, 0)), held_whole(1, d_model), pl.BlockSpec((2, lead, d_model), lambda i: (0, i, 0))],
+        in_specs=[pl.BlockSpec((1, lead, d_model), lambda i: (b, i, 0)), pl.BlockSpec((d_model,), lambda i: (0,)), pl.BlockSpec((2, lead, d_model), lambda i: (0, i, 0))],
         out_specs=[row, along_rows(lead, 2 * HEAD_DIM), row, row],
         out_shape=[jax.ShapeDtypeStruct((rows, d_model), jnp.bfloat16), jax.ShapeDtypeStruct((rows, 2 * HEAD_DIM), jnp.float32), jax.ShapeDtypeStruct((rows, d_model), jnp.bfloat16), jax.ShapeDtypeStruct((rows, d_model), jnp.bfloat16)],
         compiler_params=GRANT,
@@ -373,7 +373,7 @@
         dh = (near_ref[rows, :] + far_ref[rows, :]).astype(jnp.float32)
         prod = dh * hat
         sum_ref[...] += prod[:8] + prod[8:]
-        dhat = dh * gain_ref[...].astype(jnp.float32)
+        dhat = dh * gain_ref[...].astype(jnp.float32)[None, :]
         inner = dhat - jnp.mean(dhat, axis=-1, keepdims=True) - hat * jnp.mean(dhat * hat, axis=-1, keepdims=True)
         dx_ref[0, rows, :] = (dy_ref[0, rows, :].astype(jnp.float32) + inner * rstd).astype(jnp.bfloat16)
         return carry
@@ -427,11 +427,12 @@
     part = pl.BlockSpec((tile, d_model), lambda i: (first + i, 0))
     piece = along_rows(tile, d_model)
     row = held_whole(1, d_model)
+    flat = pl.BlockSpec((d_model,), lambda i: (0,))
     keep = [] if held is None else [held]
     return pl.pallas_call(
         norm_bwd_kernel,
         grid=(far.shape[0] // tile,),
-        in_specs=[whole, whole, row, part, piece, pl.BlockSpec((tile, 2 * HEAD_DIM), lambda i: (first + i, 0))] + [pl.BlockSpec(memory_space=pl.ANY)] * len(keep),
+        in_specs=[whole, whole, flat, part, piece, pl.BlockSpec((tile, 2 * HEAD_DIM), lambda i: (first + i, 0))] + [pl.BlockSpec(memory_space=pl.ANY)] * len(keep),
         out_specs=[whole, row],
         out_shape=[jax.ShapeDtypeStruct(x_seq.shape, jnp.bfloat16), jax.ShapeDtypeStruct((1, d_model), jnp.float32)],
         input_output_aliases={6: 0} if keep else {},
@@ -569,7 +570,7 @@
 
     def staged_step(x_seq, ln_gain, w_qkv, w_out, y_grad):
         kv_loc = w_qkv.shape[1]
-        gain = ln_gain[None, :]
+        gain = ln_gain
         token = [None]
 
         def run(fn, lead, *rest):

time: 977 us -> 976 us (level)
  no operation moved by 1% of the time
where the time goes in v4:
time: 976 us; the launch traced here: 971 us
  Pallas kernels  519 us (53%)
  waiting for transfers between devices  415 us (43%)
  starting transfers between devices  15.7 us (2%)
  between operations  14.6 us (1%)
    ppermute x14, waiting for transfers between devices, swap(): return lax.ppermute(value, 'tp', [(i, i ^ bit) for i in range(n_tp)])  409 us
    pallas_call x4, Pallas kernels, proj_wide(): pl.pallas_call(functools.partial(proj_wide_kernel, len(parts), dims, cut)...  113 us
    pallas_call x6, Pallas kernels, proj_deep(): pl.pallas_call(functools.partial(proj_deep_kernel, dims), grid=(depth //...  102 us
    pallas_call x1, Pallas kernels, dw_qkv(): pl.pallas_call(functools.partial(dw_qkv_kernel, len(acts)), grid=(d_model...  63.9 us
    pallas_call x2, Pallas kernels, attn_bwd(): pl.pallas_call(functools.partial(attn_bwd_kernel, groups), grid=(kv_loc,)...  63.7 us
    pallas_call x1, Pallas kernels, dw_out(): pl.pallas_call(functools.partial(dw_out_kernel, len(acts)), grid=(d_model...  48.8 us
    pallas_call x2, Pallas kernels, attn_fwd(): pl.pallas_call(functools.partial(attn_fwd_kernel, groups), grid=(kv_loc,)...  43.7 us
    pallas_call x1, Pallas kernels, proj_raw(): pl.pallas_call(functools.partial(proj_raw_kernel, n_parts), grid=(depth /...  37 us
  transfers between devices with their start and end apart: 30, of which 7 were waited for; matrix products, arithmetic and copies ran while one was open for 0% of the time, Pallas kernels for 53%

profile of v4, /device:TPU:0, one launch (start us, length us, event | category | flops | bytes accessed | tf_op | source)
XLA Modules:
  0.0 971.4 jit_solution(2725684796555485550)
XLA Ops:
  16.8 68.3 %collective-permute-done.3 = bf16[256,6144]{1,0:T(8,128)(2,1)S(1)} collective-permute-done((bf16[256,6144]{1,0:T(8,128)(2,1)}, bf16[256,6144]{1,0:T(8,128)(2,1)S(1)}, u32[]{:S(2)}, u32[]{:S(2)}) %collective-permute-start.3) | collective-permute-done | bytes 3145760 | tf_op jit(solution)/shard_map/ppermute | solution.py:563
  97.8 67.7 %collective-permute-done.2 = bf16[256,6144]{1,0:T(8,128)(2,1)} collective-permute-done((bf16[256,6144]{1,0:T(8,128)(2,1)}, bf16[256,6144]{1,0:T(8,128)(2,1)}, u32[]{:S(2)}, u32[]{:S(2)}) %collective-permute-start.2) | collective-permute-done | bytes 3145760 | tf_op jit(solution)/shard_map/ppermute | solution.py:563
  167.1 67.2 %collective-permute-done.5 = bf16[256,6144]{1,0:T(8,128)(2,1)} collective-permute-done((bf16[256,6144]{1,0:T(8,128)(2,1)}, bf16[256,6144]{1,0:T(8,128)(2,1)}, u32[]{:S(2)}, u32[]{:S(2)}) %collective-permute-start.5) | collective-permute-done | bytes 3145760 | tf_op jit(solution)/shard_map/ppermute | solution.py:563
  239.3 62.9 %collective-permute-done.4 = bf16[256,6144]{1,0:T(8,128)(2,1)} collective-permute-done((bf16[256,6144]{1,0:T(8,128)(2,1)}, bf16[256,6144]{1,0:T(8,128)(2,1)}, u32[]{:S(2)}, u32[]{:S(2)}) %collective-permute-start.4) | collective-permute-done | bytes 3145760 | tf_op jit(solution)/shard_map/ppermute | solution.py:563
  302.8 37.0 %proj_raw.1 = (bf16[512,2048]{1,0:T(8,128)(2,1)}, bf16[512,2048]{1,0:T(8,128)(2,1)}, bf16[6144,2048]{1,0:T(8,128)(2,1)}) custom-call(bf16[256,6144]{1,0:T(8,128)(2,1)} %get-tuple-element.65.refs_0_, bf16[256,6144]{1,0:T(8,128)(2,1)} %get-tuple-element.62.refs_1_, bf16[256,6144]{1,0:T(8,128)(2,1)} %collective-permute-done.refs_2_, ...), custom_call_target="tpu_custom_call" | custom-call | flops 25769803776 | bytes 25165824 | tf_op jit(solution)/shard_map/proj_raw/pallas_call | solution.py:497
  339.8 15.6 %proj_deep.6.down_ref = bf16[512,1536]{1,0:T(8,128)(2,1)} custom-call(bf16[2,512,6144]{2,1,0:T(8,128)(2,1)} %all-gather.12.cloned.1.call-done.a_ref.refs_4_.refs_6_, bf16[1536,6144]{1,0:T(8,128)(2,1)} %w_ref.7), custom_call_target="tpu_custom_call" | custom-call | flops 9663676416 | bytes 18874368 | tf_op jit(solution)/shard_map/proj_deep/pallas_call | solution.py:513
  355.5 15.6 %proj_deep.7.down_ref = bf16[512,1536]{1,0:T(8,128)(2,1)} custom-call(bf16[2,512,6144]{2,1,0:T(8,128)(2,1)} %all-gather.12.cloned.1.call-done.a_ref.refs_4_.refs_6_, bf16[1536,6144]{1,0:T(8,128)(2,1)} %w_ref.7), custom_call_target="tpu_custom_call" | custom-call | flops 9663676416 | bytes 18874368 | tf_op jit(solution)/shard_map/proj_deep/pallas_call | solution.py:513
  371.1 18.9 %proj_deep.8.far_ref = bf16[512,2048]{1,0:T(8,128)(2,1)} custom-call(bf16[512,6144]{1,0:T(8,128)(2,1)} %all-gather.10.cloned.1.call-done.a_ref.refs_1_, bf16[6144,2048]{1,0:T(8,128)(2,1)} %get-tuple-element.71.w_ref.refs_2_), custom_call_target="tpu_custom_call" | custom-call | flops 12884901888 | bytes 25165824 | tf_op jit(solution)/shard_map/proj_deep/pallas_call | solution.py:513
  390.1 21.9 %attn_fwd.2 = (bf16[512,1536]{1,0:T(8,128)(2,1)}, bf16[512,1536]{1,0:T(8,128)(2,1)}, f32[1024,1536]{1,0:T(8,128)}) custom-call(bf16[512,2048]{1,0:T(8,128)(2,1)} %get-tuple-element.67.own_ref, bf16[512,2048]{1,0:T(8,128)(2,1)} %proj_deep.8.far_ref, f32[1024,128]{1,0:T(8,128)} %get-tuple-element.64.cos_ref, f32[1024,128]{1,0:T(8,128)} %get-tuple-element.73.sin_ref), custom_call_target="tpu_custom_call" | custom-call | flops 12000000000 | bytes 14000000 | tf_op jit(solution)/shard_map/attn_fwd/pallas_call | solution.py:220
  411.9 24.7 %proj_wide.4 = (bf16[512,6144]{1,0:T(8,128)(2,1)}, bf16[512,6144]{1,0:T(8,128)(2,1)}) custom-call(bf16[512,1536]{1,0:T(8,128)(2,1)} %get-tuple-element.76.refs_0_.afar_ref.refs_1_, bf16[512,1536]{1,0:T(8,128)(2,1)} %get-tuple-element.102.refs_1_.aown_ref.refs_0_, bf16[1536,6144]{1,0:T(8,128)(2,1)} %w_ref.7), custom_call_target="tpu_custom_call" | custom-call | flops 19327352832 | bytes 18874368 | tf_op jit(solution)/shard_map/proj_wide/pallas_call | solution.py:546
  436.7 18.9 %proj_deep.9.far_ref = bf16[512,2048]{1,0:T(8,128)(2,1)} custom-call(bf16[512,6144]{1,0:T(8,128)(2,1)} %all-gather.8.cloned.1.call-done.a_ref.refs_3_, bf16[6144,2048]{1,0:T(8,128)(2,1)} %get-tuple-element.71.w_ref.refs_2_), custom_call_target="tpu_custom_call" | custom-call | flops 12884901888 | bytes 25165824 | tf_op jit(solution)/shard_map/proj_deep/pallas_call | solution.py:513
  455.5 21.8 %attn_fwd.3 = (bf16[512,1536]{1,0:T(8,128)(2,1)}, bf16[512,1536]{1,0:T(8,128)(2,1)}, f32[1024,1536]{1,0:T(8,128)}) custom-call(bf16[512,2048]{1,0:T(8,128)(2,1)} %get-tuple-element.66.own_ref, bf16[512,2048]{1,0:T(8,128)(2,1)} %proj_deep.9.far_ref, f32[1024,128]{1,0:T(8,128)} %get-tuple-element.64.cos_ref, f32[1024,128]{1,0:T(8,128)} %get-tuple-element.73.sin_ref), custom_call_target="tpu_custom_call" | custom-call | flops 12000000000 | bytes 14000000 | tf_op jit(solution)/shard_map/attn_fwd/pallas_call | solution.py:220
  477.3 24.5 %proj_wide.5 = (bf16[384,6144]{1,0:T(8,128)(2,1)}, bf16[128,6144]{1,0:T(8,128)(2,1)}, bf16[512,6144]{1,0:T(8,128)(2,1)}) custom-call(bf16[512,1536]{1,0:T(8,128)(2,1)} %get-tuple-element.82.refs_0_.afar_ref.refs_3_, bf16[512,1536]{1,0:T(8,128)(2,1)} %get-tuple-element.81.refs_1_.aown_ref.refs_2_, bf16[1536,6144]{1,0:T(8,128)(2,1)} %w_ref.7), custom_call_target="tpu_custom_call" | custom-call | flops 19327352832 | bytes 18874368 | tf_op jit(solution)/shard_map/proj_wide/pallas_call | solution.py:546
  504.1 16.9 %proj_deep.10.dfar_ref = bf16[512,1536]{1,0:T(8,128)(2,1)} custom-call(bf16[512,6144]{1,0:T(8,128)(2,1)} %all-gather.16.cloned.1.call-done.a_ref.refs_5_, bf16[1536,6144]{1,0:T(8,128)(2,1)} %w_ref.7), custom_call_target="tpu_custom_call" | custom-call | flops 9663676416 | bytes 18874368 | tf_op jit(solution)/shard_map/proj_deep/pallas_call | solution.py:513
  521.0 32.8 %attn_bwd.2 = (bf16[512,2048]{1,0:T(8,128)(2,1)}, bf16[512,2048]{1,0:T(8,128)(2,1)}) custom-call(bf16[512,2048]{1,0:T(8,128)(2,1)} %get-tuple-element.67.own_ref, bf16[512,2048]{1,0:T(8,128)(2,1)} %proj_deep.8.far_ref, bf16[512,1536]{1,0:T(8,128)(2,1)} %get-tuple-element.102.refs_1_.aown_ref.refs_0_, ...), custom_call_target="tpu_custom_call" | custom-call | flops 24999999488 | bytes 22000000 | tf_op jit(solution)/shard_map/attn_bwd/pallas_call | solution.py:239
  553.8 31.8 %proj_wide.6 = (bf16[512,6144]{1,0:T(8,128)(2,1)}, bf16[512,6144]{1,0:T(8,128)(2,1)}) custom-call(bf16[512,2048]{1,0:T(8,128)(2,1)} %get-tuple-element.91.refs_0_.refs_5_, bf16[512,2048]{1,0:T(8,128)(2,1)} %get-tuple-element.90.refs_1_.refs_4_, bf16[6144,2048]{1,0:T(8,128)(2,1)} %get-tuple-element.71.w_ref.refs_2_), custom_call_target="tpu_custom_call" | custom-call | flops 25769803776 | bytes 25165824 | tf_op jit(solution)/shard_map/proj_wide/pallas_call | solution.py:546
  585.6 15.6 %proj_deep.11.dfar_ref = bf16[512,1536]{1,0:T(8,128)(2,1)} custom-call(bf16[512,6144]{1,0:T(8,128)(2,1)} %all-gather.14.cloned.1.call-done.a_ref.refs_7_, bf16[1536,6144]{1,0:T(8,128)(2,1)} %w_ref.7), custom_call_target="tpu_custom_call" | custom-call | flops 9663676416 | bytes 18874368 | tf_op jit(solution)/shard_map/proj_deep/pallas_call | solution.py:513
  601.3 31.0 %attn_bwd.3 = (bf16[512,2048]{1,0:T(8,128)(2,1)}, bf16[512,2048]{1,0:T(8,128)(2,1)}) custom-call(bf16[512,2048]{1,0:T(8,128)(2,1)} %get-tuple-element.66.own_ref, bf16[512,2048]{1,0:T(8,128)(2,1)} %proj_deep.9.far_ref, bf16[512,1536]{1,0:T(8,128)(2,1)} %get-tuple-element.81.refs_1_.aown_ref.refs_2_, ...), custom_call_target="tpu_custom_call" | custom-call | flops 24999999488 | bytes 22000000 | tf_op jit(solution)/shard_map/attn_bwd/pallas_call | solution.py:239
  632.2 31.8 %proj_wide.7 = (bf16[512,6144]{1,0:T(8,128)(2,1)}, bf16[512,6144]{1,0:T(8,128)(2,1)}) custom-call(bf16[512,2048]{1,0:T(8,128)(2,1)} %get-tuple-element.97.refs_0_.refs_7_, bf16[512,2048]{1,0:T(8,128)(2,1)} %get-tuple-element.96.refs_1_.refs_6_, bf16[6144,2048]{1,0:T(8,128)(2,1)} %get-tuple-element.71.w_ref.refs_2_), custom_call_target="tpu_custom_call" | custom-call | flops 25769803776 | bytes 25165824 | tf_op jit(solution)/shard_map/proj_wide/pallas_call | solution.py:546
  669.9 48.8 %dw_out.1 = bf16[1536,6144]{1,0:T(8,128)(2,1)} custom-call(bf16[512,1536]{1,0:T(8,128)(2,1)} %get-tuple-element.102.refs_1_.aown_ref.refs_0_, bf16[512,1536]{1,0:T(8,128)(2,1)} %get-tuple-element.76.refs_0_.afar_ref.refs_1_, bf16[512,1536]{1,0:T(8,128)(2,1)} %get-tuple-element.81.refs_1_.aown_ref.refs_2_, ...), custom_call_target="tpu_custom_call" | custom-call | flops 38999998464 | bytes 50000000 | tf_op jit(solution)/shard_map/dw_out/pallas_call | solution.py:288
  722.3 67.4 %collective-permute-done.6.far0_ref = bf16[256,6144]{1,0:T(8,128)(2,1)} collective-permute-done((bf16[256,6144]{1,0:T(8,128)(2,1)}, bf16[256,6144]{1,0:T(8,128)(2,1)}, u32[]{:S(2)}, u32[]{:S(2)}) %collective-permute-start.6) | collective-permute-done | bytes 3145760 | tf_op jit(solution)/shard_map/ppermute | solution.py:563
  799.4 63.9 %dw_qkv.1 = bf16[6144,2,1024]{2,1,0:T(2,128)(2,1)} custom-call(bf16[512,6144]{1,0:T(8,128)(2,1)} %all-gather.18.cloned.1.call-done.refs_0_, bf16[512,6144]{1,0:T(8,128)(2,1)} %all-gather.10.cloned.1.call-done.a_ref.refs_1_, bf16[512,6144]{1,0:T(8,128)(2,1)} %all-gather.20.cloned.1.call-done.refs_2_, ...), custom_call_target="tpu_custom_call" | custom-call | flops 51000000512 | bytes 60000000 | tf_op jit(solution)/shard_map/dw_qkv/pallas_call | solution.py:267
  863.3 74.2 %collective-permute-done.8.far_ref = bf16[256,6144]{1,0:T(8,128)(2,1)} collective-permute-done((bf16[256,6144]{1,0:T(8,128)(2,1)}, bf16[256,6144]{1,0:T(8,128)(2,1)}, u32[]{:S(2)}, u32[]{:S(2)}) %collective-permute-start.8) | collective-permute-done | bytes 3145760 | tf_op jit(solution)/shard_map/ppermute | solution.py:563
  947.5 10.2 %norm_bwd.3 = (bf16[2,256,6144]{2,1,0:T(8,128)(2,1)}, f32[1,6144]{1,0:T(1,128)}) custom-call(bf16[2,256,6144]{2,1,0:T(8,128)(2,1)} %x_ref.10, bf16[2,256,6144]{2,1,0:T(8,128)(2,1)} %dy_ref.5, bf16[6144]{0:T(1024)(128)(2,1)} %gain_ref.7, bf16[256,6144]{1,0:T(8,128)(2,1)} %reduce-scatter.12.cloned.1.call-done.near_ref, ...), custom_call_target="tpu_custom_call", output_to_operand_aliasing={{0}: (6, {})} | custom-call | flops 4000000000 | bytes 16000000 | tf_op jit(solution)/shard_map/norm_bwd/pallas_call | solution.py:432
  (89 shorter events, 67.5 us)
Async XLA Ops:
  7.2 332.7 %all-gather.12.cloned.1.call-start = ((), (), s32[]{:S(2)}) async-start(), calls=%async_computation.11 | async-start | bytes 18874368 | tf_op jit(solution)/shard_map/all_gather | solution.py:566
  7.9 363.2 %all-gather.10.cloned.1.call-start = ((), (), s32[]{:S(2)}) async-start(), calls=%async_computation.10 | async-start | bytes 9437184 | tf_op jit(solution)/shard_map/all_gather | solution.py:566
  13.5 71.6 %collective-permute-start.3 = (bf16[256,6144]{1,0:T(8,128)(2,1)}, bf16[256,6144]{1,0:T(8,128)(2,1)S(1)}, u32[]{:S(2)}, u32[]{:S(2)}) collective-permute-start(bf16[256,6144]{1,0:T(8,128)(2,1)} %get-tuple-element.65.refs_0_), channel_id=1, source_target_pairs={{0,2},{1,3},{2,0},{3,1},{4,6},{5,7},{6,4},{7,5}} | collective-permute-start | bytes 9437192 | tf_op jit(solution)/shard_map/ppermute | solution.py:563
  86.8 349.9 %all-gather.8.cloned.1.call-start = ((), (), s32[]{:S(2)}) async-start(), calls=%async_computation.9 | async-start | bytes 9437184 | tf_op jit(solution)/shard_map/all_gather | solution.py:566
  96.1 69.5 %collective-permute-start.2 = (bf16[256,6144]{1,0:T(8,128)(2,1)}, bf16[256,6144]{1,0:T(8,128)(2,1)}, u32[]{:S(2)}, u32[]{:S(2)}) collective-permute-start(bf16[256,6144]{1,0:T(8,128)(2,1)} %get-tuple-element.62.refs_1_), channel_id=1, source_target_pairs={{0,2},{1,3},{2,0},{3,1},{4,6},{5,7},{6,4},{7,5}} | collective-permute-start | bytes 9437192 | tf_op jit(solution)/shard_map/ppermute | solution.py:563
  165.6 338.5 %all-gather.16.cloned.1.call-start = ((), (), s32[]{:S(2)}) async-start(), calls=%async_computation.14 | async-start | bytes 9437184 | tf_op jit(solution)/shard_map/all_gather | solution.py:566
  165.6 68.7 %collective-permute-start.5 = (bf16[256,6144]{1,0:T(8,128)(2,1)}, bf16[256,6144]{1,0:T(8,128)(2,1)}, u32[]{:S(2)}, u32[]{:S(2)}) collective-permute-start(bf16[256,6144]{1,0:T(8,128)(2,1)} %get-tuple-element.85), channel_id=1, source_target_pairs={{0,2},{1,3},{2,0},{3,1},{4,6},{5,7},{6,4},{7,5}} | collective-permute-start | bytes 9437192 | tf_op jit(solution)/shard_map/ppermute | solution.py:563
  234.3 351.3 %all-gather.14.cloned.1.call-start = ((), (), s32[]{:S(2)}) async-start(), calls=%async_computation.13 | async-start | bytes 9437184 | tf_op jit(solution)/shard_map/all_gather | solution.py:566
  234.4 67.8 %collective-permute-start.4 = (bf16[256,6144]{1,0:T(8,128)(2,1)}, bf16[256,6144]{1,0:T(8,128)(2,1)}, u32[]{:S(2)}, u32[]{:S(2)}) collective-permute-start(bf16[256,6144]{1,0:T(8,128)(2,1)} %get-tuple-element.84), channel_id=1, source_target_pairs={{0,2},{1,3},{2,0},{3,1},{4,6},{5,7},{6,4},{7,5}} | collective-permute-start | bytes 9437192 | tf_op jit(solution)/shard_map/ppermute | solution.py:563
  235.6 67.3 %collective-permute-start = (bf16[256,6144]{1,0:T(8,128)(2,1)S(1)}, bf16[256,6144]{1,0:T(8,128)(2,1)}, u32[]{:S(2)}, u32[]{:S(2)}) collective-permute-start(bf16[256,6144]{1,0:T(8,128)(2,1)S(1)} %copy-done), channel_id=1, source_target_pairs={{0,1},{1,0},{2,3},{3,2},{4,5},{5,4},{6,7},{7,6}} | collective-permute-start | bytes 9437192 | tf_op jit(solution)/shard_map/ppermute | solution.py:563
  235.6 67.3 %collective-permute-start.1 = (bf16[256,6144]{1,0:T(8,128)(2,1)}, bf16[256,6144]{1,0:T(8,128)(2,1)}, u32[]{:S(2)}, u32[]{:S(2)}) collective-permute-start(bf16[256,6144]{1,0:T(8,128)(2,1)} %get-tuple-element.62.refs_1_), channel_id=1, source_target_pairs={{0,1},{1,0},{2,3},{3,2},{4,5},{5,4},{6,7},{7,6}} | collective-permute-start | bytes 9437192 | tf_op jit(solution)/shard_map/ppermute | solution.py:563
  302.2 365.6 %reduce-scatter.20.cloned.1.call-start = ((), (), s32[]{:S(2)}) async-start(), calls=%async_computation.20 | async-start | bytes 7077888 | tf_op jit(solution)/shard_map/reduce_scatter | solution.py:569
  501.8 166.5 %reduce-scatter.18.cloned.1.call-start = ((), (), s32[]{:S(2)}) async-start(), calls=%async_computation.19 | async-start | bytes 9437184 | tf_op jit(solution)/shard_map/reduce_scatter | solution.py:569
  502.6 216.1 %reduce-scatter.26.cloned.1.call-start = ((), (), s32[]{:S(2)}) async-start(), calls=%async_computation.24 | async-start | bytes 2359296 | tf_op jit(solution)/shard_map/reduce_scatter | solution.py:569
  503.3 215.7 %reduce-scatter.16.cloned.1.call-start = ((), (), s32[]{:S(2)}) async-start(), calls=%async_computation.18 | async-start | bytes 9437184 | tf_op jit(solution)/shard_map/reduce_scatter | solution.py:569
  504.1 215.0 %reduce-scatter.24.cloned.1.call-start = ((), (), s32[]{:S(2)}) async-start(), calls=%async_computation.23 | async-start | bytes 9437184 | tf_op jit(solution)/shard_map/reduce_scatter | solution.py:569
  665.3 134.1 %all-gather.18.cloned.1.call-start = ((), (), s32[]{:S(2)}) async-start(), calls=%async_computation.17 | async-start | bytes 9437184 | tf_op jit(solution)/shard_map/all_gather | solution.py:566
  666.1 133.4 %all-gather.20.cloned.1.call-start = ((), (), s32[]{:S(2)}) async-start(), calls=%async_computation.21 | async-start | bytes 9437184 | tf_op jit(solution)/shard_map/all_gather | solution.py:566
  666.6 196.7 %reduce-scatter.14.cloned.1.call-start = ((), (), s32[]{:S(2)}) async-start(), calls=%async_computation.16 | async-start | bytes 9437184 | tf_op jit(solution)/shard_map/reduce_scatter | solution.py:569
  667.2 280.2 %reduce-scatter.12.cloned.1.call-start = ((), (), s32[]{:S(2)}) async-start(), calls=%async_computation.15 | async-start | bytes 9437184 | tf_op jit(solution)/shard_map/reduce_scatter | solution.py:569
  668.4 121.3 %collective-permute-start.6 = (bf16[256,6144]{1,0:T(8,128)(2,1)}, bf16[256,6144]{1,0:T(8,128)(2,1)}, u32[]{:S(2)}, u32[]{:S(2)}) collective-permute-start(bf16[256,6144]{1,0:T(8,128)(2,1)} %reduce-scatter.18.cloned.1.call-done), channel_id=1, source_target_pairs={{0,2},{1,3},{2,0},{3,1},{4,6},{5,7},{6,4},{7,5}} | collective-permute-start | bytes 9437192 | tf_op jit(solution)/shard_map/ppermute | solution.py:563
  718.6 241.7 %collective-permute-start.10 = (bf16[64,6144]{1,0:T(8,128)(2,1)}, bf16[64,6144]{1,0:T(8,128)(2,1)S(1)}, u32[]{:S(2)}, u32[]{:S(2)}) collective-permute-start(bf16[64,6144]{1,0:T(8,128)(2,1)} %reduce-scatter.26.cloned.1.call-done), channel_id=1, source_target_pairs={{0,2},{1,3},{2,0},{3,1},{4,6},{5,7},{6,4},{7,5}} | collective-permute-start | bytes 2359304 | tf_op jit(solution)/shard_map/ppermute | solution.py:563
  719.1 228.4 %collective-permute-start.9 = (bf16[256,6144]{1,0:T(8,128)(2,1)}, bf16[256,6144]{1,0:T(8,128)(2,1)}, u32[]{:S(2)}, u32[]{:S(2)}) collective-permute-start(bf16[256,6144]{1,0:T(8,128)(2,1)} %reduce-scatter.24.cloned.1.call-done), channel_id=1, source_target_pairs={{0,2},{1,3},{2,0},{3,1},{4,6},{5,7},{6,4},{7,5}} | collective-permute-start | bytes 9437192 | tf_op jit(solution)/shard_map/ppermute | solution.py:563
  720.7 216.8 %collective-permute-start.8 = (bf16[256,6144]{1,0:T(8,128)(2,1)}, bf16[256,6144]{1,0:T(8,128)(2,1)}, u32[]{:S(2)}, u32[]{:S(2)}) collective-permute-start(bf16[256,6144]{1,0:T(8,128)(2,1)} %reduce-scatter.22.cloned.1.call-done), channel_id=1, source_target_pairs={{0,2},{1,3},{2,0},{3,1},{4,6},{5,7},{6,4},{7,5}} | collective-permute-start | bytes 9437192 | tf_op jit(solution)/shard_map/ppermute | solution.py:563
  (10 other events, 266.2 us)
Sparse Core Ops, SparseCore 0:
  9.5 24.4 all-gather.11
  86.9 15.2 all-gather.9
  165.7 14.9 all-gather.7
  234.5 15.8 all-gather.15
  302.4 14.3 all-gather.13
  501.9 9.9 reduce-scatter.19
  514.2 12.5 reduce-scatter.17
  529.0 8.2 reduce-scatter.25
  539.6 12.5 reduce-scatter.15
  664.1 11.2 reduce-scatter.23
  677.7 13.2 reduce-scatter.21
  693.7 13.2 reduce-scatter.9
  708.6 16.0 all-gather.17
  726.1 15.1 all-gather.19
  743.4 12.3 reduce-scatter.13
  757.9 13.2 reduce-scatter.11
